TPU v7x, 1024 devices: a whole 4x4x32 slice. The times are simulated.
1024 devices in a mesh: gx: 64 (over z_lo, x, core), gy: 16 (over y, z_hi).
Axes of the slice: x: 4, y: 4, z: 32 (z_hi: 4, z_lo: 8; z = z_hi * 8 + z_lo), core: 2. Of those that a mesh axis runs over, the one named last changes fastest.
Arguments:
- prefix_tokens: bfloat16 [49152, 8192], P('gx'), may hold values from -6 to 6
- key_value_weight: bfloat16 [8192, 2048], P('gx', 'gy'), may hold values from -0.0625 to 0.0625
- prefix_lengths: int32 [384], P('gx'), may hold values from 1 to 128, as said below
- start_offsets: int32 [384], P('gx'), may hold values from 0 to 8064
- queries: bfloat16 [32, 8192], P('gy'), may hold values from -5 to 5
- key_value_cache: bfloat16 [2, 32, 8192, 1024], P(None, 'gy', 'gx'), may hold values from -5 to 5
- cache_lengths: int32 [32], P('gy'), may hold values from 1024 to 8192, as said below
- out_weight: bfloat16 [8192, 8192], P('gy', 'gx'), may hold values from -0.5 to 0.5
Outputs:
- prefix_kv: bfloat16 [49152, 2048], P('gx', 'gy')
- decode_out: bfloat16 [32, 8192], P('gy', 'gx')
Inputs may be any that keep to these rules, and one draw needn't show every extreme that they name: `prefix_lengths`: live tokens stand at the front of a prefix's slots; in every draw some prefix uses all 128 slots. `cache_lengths`: live positions stand at the front of a trajectory's cache; in every draw some trajectory uses all 8192 positions.
All inputs are finite; a program needn't handle non-finite values.
Results may differ from a plain program's by a relative error of at most 0.0051.
Values may be sent and summed in bfloat16 or wider, within the bound.
No kernel may reach another device: no remote copies, remote signals or barrier semaphores. Data moves between devices by JAX's collectives and lax.ppermute only.
A program may use at most 64 MiB of HBM per device.

v0:
```python
import jax
import jax.numpy as jnp
from jax import lax
from jax.sharding import Mesh
from jax.sharding import PartitionSpec as P

QUERY_HEADS = 64
KEY_VALUE_HEADS = 8
HEAD_SIZE = 128
SLOT = 128
GX = ("gx_0", "gx_1", "gx_2")


rope_base = 500000.0
masked_score = -1e30


def all_in_one(shard, axis):
    leaves = jax.tree.leaves(shard)
    order = sorted(range(len(leaves)), key=lambda k: -leaves[k].size)
    width = (1, *leaves[order[0]].shape)[-1]
    lines = [
        jnp.pad(leaves[k].reshape(-1), (0, -leaves[k].size % width)).reshape(-1, width)
        for k in order
    ]
    both, at, found = (lax.all_gather(jnp.concatenate(lines), axis), 0, {})
    for k, line in zip(order, lines):
        slab = both[:, at : at + len(line)].reshape(len(both), -1)
        found[k] = slab[:, : leaves[k].size].reshape(-1, *leaves[k].shape)
        at += len(line)
    numbers = iter(range(len(leaves)))
    return jax.tree.map(lambda _: found[next(numbers)], shard)


def joined_all(shard, axes, combine):
    for axis in axes:
        pieces = all_in_one(shard, axis)
        shard = jax.tree.map(lambda part: part[0], pieces)
        for k in range(1, lax.axis_size(axis)):
            shard = combine(shard, jax.tree.map(lambda part: part[k], pieces))
    return shard


def cut_along(shard, dim, devices):
    dims = shard.shape
    tiles = shard.reshape(*dims[:dim], devices, dims[dim] // devices, *dims[dim + 1 :])
    return jnp.moveaxis(tiles, dim, 0)


def sum_at_owner(shard, axis, dim):
    devices = lax.axis_size(axis)
    tiles = lax.all_to_all(cut_along(shard, dim, devices), axis, 0, 0, tiled=True)
    return jnp.sum(tiles, axis=0)


def rotate_and_mask(projected, first_column, prefix_lengths, start_offsets):
    tok_rows, columns = projected.shape
    slot_index = jnp.arange(SLOT, dtype=jnp.int32)
    positions = (start_offsets[:, None] + slot_index[None, :]).reshape(tok_rows)
    live_rows = (slot_index[None, :] < prefix_lengths[:, None]).reshape(tok_rows)
    half_width = HEAD_SIZE // 2
    freq_index = jnp.arange(half_width, dtype=jnp.float32)
    inverse = rope_base ** (-2.0 * freq_index / HEAD_SIZE)
    angles = positions.astype(jnp.float32)[:, None] * inverse[None, :]
    cosine = jnp.cos(angles)[:, None, :]
    sine = jnp.sin(angles)[:, None, :]
    head_list = projected.reshape(tok_rows, columns // HEAD_SIZE, HEAD_SIZE)
    first_half = head_list[:, :, :half_width]
    second_half = head_list[:, :, half_width:]
    rotary_applied = jnp.concatenate(
        [first_half * cosine - second_half * sine, second_half * cosine + first_half * sine], axis=2
    )
    head_position = first_column // HEAD_SIZE + jnp.arange(columns // HEAD_SIZE, dtype=jnp.int32)
    key_tagged = jnp.where(
        (head_position < KEY_VALUE_HEADS)[None, :, None], rotary_applied, head_list
    )
    kept = jnp.where(live_rows[:, None, None], key_tagged, 0.0)
    return kept.reshape(tok_rows, columns).astype(jnp.bfloat16)


def merge_parts(earlier, later):
    highest = jnp.maximum(earlier[0], later[0])
    early_factor = jnp.exp(earlier[0] - highest)
    late_factor = jnp.exp(later[0] - highest)
    summed = earlier[1] * early_factor + later[1] * late_factor
    weighted = earlier[2] * early_factor[..., None] + later[2] * late_factor[..., None]
    return (highest, summed, weighted)


def shards(
    prefix_tokens,
    key_value_weight,
    prefix_lengths,
    start_offsets,
    queries,
    key_value_cache,
    cache_lengths,
    out_weight,
):
    columns = key_value_weight.shape[1]
    selected = prefix_tokens
    projected = jnp.dot(
        selected,
        lax.all_gather(key_value_weight, GX, axis=0, tiled=True),
        preferred_element_type=jnp.float32,
    )
    prefix_kv = rotate_and_mask(
        projected, lax.axis_index("gy") * columns, prefix_lengths, start_offsets
    )
    trajectory_per_shard = queries.shape[0]
    cache_per_shard = key_value_cache.shape[2]
    query_group = QUERY_HEADS // KEY_VALUE_HEADS
    query_head_rows = queries.reshape(trajectory_per_shard, KEY_VALUE_HEADS, query_group, HEAD_SIZE)
    key_rows = key_value_cache[0].reshape(
        trajectory_per_shard, cache_per_shard, KEY_VALUE_HEADS, HEAD_SIZE
    )
    value_rows = key_value_cache[1].reshape(
        trajectory_per_shard, cache_per_shard, KEY_VALUE_HEADS, HEAD_SIZE
    )
    scores = jnp.einsum(
        "bhgd,bphd->bhgp", query_head_rows, key_rows, preferred_element_type=jnp.float32
    ) * HEAD_SIZE ** (-0.5)
    position = lax.axis_index(GX) * cache_per_shard + jnp.arange(cache_per_shard, dtype=jnp.int32)
    valid = (position[None, :] < cache_lengths[:, None])[:, None, None, :]
    peak = jnp.max(jnp.where(valid, scores, masked_score), axis=3)
    weights = jnp.where(valid, jnp.exp(scores - peak[..., None]), 0.0)
    block_total = jnp.sum(weights, axis=3)
    numerator = jnp.einsum(
        "bhgp,bphd->bhgd",
        weights.astype(jnp.bfloat16),
        value_rows,
        preferred_element_type=jnp.float32,
    )
    peak, block_total, numerator = joined_all((peak, block_total, numerator), GX, merge_parts)
    attention = (
        (numerator / block_total[..., None])
        .reshape(trajectory_per_shard, QUERY_HEADS * HEAD_SIZE)
        .astype(jnp.bfloat16)
    )
    spread = lax.all_to_all(attention, "gy", split_axis=1, concat_axis=0, tiled=True)
    selected = spread
    mixed = sum_at_owner(jnp.dot(selected, out_weight, preferred_element_type=jnp.float32), "gy", 0)
    return (prefix_kv, mixed.astype(jnp.bfloat16))


def solution(mesh):
    finer = Mesh(mesh.devices.reshape(8, 4, 2, mesh.shape["gy"]), ("gx_0", "gx_1", "gx_2", "gy"))
    return jax.shard_map(
        shards,
        mesh=finer,
        in_specs=(
            P(GX, None),
            P(GX, "gy"),
            P(GX),
            P(GX),
            P("gy", None),
            P(None, "gy", GX, None),
            P("gy"),
            P("gy", GX),
        ),
        out_specs=(P(GX, "gy"), P("gy", GX)),
        check_vma=False,
    )
```

profile of v0, /device:TPU:2, one launch (start us, length us, event | category | flops | bytes accessed | tf_op | source)
XLA Modules:
  0.0 180.2 jit_solution(8867225095857639104)
XLA Ops:
  7.2 0.0 copy-start
  7.2 0.0 all-gather.8.cloned.1.call-start
  7.2 0.7 all-gather.8.cloned.1.call-update
  7.9 1.3 fusion.115
  9.2 0.3 copy.35
  9.5 0.7 broadcast_compare_fusion
  10.2 1.1 select_reduce_fusion
  11.3 0.1 reshape.1294
  11.4 0.2 fusion.42
  11.6 0.1 reshape.1295
  11.7 0.3 copy.36
  11.9 0.4 fusion.44
  12.4 50.6 %all-gather.3 = f32[8,130,128]{2,1,0:T(8,128)S(1)} all-gather(f32[1,130,128]{2,1,0:T(8,128)S(1)} %maximum_bitcast_fusion), channel_id=2, replica_groups=mesh['gx_0'=8,'gx_1'=4,'gx_2'=2,'gy'=16] {'gx_0'}, dimensions={0}, use_global_device_ids=true | all-gather | bytes 599040 | tf_op jit(solution)/shard_map/all_gather | solution.py:26
  63.1 0.3 fusion.22
  63.4 19.9 %all-gather.4 = f32[4,130,128]{2,1,0:T(8,128)S(1)} all-gather(f32[1,130,128]{2,1,0:T(8,128)S(1)} %maximum_bitcast_fusion.1), channel_id=3, replica_groups=mesh['gx_0'=8,'gx_1'=4,'gx_2'=2,'gy'=16] {'gx_1'}, dimensions={0}, use_global_device_ids=true | all-gather | bytes 332800 | tf_op jit(solution)/shard_map/all_gather | solution.py:26
  83.3 0.2 fusion.13
  83.5 1.9 %all-gather.5 = f32[2,130,128]{2,1,0:T(8,128)S(1)} all-gather(f32[1,130,128]{2,1,0:T(8,128)S(1)} %maximum_bitcast_fusion.2), channel_id=4, replica_groups=mesh['gx_0'=8,'gx_1'=4,'gx_2'=2,'gy'=16] {'gx_2'}, dimensions={0}, use_global_device_ids=true | all-gather | bytes 199680 | tf_op jit(solution)/shard_map/all_gather | solution.py:26
  85.5 0.1 squeeze.203
  85.5 0.1 squeeze.202
  85.6 0.1 squeeze.199
  85.7 0.1 squeeze.200
  85.8 0.1 div.31
  86.0 0.1 mul.551
  86.1 0.1 mul.548
  86.2 0.6 copy.29
  86.9 21.7 %all-to-all-start = ((bf16[2,16,512]{2,0,1:T(2,128)(2,1)}), bf16[2,16,512]{2,0,1:T(2,128)(2,1)S(1)}, u32[]{:S(2)}, u32[]{:S(2)}) async-start(bf16[2,16,512]{2,0,1:T(2,128)(2,1)} %copy.29), calls=%async_computation | async-start | bytes 65536 | tf_op jit(solution)/shard_map/all_to_all | solution.py:140
  108.6 0.7 convert_bitcast_fusion
  109.3 23.7 %all-to-all-done = bf16[2,16,512]{2,0,1:T(2,128)(2,1)S(1)} async-done(((bf16[2,16,512]{2,0,1:T(2,128)(2,1)}), bf16[2,16,512]{2,0,1:T(2,128)(2,1)S(1)}, u32[]{:S(2)}, u32[]{:S(2)}) %all-to-all-start) | async-done | bytes 32800 | tf_op jit(solution)/shard_map/all_to_all | solution.py:140
  133.0 0.0 copy-done
  133.0 0.1 fusion.10
  133.1 0.6 copy.31
  133.8 3.5 %all-to-all-start.1 = ((f32[16,2,128]{2,1,0:T(2,128)}), f32[16,2,128]{2,1,0:T(2,128)S(1)}, u32[]{:S(2)}, u32[]{:S(2)}) async-start(f32[16,2,128]{2,1,0:T(2,128)} %copy.31), calls=%async_computation.1 | async-start | bytes 32768 | tf_op jit(solution)/shard_map/all_to_all | solution.py:52
  137.3 0.7 fusion.55
  138.0 23.6 %all-to-all-done.1 = f32[16,2,128]{2,1,0:T(2,128)S(1)} async-done(((f32[16,2,128]{2,1,0:T(2,128)}), f32[16,2,128]{2,1,0:T(2,128)S(1)}, u32[]{:S(2)}, u32[]{:S(2)}) %all-to-all-start.1) | async-done | bytes 16416 | tf_op jit(solution)/shard_map/all_to_all | solution.py:52
  161.6 0.5 reduce_sum.19
  162.2 0.0 all-gather.8.cloned.1.call-done
  162.2 9.5 %fusion.117 = f32[768,128]{0,1:T(8,128)S(1)} fusion(bf16[768,8192]{1,0:T(8,128)(2,1)} %param.8, bf16[8192,128]{1,0:T(8,128)(2,1)} %all-gather.8.cloned.1.call-done), kind=kOutput, calls=%fused_computation.210 | convolution fusion | flops 1610612736 | bytes 15073280 | tf_op jit(solution)/shard_map/dot_general | solution.py:102
  171.6 0.8 fusion.7
  172.4 0.1 fusion.1
  172.5 0.8 copy.32
  (22 shorter events, 0.3 us)
Async XLA Ops:
  7.2 125.8 %copy-start = (bf16[512,128]{1,0:T(8,128)(2,1)S(1)}, bf16[512,128]{1,0:T(8,128)(2,1)}, u32[]{:S(2)}) copy-start(bf16[512,128]{1,0:T(8,128)(2,1)} %param.15) | copy-start | bytes 393220
  7.2 155.0 %all-gather.8.cloned.1.call-start = ((), (), s32[]{:S(2)}) async-start(), calls=%async_computation.2 | async-start | bytes 2129920 | tf_op jit(solution)/shard_map/all_gather | solution.py:104
  86.9 46.1 %all-to-all-start = ((bf16[2,16,512]{2,0,1:T(2,128)(2,1)}), bf16[2,16,512]{2,0,1:T(2,128)(2,1)S(1)}, u32[]{:S(2)}, u32[]{:S(2)}) async-start(bf16[2,16,512]{2,0,1:T(2,128)(2,1)} %copy.29), calls=%async_computation | async-start | bytes 65536 | tf_op jit(solution)/shard_map/all_to_all | solution.py:140
  133.8 27.9 %all-to-all-start.1 = ((f32[16,2,128]{2,1,0:T(2,128)}), f32[16,2,128]{2,1,0:T(2,128)S(1)}, u32[]{:S(2)}, u32[]{:S(2)}) async-start(f32[16,2,128]{2,1,0:T(2,128)} %copy.31), calls=%async_computation.1 | async-start | bytes 32768 | tf_op jit(solution)/shard_map/all_to_all | solution.py:52
Sparse Core Ops, SparseCore 0:
  10.7 137.7 all-gather.7
where the time goes:
time: 181 us; the launch traced here: 180 us
  blocking collectives  72.4 us (40%)
  waiting for transfers between devices  48 us (27%)
  starting transfers between devices  25.2 us (14%)
  between operations  14.3 us (8%)
  matrix products  11.1 us (6%)
  local copies, waits for them, and re-layouts  4.77 us (3%)
  other arithmetic  4.46 us (2%)
    all_gather x3, blocking collectives, all_in_one(): both, at, found = (lax.all_gather(jnp.concatenate(lines), axis), 0, {})  72.4 us
    all_to_all x1, waiting for transfers between devices, shards(): lax.all_to_all(attention, 'gy', split_axis=1, concat_axis=0, tiled=True)  23.7 us
    all_to_all x1, waiting for transfers between devices, sum_at_owner(): lax.all_to_all(cut_along(shard, dim, devices), axis, 0, 0, tiled=True)  23.6 us
    all_to_all x1, starting transfers between devices, shards(): lax.all_to_all(attention, 'gy', split_axis=1, concat_axis=0, tiled=True)  21.7 us
    dot_general x1, matrix products, shards(): jnp.dot(selected, lax.all_gather(key_value_weight, GX, axis=0, tiled=True...  9.46 us
  transfers between devices with their start and end apart: 3, of which 2 were waited for; matrix products, arithmetic and copies ran while one was open for 5% of the time, Pallas kernels for 0%

commit v1 on v0

v1 whole, which is shorter than its diff:
```python
import jax
import jax.numpy as jnp
from jax import lax
from jax.experimental import pallas as pl
from jax.experimental.pallas import tpu as pltpu
from jax.sharding import Mesh
from jax.sharding import PartitionSpec as P

QUERY_HEADS = 64
KEY_VALUE_HEADS = 8
HEAD_SIZE = 128
SLOT = 128
GX = ("z", "x", "c")
GY = ("y", "w")
GROUP = QUERY_HEADS // KEY_VALUE_HEADS

rope_base = 500000.0
masked_score = -1e30


def swap(pieces, axis):
    return lax.all_to_all(pieces, axis, 0, 0, tiled=True)


def rotation(column, prefix_lengths, start_offsets):
    slot_index = jnp.arange(SLOT, dtype=jnp.int32)
    positions = (start_offsets[:, None] + slot_index[None, :]).reshape(-1, 1)
    live = (slot_index[None, :] < prefix_lengths[:, None]).reshape(-1, 1)
    half_width = HEAD_SIZE // 2
    lane = jnp.arange(HEAD_SIZE, dtype=jnp.int32)
    frequency = (lane % half_width).astype(jnp.float32)
    inverse = rope_base ** (-2.0 * frequency / HEAD_SIZE)
    angles = positions.astype(jnp.float32) * inverse[None, :]
    is_key = column < KEY_VALUE_HEADS
    sine = jnp.where(lane[None, :] < half_width, -jnp.sin(angles), jnp.sin(angles))
    along = jnp.where(live, jnp.where(is_key, jnp.cos(angles), 1.0), 0.0)
    across = jnp.where(live & is_key, sine, 0.0)
    return along, across


def packed(peak, total):
    lane = lax.broadcasted_iota(jnp.int32, (peak.shape[0], HEAD_SIZE), 1)
    return jnp.where(lane < HEAD_SIZE // 2, peak, total)


def block_kernel(limits_ref, query_ref, cache_ref, out_ref):
    trajectories, positions = cache_ref.shape[1], cache_ref.shape[2]
    position = lax.broadcasted_iota(jnp.int32, (GROUP, positions), 1)
    for t in range(trajectories):
        valid = position < limits_ref[t]
        for g in range(KEY_VALUE_HEADS):
            columns = slice(g * HEAD_SIZE, (g + 1) * HEAD_SIZE)
            scores = lax.dot_general(
                query_ref[t, g * GROUP : (g + 1) * GROUP, :],
                cache_ref[0, t, :, columns],
                (((1,), (1,)), ((), ())),
                preferred_element_type=jnp.float32,
            ) * HEAD_SIZE ** (-0.5)
            peak = jnp.max(jnp.where(valid, scores, masked_score), axis=1, keepdims=True)
            weights = jnp.where(valid, jnp.exp(scores - peak), 0.0)
            total = jnp.sum(weights, axis=1, keepdims=True)
            values = jnp.dot(
                weights.astype(jnp.bfloat16),
                cache_ref[1, t, :, columns],
                preferred_element_type=jnp.float32,
            )
            stats = packed(peak, total)
            for i in range(4):
                slot, row, pair = t * 4 + i, g * 2, slice(i * 2, i * 2 + 2)
                out_ref[slot, row : row + 2, :] = values[pair]
                out_ref[slot, 16 + row : 18 + row, :] = stats[pair]


def merged(parts):
    numerator, stats = parts[:, :16, :], parts[:, 16:, :]
    peak = stats[:, :, :1]
    total = stats[:, :, HEAD_SIZE // 2 : HEAD_SIZE // 2 + 1]
    top = jnp.max(peak, axis=0)
    factor = jnp.exp(peak - top[None])
    return top, jnp.sum(total * factor, axis=0), jnp.sum(numerator * factor, axis=0)


def merge_kernel(parts_ref, out_ref):
    top, total, numerator = merged(parts_ref[...])
    stats = packed(top, total)
    for k in range(out_ref.shape[0]):
        out_ref[k, :16, :] = numerator
        out_ref[k, 16:, :] = stats


def finish_kernel(parts_ref, out_ref):
    _, total, numerator = merged(parts_ref[...])
    attention = (numerator / total).astype(jnp.bfloat16).astype(jnp.float32)
    for k in range(out_ref.shape[0]):
        out_ref[k] = attention


def out_kernel(heads_ref, weight_ref, out_ref):
    trajectories = out_ref.shape[1]
    for t in range(trajectories):
        total = jnp.zeros((heads_ref.shape[1], HEAD_SIZE), jnp.float32)
        for i in range(4):
            total += jnp.dot(
                heads_ref[t * 4 + i].astype(jnp.bfloat16),
                weight_ref[i * HEAD_SIZE : (i + 1) * HEAD_SIZE, :],
                preferred_element_type=jnp.float32,
            )
        out_ref[:, t, :] = total


def prefill_kernel(place_ref, *refs):
    tokens, (own_ref, other_ref, along_ref, across_ref, out_ref, total_ref) = refs[:4], refs[4:]
    step = pl.program_id(0)

    @pl.when(step == 0)
    def _():
        total_ref[...] = jnp.zeros_like(total_ref)

    first = place_ref[2] == 0
    total = total_ref[...]
    for k, token_ref in enumerate(tokens):
        own, other = own_ref[k, 0], other_ref[k, 0]
        rows = jnp.concatenate(
            [jnp.where(first, own, other), jnp.where(first, other, own)], axis=0
        )
        total += jnp.dot(token_ref[...], rows, preferred_element_type=jnp.float32)
    total_ref[...] = total

    @pl.when(step == pl.num_programs(0) - 1)
    def _():
        swapped = pltpu.roll(total, HEAD_SIZE // 2, 1)
        rotated = total * along_ref[...] + swapped * across_ref[...]
        out_ref[...] = rotated.astype(jnp.bfloat16)


def prefill(place, tokens, own, other, along, across):
    rows, columns = tokens.shape[0], own.shape[-1]
    nx, nz = own.shape[:2]

    def token_block(k):
        def index(step, place):
            flipped = (step & 1) * 4 + (step & 2) + (step >> 2)
            return 0, (place[0] ^ flipped) * nx + ((place[1] + nx - k) & (nx - 1))

        return index

    whole = pl.BlockSpec((rows, columns), lambda step, place: (0, 0))
    piece = pl.BlockSpec((nx, 1, *own.shape[2:]), lambda step, place: (0, step, 0, 0))
    return pl.pallas_call(
        prefill_kernel,
        out_shape=jax.ShapeDtypeStruct((rows, columns), jnp.bfloat16),
        grid_spec=pltpu.PrefetchScalarGridSpec(
            num_scalar_prefetch=1,
            grid=(nz,),
            in_specs=[pl.BlockSpec((rows, 2 * HEAD_SIZE), token_block(k)) for k in range(nx)]
            + [piece, piece, whole, whole],
            out_specs=whole,
            scratch_shapes=[pltpu.VMEM((rows, columns), jnp.float32)],
        ),
        cost_estimate=pl.CostEstimate(
            flops=2 * 10**9, bytes_accessed=2 * tokens.size, transcendentals=0
        ),
    )(place, *([tokens] * nx), own, other, along, across)


VMEM = pl.BlockSpec(memory_space=pltpu.VMEM)
SMEM = pl.BlockSpec(memory_space=pltpu.SMEM)


def whole_call(kernel, shape, in_specs=(VMEM,), flops=10**7):
    return pl.pallas_call(
        kernel,
        out_shape=jax.ShapeDtypeStruct(shape, jnp.float32),
        in_specs=list(in_specs),
        out_specs=VMEM,
        cost_estimate=pl.CostEstimate(flops=flops, bytes_accessed=2**20, transcendentals=0),
    )


def shards(
    prefix_tokens,
    key_value_weight,
    prefix_lengths,
    start_offsets,
    queries,
    key_value_cache,
    cache_lengths,
    out_weight,
):
    columns = key_value_weight.shape[1]
    nz, nx, nc, ny, nw = (lax.axis_size(a) for a in ("z", "x", "c", "y", "w"))
    nxc, ngy = nx * nc, ny * nw

    blocks = key_value_weight[None]
    for far in (4, 2, 1):
        other = lax.ppermute(blocks, "z", [(i, i ^ far) for i in range(nz)])
        blocks = jnp.concatenate([blocks, other], axis=0)
    sides = [blocks]
    for k in range(1, nx):
        sides.append(lax.ppermute(blocks, "x", [(i, (i + k) % nx) for i in range(nx)]))
    own = jnp.stack(sides)
    other = lax.ppermute(own, "c", [(0, 1), (1, 0)])
    place = jnp.stack([lax.axis_index(a) for a in GX]).astype(jnp.int32)
    along, across = rotation(lax.axis_index(GY), prefix_lengths, start_offsets)
    prefix_kv = prefill(place, prefix_tokens, own, other, along, across)

    trajectories = queries.shape[0]
    cache_per_shard = key_value_cache.shape[2]
    limits = cache_lengths - lax.axis_index(GX) * cache_per_shard
    ordered = queries.reshape(trajectories, KEY_VALUE_HEADS, 2, 4, HEAD_SIZE)
    ordered = ordered.swapaxes(2, 3).reshape(trajectories, QUERY_HEADS, HEAD_SIZE)
    parts = whole_call(
        block_kernel, (nxc, 32, HEAD_SIZE), (SMEM, VMEM, VMEM), flops=10**9
    )(limits, ordered, key_value_cache)
    parts = swap(parts, ("x", "c"))
    parts = whole_call(merge_kernel, (nz, 32, HEAD_SIZE))(parts)
    parts = swap(parts, "z")
    attention = whole_call(finish_kernel, (nxc, ngy, HEAD_SIZE))(parts)
    heads = swap(attention.reshape(nxc * ngy, 1, HEAD_SIZE), ("x", "c", *GY))
    mixed = whole_call(out_kernel, (ngy, trajectories, columns), (VMEM, VMEM))(
        heads.reshape(nxc, ngy, HEAD_SIZE), out_weight
    )
    mixed = swap(mixed, GY)
    return (prefix_kv, jnp.sum(mixed, axis=0).astype(jnp.bfloat16))


def solution(mesh):
    finer = Mesh(mesh.devices.reshape(8, 4, 2, 4, 4), ("z", "x", "c", "y", "w"))
    return jax.shard_map(
        shards,
        mesh=finer,
        in_specs=(
            P(GX, None),
            P(GX, GY),
            P(GX),
            P(GX),
            P(GY, None),
            P(None, GY, GX, None),
            P(GY),
            P(GY, GX),
        ),
        out_specs=(P(GX, GY), P(GY, GX)),
        check_vma=False,
    )
```

time: 181 us -> 165 us (0.912)
  the two profiles are of different devices: /device:TPU:2 before, /device:TPU:32 now
where the time goes in v1:
time: 165 us; the launch traced here: 164 us
  starting transfers between devices  77 us (47%)
  waiting for transfers between devices  49.5 us (30%)
  Pallas kernels  22 us (13%)
  other arithmetic  9.95 us (6%)
  local copies, waits for them, and re-layouts  4.33 us (3%)
    all_to_all x4, waiting for transfers between devices, swap(): return lax.all_to_all(pieces, axis, 0, 0, tiled=True)  45.2 us
    all_to_all x4, starting transfers between devices, swap(): return lax.all_to_all(pieces, axis, 0, 0, tiled=True)  35.4 us
    ppermute x3, starting transfers between devices, shards(): other = lax.ppermute(blocks, 'z', [(i, i ^ far) for i in range(nz)])  27.3 us
    ppermute x3, starting transfers between devices, shards(): lax.ppermute(blocks, 'x', [(i, (i + k) % nx) for i in range(nx)])  12.4 us
    pallas_call x1, Pallas kernels, prefill(): pl.pallas_call(prefill_kernel, out_shape=jax.ShapeDtypeStruct((rows, colu...  11.1 us
    pallas_call x1, Pallas kernels, shards(): whole_call(block_kernel, (nxc, 32, HEAD_SIZE), (SMEM, VMEM, VMEM), flops=...  5.74 us
    ppermute x3, waiting for transfers between devices, shards(): other = lax.ppermute(blocks, 'z', [(i, i ^ far) for i in range(nz)])  4.31 us
  transfers between devices with their start and end apart: 11, of which 5 were waited for; matrix products, arithmetic and copies ran while one was open for 6% of the time, Pallas kernels for 13%

profile of v1, /device:TPU:32, one launch (start us, length us, event | category | flops | bytes accessed | tf_op | source)
XLA Modules:
  0.0 163.7 jit_solution(17470050369444593841)
XLA Ops:
  0.6 9.1 %collective-permute-start = (bf16[1,128,128]{2,1,0:T(8,128)(2,1)}, bf16[1,128,128]{2,1,0:T(8,128)(2,1)S(1)}, u32[]{:S(2)}, u32[]{:S(2)}) collective-permute-start(bf16[1,128,128]{2,1,0:T(8,128)(2,1)} %bitcast.22), channel_id=1, source_target_pairs={{0,512},{128,640},{256,768},{384,896},{512,0},{640,128},{768,256},... | collective-permute-start | bytes 98312 | tf_op jit(solution)/shard_map/ppermute | solution.py:196
  9.7 2.1 %collective-permute-done = bf16[1,128,128]{2,1,0:T(8,128)(2,1)S(1)} collective-permute-done((bf16[1,128,128]{2,1,0:T(8,128)(2,1)}, bf16[1,128,128]{2,1,0:T(8,128)(2,1)S(1)}, u32[]{:S(2)}, u32[]{:S(2)}) %collective-permute-start) | collective-permute-done | bytes 32800 | tf_op jit(solution)/shard_map/ppermute | solution.py:196
  11.8 0.8 pad_maximum_fusion.3
  12.6 5.2 %collective-permute-start.1 = (bf16[2,128,128]{2,1,0:T(8,128)(2,1)S(1)}, bf16[2,128,128]{2,1,0:T(8,128)(2,1)S(1)}, u32[]{:S(2)}, u32[]{:S(2)}) collective-permute-start(bf16[2,128,128]{2,1,0:T(8,128)(2,1)S(1)} %pad_maximum_fusion.3), channel_id=1, source_target_pairs={{0,256},{128,384},{256,0},{384,128},{512,768},{640,896},{768,512},... | collective-permute-start | bytes 196616 | tf_op jit(solution)/shard_map/ppermute | solution.py:196
  17.8 2.2 %collective-permute-done.1 = bf16[2,128,128]{2,1,0:T(8,128)(2,1)S(1)} collective-permute-done((bf16[2,128,128]{2,1,0:T(8,128)(2,1)S(1)}, bf16[2,128,128]{2,1,0:T(8,128)(2,1)S(1)}, u32[]{:S(2)}, u32[]{:S(2)}) %collective-permute-start.1) | collective-permute-done | bytes 65568 | tf_op jit(solution)/shard_map/ppermute | solution.py:196
  20.0 0.8 pad_maximum_fusion.2
  20.8 13.0 %collective-permute-start.2 = (bf16[4,128,128]{2,1,0:T(8,128)(2,1)S(1)}, bf16[4,128,128]{2,1,0:T(8,128)(2,1)S(1)}, u32[]{:S(2)}, u32[]{:S(2)}) collective-permute-start(bf16[4,128,128]{2,1,0:T(8,128)(2,1)S(1)} %pad_maximum_fusion.2), channel_id=1, source_target_pairs={{0,128},{128,0},{256,384},{384,256},{512,640},{640,512},{768,896},... | collective-permute-start | bytes 393224 | tf_op jit(solution)/shard_map/ppermute | solution.py:196
  33.8 1.2 broadcast_subtract_fusion.limits_ref
  35.0 0.8 reshape.78
  35.8 0.6 copy.11
  36.4 5.7 %shard_map.96 = f32[8,32,128]{2,1,0:T(8,128)} custom-call(s32[2]{0:T(128)} %broadcast_subtract_fusion.limits_ref, bf16[2,64,128]{2,1,0:T(8,128)(2,1)} %bitcast.31, bf16[2,2,128,1024]{3,2,1,0:T(8,128)(2,1)} %cache_ref.1), custom_call_target="tpu_custom_call" | custom-call | flops 1000000000 | bytes 1048576 | tf_op jit(solution)/shard_map/pallas_call | solution.py:212
  42.1 3.4 %all-to-all-start = ((f32[8,32,128]{2,1,0:T(8,128)}), f32[8,32,128]{2,1,0:T(8,128)S(1)}, u32[]{:S(2)}, u32[]{:S(2)}) async-start(f32[8,32,128]{2,1,0:T(8,128)} %shard_map.96), calls=%async_computation | async-start | bytes 262144 | tf_op jit(solution)/shard_map/all_to_all | solution.py:22
  45.5 0.0 collective-permute-done.2
  45.5 0.8 fusion.7
  46.3 5.3 %collective-permute-start.4 = (bf16[8,128,128]{2,1,0:T(8,128)(2,1)S(1)}, bf16[8,128,128]{2,1,0:T(8,128)(2,1)S(1)}, u32[]{:S(2)}, u32[]{:S(2)}) collective-permute-start(bf16[8,128,128]{2,1,0:T(8,128)(2,1)S(1)} %get-tuple-element.3), channel_id=1, source_target_pairs={{0,64},{32,96},{64,0},{96,32},{1,65},{33,97},{65,1},{97,33},{2,66}... | collective-permute-start | bytes 786440 | tf_op jit(solution)/shard_map/ppermute | solution.py:200
  51.7 2.5 %collective-permute-start.3 = (bf16[8,128,128]{2,1,0:T(8,128)(2,1)S(1)}, bf16[8,128,128]{2,1,0:T(8,128)(2,1)S(1)}, u32[]{:S(2)}, u32[]{:S(2)}) collective-permute-start(bf16[8,128,128]{2,1,0:T(8,128)(2,1)S(1)} %get-tuple-element.3), channel_id=1, source_target_pairs={{0,32},{32,64},{64,96},{96,0},{1,33},{33,65},{65,97},{97,1},{2,34}... | collective-permute-start | bytes 786440 | tf_op jit(solution)/shard_map/ppermute | solution.py:200
  54.2 4.6 %collective-permute-start.5 = (bf16[8,128,128]{2,1,0:T(8,128)(2,1)S(1)}, bf16[8,128,128]{2,1,0:T(8,128)(2,1)S(1)}, u32[]{:S(2)}, u32[]{:S(2)}) collective-permute-start(bf16[8,128,128]{2,1,0:T(8,128)(2,1)S(1)} %get-tuple-element.3), channel_id=1, source_target_pairs={{0,96},{32,0},{64,32},{96,64},{1,97},{33,1},{65,33},{97,65},{2,98}... | collective-permute-start | bytes 786440 | tf_op jit(solution)/shard_map/ppermute | solution.py:200
  58.8 0.0 all-to-all-done.parts_ref
  58.8 0.0 copy-start.3
  58.8 0.6 copy-done.3
  59.4 1.7 %shard_map.97 = f32[8,32,128]{2,1,0:T(8,128)} custom-call(f32[8,32,128]{2,1,0:T(8,128)} %copy-done.3), custom_call_target="tpu_custom_call" | custom-call | flops 10000000 | bytes 1048576 | tf_op jit(solution)/shard_map/pallas_call | solution.py:216
  61.2 3.3 %all-to-all-start.1 = ((f32[8,32,128]{2,1,0:T(8,128)}), f32[8,32,128]{2,1,0:T(8,128)S(1)}, u32[]{:S(2)}, u32[]{:S(2)}) async-start(f32[8,32,128]{2,1,0:T(8,128)} %shard_map.97), calls=%async_computation.1 | async-start | bytes 262144 | tf_op jit(solution)/shard_map/all_to_all | solution.py:22
  64.5 0.0 collective-permute-done.4
  64.5 0.0 collective-permute-done.3
  64.5 0.0 collective-permute-done.5
  64.5 0.1 pad_maximum_fusion.refs_4_
  64.7 0.0 copy-start
  64.7 1.9 %collective-permute-start.6 = (bf16[4,8,128,128]{3,2,1,0:T(8,128)(2,1)S(1)}, bf16[4,8,128,128]{3,2,1,0:T(8,128)(2,1)S(1)}, u32[]{:S(2)}, u32[]{:S(2)}) collective-permute-start(bf16[4,8,128,128]{3,2,1,0:T(8,128)(2,1)S(1)} %pad_maximum_fusion.refs_4_), channel_id=1, source_target_pairs={{0,16},{16,0},{1,17},{17,1},{2,18},{18,2},{3,19},{19,3},{4,20},{20... | collective-permute-start | bytes 3145736 | tf_op jit(solution)/shard_map/ppermute | solution.py:202
  66.6 0.7 fusion.3
  67.4 0.7 broadcast_and_fusion
  68.1 7.3 %all-to-all-done.1.parts_ref = f32[8,32,128]{2,1,0:T(8,128)S(1)} async-done(((f32[8,32,128]{2,1,0:T(8,128)}), f32[8,32,128]{2,1,0:T(8,128)S(1)}, u32[]{:S(2)}, u32[]{:S(2)}) %all-to-all-start.1) | async-done | bytes 131104 | tf_op jit(solution)/shard_map/all_to_all | solution.py:22
  75.4 0.0 copy-start.2
  75.4 0.7 copy-done.2
  76.0 1.7 %shard_map.98 = f32[8,16,128]{2,1,0:T(8,128)} custom-call(f32[8,32,128]{2,1,0:T(8,128)} %copy-done.2), custom_call_target="tpu_custom_call" | custom-call | flops 10000000 | bytes 1048576 | tf_op jit(solution)/shard_map/pallas_call | solution.py:218
  77.7 25.2 %all-to-all-start.2 = ((f32[128,1,128]{2,1,0:T(1,128)}), f32[128,1,128]{2,1,0:T(1,128)S(1)}, u32[]{:S(2)}, u32[]{:S(2)}) async-start(f32[128,1,128]{2,1,0:T(1,128)} %bitcast.26), calls=%async_computation.2 | async-start | bytes 131072 | tf_op jit(solution)/shard_map/all_to_all | solution.py:22
  102.9 0.6 pad_add_fusion.place_ref
  103.6 0.7 convert_bitcast_fusion
  104.3 2.9 %fusion.2 = (f32[768,128]{1,0:T(8,128)}, f32[768,128]{1,0:T(8,128)}) fusion(f32[128]{0:T(128)S(1)} %fusion.6, f32[768]{0:T(1024)S(1)} %convert_bitcast_fusion, pred[768]{0:T(1024)(128)(4,1)S(1)} %broadcast_and_fusion, pred[128]{0:T(512)(128)(4,1)S(1)} %iota_compare_fusion.1, pred[]{:T(512)S(6)} %lt.48, pred[768]{0:T(1024)(128)(4,1)S(1)} %fusion.3), kind=kLoop, calls=%fused_computation.6 | loop fusion | flops 589824 | bytes 791681 | tf_op jit(solution)/shard_map/jit(_where)/select_n | solution.py:37
  107.2 25.7 %all-to-all-done.2 = f32[128,1,128]{2,1,0:T(1,128)S(1)} async-done(((f32[128,1,128]{2,1,0:T(1,128)}), f32[128,1,128]{2,1,0:T(1,128)S(1)}, u32[]{:S(2)}, u32[]{:S(2)}) %all-to-all-start.2) | async-done | bytes 65568 | tf_op jit(solution)/shard_map/all_to_all | solution.py:22
  132.9 0.0 copy-start.4
  132.9 0.6 copy-done.4
  133.5 1.7 %shard_map.99 = f32[16,2,128]{2,1,0:T(2,128)} custom-call(f32[8,16,128]{2,1,0:T(8,128)} %bitcast.27, bf16[512,128]{1,0:T(8,128)(2,1)} %weight_ref.1), custom_call_target="tpu_custom_call" | custom-call | flops 10000000 | bytes 1048576 | tf_op jit(solution)/shard_map/pallas_call | solution.py:220
  135.3 3.5 %all-to-all-start.3 = ((f32[16,2,128]{2,1,0:T(2,128)}), f32[16,2,128]{2,1,0:T(2,128)S(1)}, u32[]{:S(2)}, u32[]{:S(2)}) async-start(f32[16,2,128]{2,1,0:T(2,128)} %shard_map.99), calls=%async_computation.3 | async-start | bytes 32768 | tf_op jit(solution)/shard_map/all_to_all | solution.py:22
  138.8 0.0 collective-permute-done.6.refs_5_
  138.8 0.0 copy-start.1
  138.8 0.0 copy-done
  138.8 1.0 copy-done.1
  139.8 11.1 %shard_map.95 = bf16[768,128]{1,0:T(8,128)(2,1)} custom-call(s32[3]{0:T(128)} %pad_add_fusion.place_ref, bf16[768,8192]{1,0:T(8,128)(2,1)} %refs_3_.1, bf16[768,8192]{1,0:T(8,128)(2,1)} %refs_3_.1, bf16[768,8192]{1,0:T(8,128)(2,1)} %refs_3_.1, bf16[768,8192]{1,0:T(8,128)(2,1)} %refs_3_.1, bf16[4,8,128,128]{3,2,1,0:T(8,128)(2,1)} %copy-done, ...), custom_call_target="tpu_custom_call" | custom-call | flops 2000000000 | bytes 12582912 | tf_op jit(solution)/shard_map/pallas_call | solution.py:149
  150.9 12.2 %all-to-all-done.3 = f32[16,2,128]{2,1,0:T(2,128)S(1)} async-done(((f32[16,2,128]{2,1,0:T(2,128)}), f32[16,2,128]{2,1,0:T(2,128)S(1)}, u32[]{:S(2)}, u32[]{:S(2)}) %all-to-all-start.3) | async-done | bytes 16416 | tf_op jit(solution)/shard_map/all_to_all | solution.py:22
  163.1 0.5 reduce_sum.9
  (2 shorter events, 0.0 us)
Async XLA Ops:
  0.6 11.2 %collective-permute-start = (bf16[1,128,128]{2,1,0:T(8,128)(2,1)}, bf16[1,128,128]{2,1,0:T(8,128)(2,1)S(1)}, u32[]{:S(2)}, u32[]{:S(2)}) collective-permute-start(bf16[1,128,128]{2,1,0:T(8,128)(2,1)} %bitcast.22), channel_id=1, source_target_pairs={{0,512},{128,640},{256,768},{384,896},{512,0},{640,128},{768,256},... | collective-permute-start | bytes 98312 | tf_op jit(solution)/shard_map/ppermute | solution.py:196
  12.6 7.4 %collective-permute-start.1 = (bf16[2,128,128]{2,1,0:T(8,128)(2,1)S(1)}, bf16[2,128,128]{2,1,0:T(8,128)(2,1)S(1)}, u32[]{:S(2)}, u32[]{:S(2)}) collective-permute-start(bf16[2,128,128]{2,1,0:T(8,128)(2,1)S(1)} %pad_maximum_fusion.3), channel_id=1, source_target_pairs={{0,256},{128,384},{256,0},{384,128},{512,768},{640,896},{768,512},... | collective-permute-start | bytes 196616 | tf_op jit(solution)/shard_map/ppermute | solution.py:196
  20.8 24.8 %collective-permute-start.2 = (bf16[4,128,128]{2,1,0:T(8,128)(2,1)S(1)}, bf16[4,128,128]{2,1,0:T(8,128)(2,1)S(1)}, u32[]{:S(2)}, u32[]{:S(2)}) collective-permute-start(bf16[4,128,128]{2,1,0:T(8,128)(2,1)S(1)} %pad_maximum_fusion.2), channel_id=1, source_target_pairs={{0,128},{128,0},{256,384},{384,256},{512,640},{640,512},{768,896},... | collective-permute-start | bytes 393224 | tf_op jit(solution)/shard_map/ppermute | solution.py:196
  42.1 16.6 %all-to-all-start = ((f32[8,32,128]{2,1,0:T(8,128)}), f32[8,32,128]{2,1,0:T(8,128)S(1)}, u32[]{:S(2)}, u32[]{:S(2)}) async-start(f32[8,32,128]{2,1,0:T(8,128)} %shard_map.96), calls=%async_computation | async-start | bytes 262144 | tf_op jit(solution)/shard_map/all_to_all | solution.py:22
  46.3 18.2 %collective-permute-start.4 = (bf16[8,128,128]{2,1,0:T(8,128)(2,1)S(1)}, bf16[8,128,128]{2,1,0:T(8,128)(2,1)S(1)}, u32[]{:S(2)}, u32[]{:S(2)}) collective-permute-start(bf16[8,128,128]{2,1,0:T(8,128)(2,1)S(1)} %get-tuple-element.3), channel_id=1, source_target_pairs={{0,64},{32,96},{64,0},{96,32},{1,65},{33,97},{65,1},{97,33},{2,66}... | collective-permute-start | bytes 786440 | tf_op jit(solution)/shard_map/ppermute | solution.py:200
  51.7 12.8 %collective-permute-start.3 = (bf16[8,128,128]{2,1,0:T(8,128)(2,1)S(1)}, bf16[8,128,128]{2,1,0:T(8,128)(2,1)S(1)}, u32[]{:S(2)}, u32[]{:S(2)}) collective-permute-start(bf16[8,128,128]{2,1,0:T(8,128)(2,1)S(1)} %get-tuple-element.3), channel_id=1, source_target_pairs={{0,32},{32,64},{64,96},{96,0},{1,33},{33,65},{65,97},{97,1},{2,34}... | collective-permute-start | bytes 786440 | tf_op jit(solution)/shard_map/ppermute | solution.py:200
  54.2 10.3 %collective-permute-start.5 = (bf16[8,128,128]{2,1,0:T(8,128)(2,1)S(1)}, bf16[8,128,128]{2,1,0:T(8,128)(2,1)S(1)}, u32[]{:S(2)}, u32[]{:S(2)}) collective-permute-start(bf16[8,128,128]{2,1,0:T(8,128)(2,1)S(1)} %get-tuple-element.3), channel_id=1, source_target_pairs={{0,96},{32,0},{64,32},{96,64},{1,97},{33,1},{65,33},{97,65},{2,98}... | collective-permute-start | bytes 786440 | tf_op jit(solution)/shard_map/ppermute | solution.py:200
  58.8 0.7 copy-start.3
  61.2 14.2 %all-to-all-start.1 = ((f32[8,32,128]{2,1,0:T(8,128)}), f32[8,32,128]{2,1,0:T(8,128)S(1)}, u32[]{:S(2)}, u32[]{:S(2)}) async-start(f32[8,32,128]{2,1,0:T(8,128)} %shard_map.97), calls=%async_computation.1 | async-start | bytes 262144 | tf_op jit(solution)/shard_map/all_to_all | solution.py:22
  64.7 74.1 %copy-start = (bf16[4,8,128,128]{3,2,1,0:T(8,128)(2,1)}, bf16[4,8,128,128]{3,2,1,0:T(8,128)(2,1)S(1)}, u32[]{:S(2)}) copy-start(bf16[4,8,128,128]{3,2,1,0:T(8,128)(2,1)S(1)} %pad_maximum_fusion.refs_4_) | copy-start | bytes 3145732
  64.7 74.1 %collective-permute-start.6 = (bf16[4,8,128,128]{3,2,1,0:T(8,128)(2,1)S(1)}, bf16[4,8,128,128]{3,2,1,0:T(8,128)(2,1)S(1)}, u32[]{:S(2)}, u32[]{:S(2)}) collective-permute-start(bf16[4,8,128,128]{3,2,1,0:T(8,128)(2,1)S(1)} %pad_maximum_fusion.refs_4_), channel_id=1, source_target_pairs={{0,16},{16,0},{1,17},{17,1},{2,18},{18,2},{3,19},{19,3},{4,20},{20... | collective-permute-start | bytes 3145736 | tf_op jit(solution)/shard_map/ppermute | solution.py:202
  75.4 0.7 copy-start.2
  77.7 55.2 %all-to-all-start.2 = ((f32[128,1,128]{2,1,0:T(1,128)}), f32[128,1,128]{2,1,0:T(1,128)S(1)}, u32[]{:S(2)}, u32[]{:S(2)}) async-start(f32[128,1,128]{2,1,0:T(1,128)} %bitcast.26), calls=%async_computation.2 | async-start | bytes 131072 | tf_op jit(solution)/shard_map/all_to_all | solution.py:22
  132.9 0.6 copy-start.4
  135.3 27.9 %all-to-all-start.3 = ((f32[16,2,128]{2,1,0:T(2,128)}), f32[16,2,128]{2,1,0:T(2,128)S(1)}, u32[]{:S(2)}, u32[]{:S(2)}) async-start(f32[16,2,128]{2,1,0:T(2,128)} %shard_map.99), calls=%async_computation.3 | async-start | bytes 32768 | tf_op jit(solution)/shard_map/all_to_all | solution.py:22
  138.8 1.0 copy-start.1

commit v2 on v1

v2 whole, which is shorter than its diff:
```python
import jax
import jax.numpy as jnp
import numpy as np
from jax import lax
from jax.experimental import pallas as pl
from jax.experimental.pallas import tpu as pltpu
from jax.sharding import Mesh
from jax.sharding import PartitionSpec as P

QUERY_HEADS = 64
KEY_VALUE_HEADS = 8
HEAD_SIZE = 128
SLOT = 128
GX = ("z", "x", "c")
GY = ("y", "w")
GROUP = QUERY_HEADS // KEY_VALUE_HEADS

rope_base = 500000.0
masked_score = -1e30


def swap(pieces, axis):
    return lax.all_to_all(pieces, axis, 0, 0, tiled=True)


def turns():
    half_width = HEAD_SIZE // 2
    inverse = rope_base ** (-2.0 * (np.arange(HEAD_SIZE) % half_width) / HEAD_SIZE)
    angles = np.arange(SLOT)[:, None] * inverse[None, :]
    return tuple(np.float32(table) for table in (inverse, np.cos(angles), np.sin(angles)))


def packed(peak, total):
    lane = lax.broadcasted_iota(jnp.int32, (peak.shape[0], HEAD_SIZE), 1)
    return jnp.where(lane < HEAD_SIZE // 2, peak, total)


def block_kernel(place_ref, limits_ref, query_ref, cache_ref, out_ref):
    trajectories, positions = cache_ref.shape[1], cache_ref.shape[2]
    side = place_ref[2]
    pairs = [(t, g) for t in range(trajectories) for g in range(KEY_VALUE_HEADS)]
    columns = [slice(g * HEAD_SIZE, (g + 1) * HEAD_SIZE) for g in range(KEY_VALUE_HEADS)]
    scores = jnp.concatenate(
        [
            lax.dot_general(
                query_ref[t, g * GROUP : (g + 1) * GROUP, :],
                cache_ref[0, t, :, columns[g]],
                (((1,), (1,)), ((), ())),
                preferred_element_type=jnp.float32,
            )
            for t, g in pairs
        ],
        axis=0,
    ) * HEAD_SIZE ** (-0.5)
    position = lax.broadcasted_iota(jnp.int32, (QUERY_HEADS, positions), 1)
    valid = jnp.concatenate([position < limits_ref[t] for t in range(trajectories)], axis=0)
    peak = jnp.max(jnp.where(valid, scores, masked_score), axis=1, keepdims=True)
    weights = jnp.where(valid, jnp.exp(scores - peak), 0.0)
    stats = packed(peak, jnp.sum(weights, axis=1, keepdims=True))
    for k, (t, g) in enumerate(pairs):
        rows = slice(k * GROUP, (k + 1) * GROUP)
        values = jnp.dot(
            weights[rows].astype(jnp.bfloat16),
            cache_ref[1, t, :, columns[g]],
            preferred_element_type=jnp.float32,
        )
        for half in range(2):
            kept, slot, row = half ^ side, t * 2 + g % 2, (g // 2) * 4
            some = slice(half * 4, half * 4 + 4)
            out_ref[kept, slot, row : row + 4, :] = values[some]
            out_ref[kept, slot, 16 + row : 20 + row, :] = stats[rows][some]


def merged(one, two):
    half_width = HEAD_SIZE // 2
    peaks = [part[16:, :1] for part in (one, two)]
    totals = [part[16:, half_width : half_width + 1] for part in (one, two)]
    top = jnp.maximum(*peaks)
    factors = [jnp.exp(peak - top) for peak in peaks]
    total = totals[0] * factors[0] + totals[1] * factors[1]
    return top, total, one[:16] * factors[0] + two[:16] * factors[1]


def store_merged(out_ref, index, one, two):
    top, total, numerator = merged(one, two)
    out_ref[(*index, slice(0, 16))] = numerator
    out_ref[(*index, slice(16, 32))] = packed(top, total)


def merge_pairs_kernel(place_ref, mine_ref, other_ref, out_ref):
    for slot in range(4):
        index = (slot & 1) ^ (place_ref[1] & 1), slot >> 1
        store_merged(out_ref, index, mine_ref[0, slot], other_ref[slot])


def merge_sides_kernel(place_ref, mine_ref, other_ref, out_ref):
    for slot in range(2):
        index = (slot ^ (place_ref[1] >> 1),)
        store_merged(out_ref, index, mine_ref[0, slot], other_ref[slot])


def merge_last_kernel(mine_ref, other_ref, out_ref):
    store_merged(out_ref, (), mine_ref[0], other_ref[...])


def merge_kernel(mine_ref, other_ref, out_ref):
    store_merged(out_ref, (), mine_ref[...], other_ref[...])


def finish_kernel(mine_ref, other_ref, out_ref):
    _, total, numerator = merged(mine_ref[...], other_ref[...])
    attention = (numerator / total).astype(jnp.bfloat16).astype(jnp.float32)
    for k in range(out_ref.shape[0]):
        out_ref[k] = attention


def out_kernel(heads_ref, weight_ref, out_ref):
    ny, trajectories = out_ref.shape[:2]
    total = jnp.zeros((trajectories * ny, HEAD_SIZE), jnp.float32)
    for quarter in range(4):
        heads = [
            jnp.concatenate(
                [
                    heads_ref[pl.ds((t * 4 + quarter) * 4 * ny + i, ny, stride=4), :]
                    for t in range(trajectories)
                ],
                axis=0,
            )
            for i in range(4)
        ]
        total += jnp.dot(
            jnp.concatenate(heads, axis=1).astype(jnp.bfloat16),
            weight_ref[quarter],
            preferred_element_type=jnp.float32,
        )
    for t in range(trajectories):
        out_ref[:, t, :] = total[t * ny : (t + 1) * ny]


def prefill_kernel(place_ref, *refs):
    tokens, refs = refs[:4], refs[4:]
    own_ref, other_ref, live_ref, starts_ref, cosine_ref, sine_ref, out_ref, total_ref = refs
    step = pl.program_id(0)

    @pl.when(step == 0)
    def _():
        total_ref[...] = jnp.zeros_like(total_ref)

    first = place_ref[2] == 0
    total = total_ref[...]
    for k, token_ref in enumerate(tokens):
        own, other = own_ref[k, 0], other_ref[k, 0]
        rows = jnp.concatenate(
            [jnp.where(first, own, other), jnp.where(first, other, own)], axis=0
        )
        total += jnp.dot(token_ref[...], rows, preferred_element_type=jnp.float32)
    total_ref[...] = total

    @pl.when(step == pl.num_programs(0) - 1)
    def _():
        prefixes = starts_ref.shape[0] // 2
        slot = lax.broadcasted_iota(jnp.int32, (SLOT, HEAD_SIZE), 0)
        front = lax.broadcasted_iota(jnp.int32, (SLOT, HEAD_SIZE), 1) < HEAD_SIZE // 2
        for i in range(prefixes):
            rows = slice(i * SLOT, (i + 1) * SLOT)
            plain = total_ref[rows, :]
            along, across = starts_ref[i : i + 1, :], starts_ref[prefixes + i : prefixes + i + 1, :]
            cosine = cosine_ref[...] * along - sine_ref[...] * across
            sine = sine_ref[...] * along + cosine_ref[...] * across
            swapped = pltpu.roll(plain, HEAD_SIZE // 2, 1)
            turned = plain * cosine + swapped * jnp.where(front, -sine, sine)
            kept = jnp.where(place_ref[3] > 0, turned, plain)
            out_ref[rows, :] = jnp.where(slot < live_ref[i], kept, 0.0).astype(jnp.bfloat16)


def prefill(place, tokens, own, other, live, starts, cosine, sine):
    rows, columns = tokens.shape[0], own.shape[-1]
    nx, nz = own.shape[:2]

    def token_block(k):
        def index(step, place):
            flipped = (step & 1) * 4 + (step & 2) + (step >> 2)
            return 0, (place[0] ^ flipped) * nx + ((place[1] + nx - k) & (nx - 1))

        return index

    def whole(array):
        return pl.BlockSpec(array.shape, lambda step, place: (0, 0))

    piece = pl.BlockSpec((nx, 1, *own.shape[2:]), lambda step, place: (0, step, 0, 0))
    result = jax.ShapeDtypeStruct((rows, columns), jnp.bfloat16)
    return pl.pallas_call(
        prefill_kernel,
        out_shape=result,
        grid_spec=pltpu.PrefetchScalarGridSpec(
            num_scalar_prefetch=1,
            grid=(nz,),
            in_specs=[pl.BlockSpec((rows, 2 * HEAD_SIZE), token_block(k)) for k in range(nx)]
            + [piece, piece, SMEM, whole(starts), whole(cosine), whole(sine)],
            out_specs=whole(result),
            scratch_shapes=[pltpu.VMEM((rows, columns), jnp.float32)],
        ),
        cost_estimate=pl.CostEstimate(
            flops=2 * 10**9, bytes_accessed=2 * tokens.size, transcendentals=0
        ),
    )(place, *([tokens] * nx), own, other, live, starts, cosine, sine)


VMEM = pl.BlockSpec(memory_space=pltpu.VMEM)
SMEM = pl.BlockSpec(memory_space=pltpu.SMEM)


def whole_call(kernel, shape, in_specs=(VMEM,), flops=10**7):
    return pl.pallas_call(
        kernel,
        out_shape=jax.ShapeDtypeStruct(shape, jnp.float32),
        in_specs=list(in_specs),
        out_specs=VMEM,
        cost_estimate=pl.CostEstimate(flops=flops, bytes_accessed=2**20, transcendentals=0),
    )


def shards(
    prefix_tokens,
    key_value_weight,
    prefix_lengths,
    start_offsets,
    queries,
    key_value_cache,
    cache_lengths,
    out_weight,
):
    columns = key_value_weight.shape[1]
    nz, nx, nc, ny, nw = (lax.axis_size(a) for a in ("z", "x", "c", "y", "w"))
    nxc = nx * nc

    blocks = key_value_weight[None]
    for far in (4, 2, 1):
        other = lax.ppermute(blocks, "z", [(i, i ^ far) for i in range(nz)])
        blocks = jnp.concatenate([blocks, other], axis=0)
    sides = [blocks]
    for k in range(1, nx):
        sides.append(lax.ppermute(blocks, "x", [(i, (i + k) % nx) for i in range(nx)]))
    own = jnp.stack(sides)
    other = lax.ppermute(own, "c", [(0, 1), (1, 0)])
    column = lax.axis_index(GY)
    place = jnp.stack([*(lax.axis_index(a) for a in GX), KEY_VALUE_HEADS - column])
    inverse, cosine, sine = turns()
    angles = start_offsets.astype(jnp.float32)[:, None] * inverse[None, :]
    starts = jnp.concatenate([jnp.cos(angles), jnp.sin(angles)], axis=0)
    prefix_kv = prefill(
        place, prefix_tokens, own, other, prefix_lengths, starts, cosine, sine
    )

    out_rows = swap(jnp.broadcast_to(out_weight[None], (nw, *out_weight.shape)), "w")

    trajectories = queries.shape[0]
    cache_per_shard = key_value_cache.shape[2]
    limits = cache_lengths - lax.axis_index(GX) * cache_per_shard
    by_head = queries.reshape(trajectories, QUERY_HEADS, HEAD_SIZE)
    parts = whole_call(
        block_kernel, (2, nx, 32, HEAD_SIZE), (SMEM, SMEM, VMEM, VMEM), flops=10**9
    )(place, limits, by_head, key_value_cache)
    other = lax.ppermute(parts[1], "c", [(0, 1), (1, 0)])
    parts = whole_call(merge_pairs_kernel, (2, 2, 32, HEAD_SIZE), (SMEM, VMEM, VMEM))(
        place, parts, other
    )
    other = lax.ppermute(parts[1], "x", [(i, i ^ 1) for i in range(nx)])
    parts = whole_call(merge_sides_kernel, (2, 32, HEAD_SIZE), (SMEM, VMEM, VMEM))(
        place, parts, other
    )
    other = lax.ppermute(parts[1], "x", [(i, i ^ 2) for i in range(nx)])
    parts = whole_call(merge_last_kernel, (32, HEAD_SIZE), (VMEM, VMEM))(parts, other)
    other = lax.ppermute(parts, "z", [(i, i ^ 1) for i in range(nz)])
    parts = whole_call(merge_kernel, (32, HEAD_SIZE), (VMEM, VMEM))(parts, other)
    other = lax.ppermute(parts, "z", [(i, i ^ 2) for i in range(nz)])
    parts = whole_call(merge_kernel, (32, HEAD_SIZE), (VMEM, VMEM))(parts, other)
    other = lax.ppermute(parts, "z", [(i, i ^ 4) for i in range(nz)])
    attention = whole_call(finish_kernel, (nxc, 16, HEAD_SIZE), (VMEM, VMEM))(parts, other)
    heads = swap(attention.reshape(nxc * ny, 4, HEAD_SIZE), ("x", "c", "y"))
    mixed = whole_call(out_kernel, (ny, trajectories, columns), (VMEM, VMEM))(
        heads.reshape(nxc * ny * 4, HEAD_SIZE), out_rows
    )
    mixed = swap(mixed, "y")
    return (prefix_kv, jnp.sum(mixed, axis=0).astype(jnp.bfloat16))


def solution(mesh):
    finer = Mesh(mesh.devices.reshape(8, 4, 2, 4, 4), ("z", "x", "c", "y", "w"))
    return jax.shard_map(
        shards,
        mesh=finer,
        in_specs=(
            P(GX, None),
            P(GX, GY),
            P(GX),
            P(GX),
            P(GY, None),
            P(None, GY, GX, None),
            P(GY),
            P(GY, GX),
        ),
        out_specs=(P(GX, GY), P(GY, GX)),
        check_vma=False,
    )
```

time: 165 us -> 207 us (1.25)
  the two profiles are of different devices: /device:TPU:32 before, /device:TPU:73 now
where the time goes in v2:
time: 207 us; the launch traced here: 206 us
  starting transfers between devices  76.3 us (37%)
  waiting for transfers between devices  61.9 us (30%)
  Pallas kernels  24.7 us (12%)
  blocking collectives  24.3 us (12%)
  local copies, waits for them, and re-layouts  10.9 us (5%)
  other arithmetic  6.81 us (3%)
    ppermute x3, waiting for transfers between devices, shards(): other = lax.ppermute(blocks, 'z', [(i, i ^ far) for i in range(nz)])  44 us
    all_to_all x1, blocking collectives, swap(): return lax.all_to_all(pieces, axis, 0, 0, tiled=True)  24.3 us
    all_to_all x2, starting transfers between devices, swap(): return lax.all_to_all(pieces, axis, 0, 0, tiled=True)  24.1 us
    ppermute x3, starting transfers between devices, shards(): other = lax.ppermute(blocks, 'z', [(i, i ^ far) for i in range(nz)])  15.9 us
    pallas_call x1, Pallas kernels, prefill(): pl.pallas_call(prefill_kernel, out_shape=result, grid_spec=pltpu.Prefetch...  11 us
    ppermute x3, starting transfers between devices, shards(): lax.ppermute(blocks, 'x', [(i, (i + k) % nx) for i in range(nx)])  9.37 us
    ppermute x1, starting transfers between devices, shards(): other = lax.ppermute(parts, 'z', [(i, i ^ 4) for i in range(nz)])  8.8 us
    ppermute x3, waiting for transfers between devices, shards(): lax.ppermute(blocks, 'x', [(i, (i + k) % nx) for i in range(nx)])  7.85 us
  transfers between devices with their start and end apart: 15, of which 11 were waited for; matrix products, arithmetic and copies ran while one was open for 2% of the time, Pallas kernels for 6%

profile of v2, /device:TPU:73, one launch (start us, length us, event | category | flops | bytes accessed | tf_op | source)
XLA Modules:
  0.0 205.7 jit_solution(3946277491451636549)
XLA Ops:
  0.6 1.4 copy.15
  2.0 1.2 broadcast_subtract_fusion.limits_ref
  3.2 0.6 pad_add_fusion.place_ref
  3.8 2.5 %shard_map.123.mine_ref = f32[2,4,32,128]{3,2,1,0:T(8,128)} custom-call(s32[4]{0:T(128)} %pad_add_fusion.place_ref, s32[2]{0:T(128)} %broadcast_subtract_fusion.limits_ref, bf16[2,64,128]{2,1,0:T(8,128)(2,1)} %bitcast.32, bf16[2,2,128,1024]{3,2,1,0:T(8,128)(2,1)} %cache_ref.1), custom_call_target="tpu_custom_call" | custom-call | flops 1000000000 | bytes 1048576 | tf_op jit(solution)/shard_map/pallas_call | solution.py:261
  6.3 0.8 slice_bitcast_fusion
  7.2 2.6 %collective-permute-start.7 = (f32[4,32,128]{2,1,0:T(8,128)S(1)}, f32[4,32,128]{2,1,0:T(8,128)S(1)}, u32[]{:S(2)}, u32[]{:S(2)}) collective-permute-start(f32[4,32,128]{2,1,0:T(8,128)S(1)} %slice_bitcast_fusion), channel_id=1, source_target_pairs={{0,16},{16,0},{1,17},{17,1},{2,18},{18,2},{3,19},{19,3},{4,20},{20... | collective-permute-start | bytes 196616 | tf_op jit(solution)/shard_map/ppermute | solution.py:264
  9.7 0.9 collective-permute-done.7.other_ref
  10.6 0.6 copy-done.3
  11.2 1.7 shard_map.124.mine_ref
  12.9 0.8 slice_bitcast_fusion.1
  13.7 3.1 %collective-permute-start.8 = (f32[2,32,128]{2,1,0:T(8,128)S(1)}, f32[2,32,128]{2,1,0:T(8,128)S(1)}, u32[]{:S(2)}, u32[]{:S(2)}) collective-permute-start(f32[2,32,128]{2,1,0:T(8,128)S(1)} %slice_bitcast_fusion.1), channel_id=1, source_target_pairs={{0,32},{32,0},{64,96},{96,64},{1,33},{33,1},{65,97},{97,65},{2,34}... | collective-permute-start | bytes 98312 | tf_op jit(solution)/shard_map/ppermute | solution.py:268
  16.8 1.5 collective-permute-done.8.other_ref
  18.3 0.6 copy-done.4
  19.0 1.6 shard_map.125.mine_ref
  20.6 0.7 slice_bitcast_fusion.2
  21.3 4.6 %collective-permute-start.9 = (f32[32,128]{1,0:T(8,128)S(1)}, f32[32,128]{1,0:T(8,128)S(1)}, u32[]{:S(2)}, u32[]{:S(2)}) collective-permute-start(f32[32,128]{1,0:T(8,128)S(1)} %slice_bitcast_fusion.2), channel_id=1, source_target_pairs={{0,64},{32,96},{64,0},{96,32},{1,65},{33,97},{65,1},{97,33},{2,66}... | collective-permute-start | bytes 49160 | tf_op jit(solution)/shard_map/ppermute | solution.py:272
  25.9 1.3 collective-permute-done.9.other_ref
  27.3 0.6 copy-done.7
  27.9 1.5 shard_map.126.mine_ref
  29.4 3.5 %collective-permute-start.10 = (f32[32,128]{1,0:T(8,128)}, f32[32,128]{1,0:T(8,128)S(1)}, u32[]{:S(2)}, u32[]{:S(2)}) collective-permute-start(f32[32,128]{1,0:T(8,128)} %shard_map.126.mine_ref), channel_id=1, source_target_pairs={{0,128},{128,0},{256,384},{384,256},{512,640},{640,512},{768,896},... | collective-permute-start | bytes 49160 | tf_op jit(solution)/shard_map/ppermute | solution.py:274
  32.9 1.3 collective-permute-done.10.other_ref
  34.2 0.6 copy-done.5
  34.8 1.5 shard_map.127.mine_ref
  36.3 1.9 collective-permute-start.11
  38.2 3.7 %collective-permute-done.11.other_ref = f32[32,128]{1,0:T(8,128)S(1)} collective-permute-done((f32[32,128]{1,0:T(8,128)}, f32[32,128]{1,0:T(8,128)S(1)}, u32[]{:S(2)}, u32[]{:S(2)}) %collective-permute-start.11) | collective-permute-done | bytes 16416 | tf_op jit(solution)/shard_map/ppermute | solution.py:276
  41.9 0.6 copy-done.6
  42.5 1.5 shard_map.128.mine_ref
  44.0 8.8 %collective-permute-start.12 = (f32[32,128]{1,0:T(8,128)}, f32[32,128]{1,0:T(8,128)S(1)}, u32[]{:S(2)}, u32[]{:S(2)}) collective-permute-start(f32[32,128]{1,0:T(8,128)} %shard_map.128.mine_ref), channel_id=1, source_target_pairs={{0,512},{128,640},{256,768},{384,896},{512,0},{640,128},{768,256},... | collective-permute-start | bytes 49160 | tf_op jit(solution)/shard_map/ppermute | solution.py:278
  52.8 1.3 collective-permute-done.12.other_ref
  54.1 0.6 copy-done.8
  54.7 1.5 shard_map.129
  56.3 24.3 %all_to_all.15 = f32[32,4,128]{2,1,0:T(4,128)} all-to-all(f32[32,4,128]{2,1,0:T(4,128)} %bitcast.27), channel_id=1, replica_groups=mesh['z'=8,'x'=4,'c'=2,'y'=4,'w'=4] {'x','c','y'}, dimensions={0} | all-to-all | bytes 131072 | tf_op jit(solution)/shard_map/all_to_all | solution.py:23
  80.5 1.8 broadcast_in_dim.5
  82.3 19.8 %all-to-all-start.1 = ((bf16[4,512,128]{2,1,0:T(8,128)(2,1)}), bf16[4,512,128]{2,1,0:T(8,128)(2,1)S(1)}, u32[]{:S(2)}, u32[]{:S(2)}) async-start(bf16[4,512,128]{2,1,0:T(8,128)(2,1)} %broadcast_in_dim.5), calls=%async_computation.1 | async-start | bytes 1048576 | tf_op jit(solution)/shard_map/all_to_all | solution.py:23
  102.1 4.0 %collective-permute-start = (bf16[1,128,128]{2,1,0:T(8,128)(2,1)}, bf16[1,128,128]{2,1,0:T(8,128)(2,1)S(1)}, u32[]{:S(2)}, u32[]{:S(2)}) collective-permute-start(bf16[1,128,128]{2,1,0:T(8,128)(2,1)} %bitcast.22), channel_id=1, source_target_pairs={{0,512},{128,640},{256,768},{384,896},{512,0},{640,128},{768,256},... | collective-permute-start | bytes 98312 | tf_op jit(solution)/shard_map/ppermute | solution.py:239
  106.1 27.6 %collective-permute-done = bf16[1,128,128]{2,1,0:T(8,128)(2,1)S(1)} collective-permute-done((bf16[1,128,128]{2,1,0:T(8,128)(2,1)}, bf16[1,128,128]{2,1,0:T(8,128)(2,1)S(1)}, u32[]{:S(2)}, u32[]{:S(2)}) %collective-permute-start) | collective-permute-done | bytes 32800 | tf_op jit(solution)/shard_map/ppermute | solution.py:239
  133.7 0.8 pad_maximum_fusion.3
  134.4 5.8 %collective-permute-start.1 = (bf16[2,128,128]{2,1,0:T(8,128)(2,1)S(1)}, bf16[2,128,128]{2,1,0:T(8,128)(2,1)S(1)}, u32[]{:S(2)}, u32[]{:S(2)}) collective-permute-start(bf16[2,128,128]{2,1,0:T(8,128)(2,1)S(1)} %pad_maximum_fusion.3), channel_id=1, source_target_pairs={{0,256},{128,384},{256,0},{384,128},{512,768},{640,896},{768,512},... | collective-permute-start | bytes 196616 | tf_op jit(solution)/shard_map/ppermute | solution.py:239
  140.2 12.6 %collective-permute-done.1 = bf16[2,128,128]{2,1,0:T(8,128)(2,1)S(1)} collective-permute-done((bf16[2,128,128]{2,1,0:T(8,128)(2,1)S(1)}, bf16[2,128,128]{2,1,0:T(8,128)(2,1)S(1)}, u32[]{:S(2)}, u32[]{:S(2)}) %collective-permute-start.1) | collective-permute-done | bytes 65568 | tf_op jit(solution)/shard_map/ppermute | solution.py:239
  152.9 0.8 pad_maximum_fusion.2
  153.6 6.1 %collective-permute-start.2 = (bf16[4,128,128]{2,1,0:T(8,128)(2,1)S(1)}, bf16[4,128,128]{2,1,0:T(8,128)(2,1)S(1)}, u32[]{:S(2)}, u32[]{:S(2)}) collective-permute-start(bf16[4,128,128]{2,1,0:T(8,128)(2,1)S(1)} %pad_maximum_fusion.2), channel_id=1, source_target_pairs={{0,128},{128,0},{256,384},{384,256},{512,640},{640,512},{768,896},... | collective-permute-start | bytes 393224 | tf_op jit(solution)/shard_map/ppermute | solution.py:239
  159.7 3.8 %collective-permute-done.2 = bf16[4,128,128]{2,1,0:T(8,128)(2,1)S(1)} collective-permute-done((bf16[4,128,128]{2,1,0:T(8,128)(2,1)S(1)}, bf16[4,128,128]{2,1,0:T(8,128)(2,1)S(1)}, u32[]{:S(2)}, u32[]{:S(2)}) %collective-permute-start.2) | collective-permute-done | bytes 131104 | tf_op jit(solution)/shard_map/ppermute | solution.py:239
  163.5 0.8 fusion
  164.3 2.9 %collective-permute-start.4 = (bf16[8,128,128]{2,1,0:T(8,128)(2,1)S(1)}, bf16[8,128,128]{2,1,0:T(8,128)(2,1)S(1)}, u32[]{:S(2)}, u32[]{:S(2)}) collective-permute-start(bf16[8,128,128]{2,1,0:T(8,128)(2,1)S(1)} %get-tuple-element.3), channel_id=1, source_target_pairs={{0,64},{32,96},{64,0},{96,32},{1,65},{33,97},{65,1},{97,33},{2,66}... | collective-permute-start | bytes 786440 | tf_op jit(solution)/shard_map/ppermute | solution.py:243
  167.2 2.4 %collective-permute-start.3 = (bf16[8,128,128]{2,1,0:T(8,128)(2,1)S(1)}, bf16[8,128,128]{2,1,0:T(8,128)(2,1)S(1)}, u32[]{:S(2)}, u32[]{:S(2)}) collective-permute-start(bf16[8,128,128]{2,1,0:T(8,128)(2,1)S(1)} %get-tuple-element.3), channel_id=1, source_target_pairs={{0,32},{32,64},{64,96},{96,0},{1,33},{33,65},{65,97},{97,1},{2,34}... | collective-permute-start | bytes 786440 | tf_op jit(solution)/shard_map/ppermute | solution.py:243
  169.6 4.1 %collective-permute-start.5 = (bf16[8,128,128]{2,1,0:T(8,128)(2,1)S(1)}, bf16[8,128,128]{2,1,0:T(8,128)(2,1)S(1)}, u32[]{:S(2)}, u32[]{:S(2)}) collective-permute-start(bf16[8,128,128]{2,1,0:T(8,128)(2,1)S(1)} %get-tuple-element.3), channel_id=1, source_target_pairs={{0,96},{32,0},{64,32},{96,64},{1,97},{33,1},{65,33},{97,65},{2,98}... | collective-permute-start | bytes 786440 | tf_op jit(solution)/shard_map/ppermute | solution.py:243
  173.7 0.9 collective-permute-done.4
  174.6 7.0 %collective-permute-done.3 = bf16[8,128,128]{2,1,0:T(8,128)(2,1)S(1)} collective-permute-done((bf16[8,128,128]{2,1,0:T(8,128)(2,1)S(1)}, bf16[8,128,128]{2,1,0:T(8,128)(2,1)S(1)}, u32[]{:S(2)}, u32[]{:S(2)}) %collective-permute-start.3) | collective-permute-done | bytes 262176 | tf_op jit(solution)/shard_map/ppermute | solution.py:243
  181.5 0.0 collective-permute-done.5
  181.5 0.1 pad_maximum_fusion.refs_4_
  181.7 0.0 copy-start
  181.7 2.4 %collective-permute-start.6 = (bf16[4,8,128,128]{3,2,1,0:T(8,128)(2,1)S(1)}, bf16[4,8,128,128]{3,2,1,0:T(8,128)(2,1)S(1)}, u32[]{:S(2)}, u32[]{:S(2)}) collective-permute-start(bf16[4,8,128,128]{3,2,1,0:T(8,128)(2,1)S(1)} %pad_maximum_fusion.refs_4_), channel_id=1, source_target_pairs={{0,16},{16,0},{1,17},{17,1},{2,18},{18,2},{3,19},{19,3},{4,20},{20... | collective-permute-start | bytes 3145736 | tf_op jit(solution)/shard_map/ppermute | solution.py:245
  184.1 0.7 convert_element_type.6
  184.8 0.8 multiply_cosine_fusion
  185.5 0.6 pad_maximum_fusion.4.refs_7_
  186.1 0.0 all-to-all-done.1.weight_ref
  186.1 0.8 copy-done.1
  186.9 1.9 shard_map.130
  188.8 4.3 %all-to-all-start.2 = ((f32[4,2,128]{2,1,0:T(2,128)}), f32[4,2,128]{2,1,0:T(2,128)S(1)}, u32[]{:S(2)}, u32[]{:S(2)}) async-start(f32[4,2,128]{2,1,0:T(2,128)} %shard_map.130), calls=%async_computation.2 | async-start | bytes 8192 | tf_op jit(solution)/shard_map/all_to_all | solution.py:23
  193.1 0.0 collective-permute-done.6.refs_5_
  193.1 1.0 copy-done.2
  194.1 11.0 %shard_map.122 = bf16[768,128]{1,0:T(8,128)(2,1)} custom-call(s32[4]{0:T(128)} %pad_add_fusion.place_ref, bf16[768,8192]{1,0:T(8,128)(2,1)} %refs_3_.1, bf16[768,8192]{1,0:T(8,128)(2,1)} %refs_3_.1, bf16[768,8192]{1,0:T(8,128)(2,1)} %refs_3_.1, bf16[768,8192]{1,0:T(8,128)(2,1)} %refs_3_.1, bf16[4,8,128,128]{3,2,1,0:T(8,128)(2,1)} %copy-done, ...), custom_call_target="tpu_custom_call" | custom-call | flops 2000000000 | bytes 12582912 | tf_op jit(solution)/shard_map/pallas_call | solution.py:192
  205.1 0.0 all-to-all-done.2
  205.1 0.5 reduce_sum.9
  (9 shorter events, 0.0 us)
Async XLA Ops:
  7.2 3.5 %collective-permute-start.7 = (f32[4,32,128]{2,1,0:T(8,128)S(1)}, f32[4,32,128]{2,1,0:T(8,128)S(1)}, u32[]{:S(2)}, u32[]{:S(2)}) collective-permute-start(f32[4,32,128]{2,1,0:T(8,128)S(1)} %slice_bitcast_fusion), channel_id=1, source_target_pairs={{0,16},{16,0},{1,17},{17,1},{2,18},{18,2},{3,19},{19,3},{4,20},{20... | collective-permute-start | bytes 196616 | tf_op jit(solution)/shard_map/ppermute | solution.py:264
  10.6 0.6 copy-start.3
  13.7 4.6 %collective-permute-start.8 = (f32[2,32,128]{2,1,0:T(8,128)S(1)}, f32[2,32,128]{2,1,0:T(8,128)S(1)}, u32[]{:S(2)}, u32[]{:S(2)}) collective-permute-start(f32[2,32,128]{2,1,0:T(8,128)S(1)} %slice_bitcast_fusion.1), channel_id=1, source_target_pairs={{0,32},{32,0},{64,96},{96,64},{1,33},{33,1},{65,97},{97,65},{2,34}... | collective-permute-start | bytes 98312 | tf_op jit(solution)/shard_map/ppermute | solution.py:268
  18.3 0.6 copy-start.4
  21.3 6.0 %collective-permute-start.9 = (f32[32,128]{1,0:T(8,128)S(1)}, f32[32,128]{1,0:T(8,128)S(1)}, u32[]{:S(2)}, u32[]{:S(2)}) collective-permute-start(f32[32,128]{1,0:T(8,128)S(1)} %slice_bitcast_fusion.2), channel_id=1, source_target_pairs={{0,64},{32,96},{64,0},{96,32},{1,65},{33,97},{65,1},{97,33},{2,66}... | collective-permute-start | bytes 49160 | tf_op jit(solution)/shard_map/ppermute | solution.py:272
  27.3 0.6 copy-start.7
  29.4 4.9 %collective-permute-start.10 = (f32[32,128]{1,0:T(8,128)}, f32[32,128]{1,0:T(8,128)S(1)}, u32[]{:S(2)}, u32[]{:S(2)}) collective-permute-start(f32[32,128]{1,0:T(8,128)} %shard_map.126.mine_ref), channel_id=1, source_target_pairs={{0,128},{128,0},{256,384},{384,256},{512,640},{640,512},{768,896},... | collective-permute-start | bytes 49160 | tf_op jit(solution)/shard_map/ppermute | solution.py:274
  34.2 0.6 copy-start.5
  36.3 5.6 %collective-permute-start.11 = (f32[32,128]{1,0:T(8,128)}, f32[32,128]{1,0:T(8,128)S(1)}, u32[]{:S(2)}, u32[]{:S(2)}) collective-permute-start(f32[32,128]{1,0:T(8,128)} %shard_map.127.mine_ref), channel_id=1, source_target_pairs={{0,256},{128,384},{256,0},{384,128},{512,768},{640,896},{768,512},... | collective-permute-start | bytes 49160 | tf_op jit(solution)/shard_map/ppermute | solution.py:276
  41.9 0.6 copy-start.6
  44.0 10.1 %collective-permute-start.12 = (f32[32,128]{1,0:T(8,128)}, f32[32,128]{1,0:T(8,128)S(1)}, u32[]{:S(2)}, u32[]{:S(2)}) collective-permute-start(f32[32,128]{1,0:T(8,128)} %shard_map.128.mine_ref), channel_id=1, source_target_pairs={{0,512},{128,640},{256,768},{384,896},{512,0},{640,128},{768,256},... | collective-permute-start | bytes 49160 | tf_op jit(solution)/shard_map/ppermute | solution.py:278
  54.1 0.6 copy-start.8
  82.3 103.8 %all-to-all-start.1 = ((bf16[4,512,128]{2,1,0:T(8,128)(2,1)}), bf16[4,512,128]{2,1,0:T(8,128)(2,1)S(1)}, u32[]{:S(2)}, u32[]{:S(2)}) async-start(bf16[4,512,128]{2,1,0:T(8,128)(2,1)} %broadcast_in_dim.5), calls=%async_computation.1 | async-start | bytes 1048576 | tf_op jit(solution)/shard_map/all_to_all | solution.py:23
  102.1 31.6 %collective-permute-start = (bf16[1,128,128]{2,1,0:T(8,128)(2,1)}, bf16[1,128,128]{2,1,0:T(8,128)(2,1)S(1)}, u32[]{:S(2)}, u32[]{:S(2)}) collective-permute-start(bf16[1,128,128]{2,1,0:T(8,128)(2,1)} %bitcast.22), channel_id=1, source_target_pairs={{0,512},{128,640},{256,768},{384,896},{512,0},{640,128},{768,256},... | collective-permute-start | bytes 98312 | tf_op jit(solution)/shard_map/ppermute | solution.py:239
  134.4 18.4 %collective-permute-start.1 = (bf16[2,128,128]{2,1,0:T(8,128)(2,1)S(1)}, bf16[2,128,128]{2,1,0:T(8,128)(2,1)S(1)}, u32[]{:S(2)}, u32[]{:S(2)}) collective-permute-start(bf16[2,128,128]{2,1,0:T(8,128)(2,1)S(1)} %pad_maximum_fusion.3), channel_id=1, source_target_pairs={{0,256},{128,384},{256,0},{384,128},{512,768},{640,896},{768,512},... | collective-permute-start | bytes 196616 | tf_op jit(solution)/shard_map/ppermute | solution.py:239
  153.6 9.9 %collective-permute-start.2 = (bf16[4,128,128]{2,1,0:T(8,128)(2,1)S(1)}, bf16[4,128,128]{2,1,0:T(8,128)(2,1)S(1)}, u32[]{:S(2)}, u32[]{:S(2)}) collective-permute-start(bf16[4,128,128]{2,1,0:T(8,128)(2,1)S(1)} %pad_maximum_fusion.2), channel_id=1, source_target_pairs={{0,128},{128,0},{256,384},{384,256},{512,640},{640,512},{768,896},... | collective-permute-start | bytes 393224 | tf_op jit(solution)/shard_map/ppermute | solution.py:239
  164.3 10.3 %collective-permute-start.4 = (bf16[8,128,128]{2,1,0:T(8,128)(2,1)S(1)}, bf16[8,128,128]{2,1,0:T(8,128)(2,1)S(1)}, u32[]{:S(2)}, u32[]{:S(2)}) collective-permute-start(bf16[8,128,128]{2,1,0:T(8,128)(2,1)S(1)} %get-tuple-element.3), channel_id=1, source_target_pairs={{0,64},{32,96},{64,0},{96,32},{1,65},{33,97},{65,1},{97,33},{2,66}... | collective-permute-start | bytes 786440 | tf_op jit(solution)/shard_map/ppermute | solution.py:243
  167.2 14.4 %collective-permute-start.3 = (bf16[8,128,128]{2,1,0:T(8,128)(2,1)S(1)}, bf16[8,128,128]{2,1,0:T(8,128)(2,1)S(1)}, u32[]{:S(2)}, u32[]{:S(2)}) collective-permute-start(bf16[8,128,128]{2,1,0:T(8,128)(2,1)S(1)} %get-tuple-element.3), channel_id=1, source_target_pairs={{0,32},{32,64},{64,96},{96,0},{1,33},{33,65},{65,97},{97,1},{2,34}... | collective-permute-start | bytes 786440 | tf_op jit(solution)/shard_map/ppermute | solution.py:243
  169.6 12.0 %collective-permute-start.5 = (bf16[8,128,128]{2,1,0:T(8,128)(2,1)S(1)}, bf16[8,128,128]{2,1,0:T(8,128)(2,1)S(1)}, u32[]{:S(2)}, u32[]{:S(2)}) collective-permute-start(bf16[8,128,128]{2,1,0:T(8,128)(2,1)S(1)} %get-tuple-element.3), channel_id=1, source_target_pairs={{0,96},{32,0},{64,32},{96,64},{1,97},{33,1},{65,33},{97,65},{2,98}... | collective-permute-start | bytes 786440 | tf_op jit(solution)/shard_map/ppermute | solution.py:243
  181.7 11.4 %copy-start = (bf16[4,8,128,128]{3,2,1,0:T(8,128)(2,1)}, bf16[4,8,128,128]{3,2,1,0:T(8,128)(2,1)S(1)}, u32[]{:S(2)}) copy-start(bf16[4,8,128,128]{3,2,1,0:T(8,128)(2,1)S(1)} %pad_maximum_fusion.refs_4_) | copy-start | bytes 3145732
  181.7 11.4 %collective-permute-start.6 = (bf16[4,8,128,128]{3,2,1,0:T(8,128)(2,1)S(1)}, bf16[4,8,128,128]{3,2,1,0:T(8,128)(2,1)S(1)}, u32[]{:S(2)}, u32[]{:S(2)}) collective-permute-start(bf16[4,8,128,128]{3,2,1,0:T(8,128)(2,1)S(1)} %pad_maximum_fusion.refs_4_), channel_id=1, source_target_pairs={{0,16},{16,0},{1,17},{17,1},{2,18},{18,2},{3,19},{19,3},{4,20},{20... | collective-permute-start | bytes 3145736 | tf_op jit(solution)/shard_map/ppermute | solution.py:245
  186.1 0.8 copy-start.1
  188.8 16.4 %all-to-all-start.2 = ((f32[4,2,128]{2,1,0:T(2,128)}), f32[4,2,128]{2,1,0:T(2,128)S(1)}, u32[]{:S(2)}, u32[]{:S(2)}) async-start(f32[4,2,128]{2,1,0:T(2,128)} %shard_map.130), calls=%async_computation.2 | async-start | bytes 8192 | tf_op jit(solution)/shard_map/all_to_all | solution.py:23
  193.1 1.0 copy-start.2

commit v3 on v2

v3 whole, which is shorter than its diff:
```python
import jax
import jax.numpy as jnp
import numpy as np
from jax import lax
from jax.experimental import pallas as pl
from jax.experimental.pallas import tpu as pltpu
from jax.sharding import Mesh
from jax.sharding import PartitionSpec as P

QUERY_HEADS = 64
KEY_VALUE_HEADS = 8
HEAD_SIZE = 128
SLOT = 128
GX = ("z", "x", "c")
GY = ("y", "w")
GROUP = QUERY_HEADS // KEY_VALUE_HEADS

rope_base = 500000.0
masked_score = -1e30


def swap(pieces, axis):
    return lax.all_to_all(pieces, axis, 0, 0, tiled=True)


def turns():
    half_width = HEAD_SIZE // 2
    inverse = rope_base ** (-2.0 * (np.arange(HEAD_SIZE) % half_width) / HEAD_SIZE)
    angles = np.arange(SLOT)[:, None] * inverse[None, :]
    return tuple(np.float32(table) for table in (inverse, np.cos(angles), np.sin(angles)))


def block_kernel(place_ref, lengths_ref, query_ref, cache_ref, out_ref):
    trajectories, positions = cache_ref.shape[1], cache_ref.shape[2]
    start = place_ref[4] * positions
    pairs = [(t, g) for t in range(trajectories) for g in range(KEY_VALUE_HEADS)]
    columns = [slice(g * HEAD_SIZE, (g + 1) * HEAD_SIZE) for g in range(KEY_VALUE_HEADS)]
    scores = jnp.concatenate(
        [
            lax.dot_general(
                query_ref[t, g * GROUP : (g + 1) * GROUP, :],
                cache_ref[0, t, :, columns[g]],
                (((1,), (1,)), ((), ())),
                preferred_element_type=jnp.float32,
            )
            for t, g in pairs
        ],
        axis=0,
    ) * HEAD_SIZE ** (-0.5)
    position = start + lax.broadcasted_iota(jnp.int32, (QUERY_HEADS, positions), 1)
    valid = jnp.concatenate([position < lengths_ref[t] for t in range(trajectories)], axis=0)
    peak = jnp.max(jnp.where(valid, scores, masked_score), axis=1, keepdims=True)
    weights = jnp.where(valid, jnp.exp(scores - peak), 0.0)
    total = jnp.sum(weights, axis=1, keepdims=True)
    lane = lax.broadcasted_iota(jnp.int32, weights.shape, 1)
    stats = jnp.where(lane < HEAD_SIZE // 2, peak, total)
    for k, (t, g) in enumerate(pairs):
        rows = slice(k * GROUP, (k + 1) * GROUP)
        values = jnp.dot(
            weights[rows].astype(jnp.bfloat16),
            cache_ref[1, t, :, columns[g]],
            preferred_element_type=jnp.float32,
        )
        for i in range(4):
            owner, row, pair = (t * 4 + i) * 4 + g // 2, (g % 2) * 2, slice(i * 2, i * 2 + 2)
            out_ref[owner, row : row + 2, :] = values[pair]
            out_ref[owner, row + 4 : row + 6, :] = stats[rows][pair]


def merge_kernel(parts_ref, out_ref):
    ny = parts_ref.shape[1]
    lane = lax.broadcasted_iota(jnp.int32, (4, HEAD_SIZE), 1)
    merged = []
    for y in range(ny):
        numerator, stats = parts_ref[:, y, :4, :], parts_ref[:, y, 4:, :]
        peak, total = stats[:, :, :1], stats[:, :, HEAD_SIZE // 2 : HEAD_SIZE // 2 + 1]
        top = jnp.max(peak, axis=0)
        factor = jnp.exp(peak - top[None])
        total = jnp.sum(total * factor, axis=0)
        some = total > 0.0
        safe = jnp.where(some, total, 1.0)
        attention = jnp.sum(numerator * factor, axis=0) / safe
        weight = jnp.where(some, top + jnp.log(safe), masked_score)
        high = weight.astype(jnp.bfloat16).astype(jnp.float32)
        middle = (weight - high).astype(jnp.bfloat16).astype(jnp.float32)
        low = weight - high - middle
        weight = jnp.where(lane < 32, high, jnp.where(lane < 64, middle, low))
        merged.append((attention, weight))
    for w in range(4):
        rows = [part[w : w + 1] for kind in range(2) for part in (pair[kind] for pair in merged)]
        piece = jnp.concatenate(rows, axis=0).astype(jnp.bfloat16)
        for z in range(out_ref.shape[0]):
            out_ref[z, w] = piece


def finish_kernel(parts_ref, out_ref):
    for w in range(parts_ref.shape[1]):
        parts = parts_ref[:, w].astype(jnp.float32)
        attention, stats = parts[:, :4, :], parts[:, 4:, :]
        weight = stats[:, :, :1] + stats[:, :, 32:33] + stats[:, :, 64:65]
        factor = jnp.exp(weight - jnp.max(weight, axis=0)[None])
        rows = jnp.sum(attention * factor, axis=0) / jnp.sum(factor, axis=0)
        rows = rows.astype(jnp.bfloat16).astype(jnp.float32)
        for k in range(out_ref.shape[0]):
            out_ref[k, pl.ds(w, 4, stride=4), :] = rows


def out_kernel(heads_ref, weight_ref, out_ref):
    trajectories = out_ref.shape[1]
    for t in range(trajectories):
        total = jnp.zeros((heads_ref.shape[1], HEAD_SIZE), jnp.float32)
        for i in range(4):
            total += jnp.dot(
                heads_ref[t * 4 + i].astype(jnp.bfloat16),
                weight_ref[i * HEAD_SIZE : (i + 1) * HEAD_SIZE, :],
                preferred_element_type=jnp.float32,
            )
        out_ref[:, t, :] = total


def prefill_kernel(place_ref, *refs):
    tokens, refs = refs[:4], refs[4:]
    own_ref, other_ref, live_ref, starts_ref, cosine_ref, sine_ref, out_ref, total_ref = refs
    step = pl.program_id(0)

    @pl.when(step == 0)
    def _():
        total_ref[...] = jnp.zeros_like(total_ref)

    first = place_ref[2] == 0
    total = total_ref[...]
    for k, token_ref in enumerate(tokens):
        own, other = own_ref[k, 0], other_ref[k, 0]
        rows = jnp.concatenate(
            [jnp.where(first, own, other), jnp.where(first, other, own)], axis=0
        )
        total += jnp.dot(token_ref[...], rows, preferred_element_type=jnp.float32)
    total_ref[...] = total

    @pl.when(step == pl.num_programs(0) - 1)
    def _():
        prefixes = starts_ref.shape[0] // 2
        slot = lax.broadcasted_iota(jnp.int32, (SLOT, HEAD_SIZE), 0)
        front = lax.broadcasted_iota(jnp.int32, (SLOT, HEAD_SIZE), 1) < HEAD_SIZE // 2
        for i in range(prefixes):
            rows = slice(i * SLOT, (i + 1) * SLOT)
            plain = total_ref[rows, :]
            along, across = starts_ref[i : i + 1, :], starts_ref[prefixes + i : prefixes + i + 1, :]
            cosine = cosine_ref[...] * along - sine_ref[...] * across
            sine = sine_ref[...] * along + cosine_ref[...] * across
            swapped = pltpu.roll(plain, HEAD_SIZE // 2, 1)
            turned = plain * cosine + swapped * jnp.where(front, -sine, sine)
            kept = jnp.where(place_ref[3] > 0, turned, plain)
            out_ref[rows, :] = jnp.where(slot < live_ref[i], kept, 0.0).astype(jnp.bfloat16)


def prefill(place, tokens, own, other, live, starts, cosine, sine):
    rows, columns = tokens.shape[0], own.shape[-1]
    nx, nz = own.shape[:2]

    def token_block(k):
        def index(step, place):
            flipped = (step & 1) * 4 + (step & 2) + (step >> 2)
            return 0, (place[0] ^ flipped) * nx + ((place[1] + nx - k) & (nx - 1))

        return index

    def whole(array):
        return pl.BlockSpec(array.shape, lambda step, place: (0, 0))

    piece = pl.BlockSpec((nx, 1, *own.shape[2:]), lambda step, place: (0, step, 0, 0))
    result = jax.ShapeDtypeStruct((rows, columns), jnp.bfloat16)
    return pl.pallas_call(
        prefill_kernel,
        out_shape=result,
        grid_spec=pltpu.PrefetchScalarGridSpec(
            num_scalar_prefetch=1,
            grid=(nz,),
            in_specs=[pl.BlockSpec((rows, 2 * HEAD_SIZE), token_block(k)) for k in range(nx)]
            + [piece, piece, SMEM, whole(starts), whole(cosine), whole(sine)],
            out_specs=whole(result),
            scratch_shapes=[pltpu.VMEM((rows, columns), jnp.float32)],
        ),
        cost_estimate=pl.CostEstimate(
            flops=2 * 10**9, bytes_accessed=2 * tokens.size, transcendentals=0
        ),
    )(place, *([tokens] * nx), own, other, live, starts, cosine, sine)


VMEM = pl.BlockSpec(memory_space=pltpu.VMEM)
SMEM = pl.BlockSpec(memory_space=pltpu.SMEM)


def whole_call(kernel, shape, in_specs=(VMEM,), flops=10**7, dtype=jnp.float32):
    return pl.pallas_call(
        kernel,
        out_shape=jax.ShapeDtypeStruct(shape, dtype),
        in_specs=list(in_specs),
        out_specs=VMEM,
        cost_estimate=pl.CostEstimate(flops=flops, bytes_accessed=2**20, transcendentals=0),
    )


def shards(
    prefix_tokens,
    key_value_weight,
    prefix_lengths,
    start_offsets,
    queries,
    key_value_cache,
    cache_lengths,
    out_weight,
):
    columns = key_value_weight.shape[1]
    nz, nx, nc, ny, nw = (lax.axis_size(a) for a in ("z", "x", "c", "y", "w"))
    nxc, ngy = nx * nc, ny * nw

    blocks = key_value_weight[None]
    for far in (4, 2, 1):
        other = lax.ppermute(blocks, "z", [(i, i ^ far) for i in range(nz)])
        blocks = jnp.concatenate([blocks, other], axis=0)
    sides = [blocks]
    for k in range(1, nx):
        sides.append(lax.ppermute(blocks, "x", [(i, (i + k) % nx) for i in range(nx)]))
    own = jnp.stack(sides)
    other = lax.ppermute(own, "c", [(0, 1), (1, 0)])
    column = lax.axis_index(GY)
    place = jnp.stack(
        [*(lax.axis_index(a) for a in GX), KEY_VALUE_HEADS - column, lax.axis_index(GX)]
    )
    inverse, cosine, sine = turns()
    angles = start_offsets.astype(jnp.float32)[:, None] * inverse[None, :]
    starts = jnp.concatenate([jnp.cos(angles), jnp.sin(angles)], axis=0)
    prefix_kv = prefill(
        place, prefix_tokens, own, other, prefix_lengths, starts, cosine, sine
    )

    trajectories = queries.shape[0]
    ordered = queries.reshape(trajectories, KEY_VALUE_HEADS, 2, 4, HEAD_SIZE)
    ordered = ordered.swapaxes(2, 3).reshape(trajectories, QUERY_HEADS, HEAD_SIZE)
    parts = whole_call(
        block_kernel, (nxc * ny, 8, HEAD_SIZE), (SMEM, SMEM, VMEM, VMEM), flops=10**9
    )(place, cache_lengths, ordered, key_value_cache)
    parts = swap(parts, ("x", "c", "y"))
    parts = whole_call(merge_kernel, (nz, nw, 8, HEAD_SIZE), dtype=jnp.bfloat16)(
        parts.reshape(nxc, ny, 8, HEAD_SIZE)
    )
    parts = swap(parts.reshape(nz * nw, 8, HEAD_SIZE), ("z", "w"))
    attention = whole_call(finish_kernel, (nxc, ngy, HEAD_SIZE))(
        parts.reshape(nz, nw, 8, HEAD_SIZE)
    )
    heads = swap(attention, ("x", "c"))
    mixed = whole_call(out_kernel, (ngy, trajectories, columns), (VMEM, VMEM))(heads, out_weight)
    mixed = swap(mixed, GY)
    return (prefix_kv, jnp.sum(mixed, axis=0).astype(jnp.bfloat16))


def solution(mesh):
    finer = Mesh(mesh.devices.reshape(8, 4, 2, 4, 4), ("z", "x", "c", "y", "w"))
    return jax.shard_map(
        shards,
        mesh=finer,
        in_specs=(
            P(GX, None),
            P(GX, GY),
            P(GX),
            P(GX),
            P(GY, None),
            P(None, GY, GX, None),
            P(GY),
            P(GY, GX),
        ),
        out_specs=(P(GX, GY), P(GY, GX)),
        check_vma=False,
    )
```

time: 207 us -> 174 us (0.84)
  the two profiles are of different devices: /device:TPU:73 before, /device:TPU:32 now
where the time goes in v3:
time: 174 us; the launch traced here: 173 us
  blocking collectives  59.5 us (34%)
  starting transfers between devices  46 us (26%)
  waiting for transfers between devices  39.2 us (23%)
  Pallas kernels  18.9 us (11%)
  other arithmetic  5.04 us (3%)
  local copies, waits for them, and re-layouts  3.69 us (2%)
    all_to_all x2, blocking collectives, swap(): return lax.all_to_all(pieces, axis, 0, 0, tiled=True)  59.5 us
    all_to_all x2, waiting for transfers between devices, swap(): return lax.all_to_all(pieces, axis, 0, 0, tiled=True)  27.9 us
    ppermute x3, starting transfers between devices, shards(): other = lax.ppermute(blocks, 'z', [(i, i ^ far) for i in range(nz)])  27.3 us
    pallas_call x1, Pallas kernels, prefill(): pl.pallas_call(prefill_kernel, out_shape=result, grid_spec=pltpu.Prefetch...  11.1 us
    ppermute x3, starting transfers between devices, shards(): lax.ppermute(blocks, 'x', [(i, (i + k) % nx) for i in range(nx)])  8.97 us
    all_to_all x2, starting transfers between devices, swap(): return lax.all_to_all(pieces, axis, 0, 0, tiled=True)  7.87 us
    ppermute x3, waiting for transfers between devices, shards(): other = lax.ppermute(blocks, 'z', [(i, i ^ far) for i in range(nz)])  7.25 us
    ppermute x3, waiting for transfers between devices, shards(): lax.ppermute(blocks, 'x', [(i, (i + k) % nx) for i in range(nx)])  3.99 us
  transfers between devices with their start and end apart: 9, of which 7 were waited for; matrix products, arithmetic and copies ran while one was open for 3% of the time, Pallas kernels for 5%

profile of v3, /device:TPU:32, one launch (start us, length us, event | category | flops | bytes accessed | tf_op | source)
XLA Modules:
  0.0 173.0 jit_solution(17012221066255505108)
XLA Ops:
  0.6 9.1 %collective-permute-start = (bf16[1,128,128]{2,1,0:T(8,128)(2,1)}, bf16[1,128,128]{2,1,0:T(8,128)(2,1)S(1)}, u32[]{:S(2)}, u32[]{:S(2)}) collective-permute-start(bf16[1,128,128]{2,1,0:T(8,128)(2,1)} %bitcast.18), channel_id=1, source_target_pairs={{0,512},{128,640},{256,768},{384,896},{512,0},{640,128},{768,256},... | collective-permute-start | bytes 98312 | tf_op jit(solution)/shard_map/ppermute | solution.py:220
  9.7 2.1 %collective-permute-done = bf16[1,128,128]{2,1,0:T(8,128)(2,1)S(1)} collective-permute-done((bf16[1,128,128]{2,1,0:T(8,128)(2,1)}, bf16[1,128,128]{2,1,0:T(8,128)(2,1)S(1)}, u32[]{:S(2)}, u32[]{:S(2)}) %collective-permute-start) | collective-permute-done | bytes 32800 | tf_op jit(solution)/shard_map/ppermute | solution.py:220
  11.8 0.8 pad_maximum_fusion.3
  12.6 5.2 %collective-permute-start.1 = (bf16[2,128,128]{2,1,0:T(8,128)(2,1)S(1)}, bf16[2,128,128]{2,1,0:T(8,128)(2,1)S(1)}, u32[]{:S(2)}, u32[]{:S(2)}) collective-permute-start(bf16[2,128,128]{2,1,0:T(8,128)(2,1)S(1)} %pad_maximum_fusion.3), channel_id=1, source_target_pairs={{0,256},{128,384},{256,0},{384,128},{512,768},{640,896},{768,512},... | collective-permute-start | bytes 196616 | tf_op jit(solution)/shard_map/ppermute | solution.py:220
  17.8 2.2 %collective-permute-done.1 = bf16[2,128,128]{2,1,0:T(8,128)(2,1)S(1)} collective-permute-done((bf16[2,128,128]{2,1,0:T(8,128)(2,1)S(1)}, bf16[2,128,128]{2,1,0:T(8,128)(2,1)S(1)}, u32[]{:S(2)}, u32[]{:S(2)}) %collective-permute-start.1) | collective-permute-done | bytes 65568 | tf_op jit(solution)/shard_map/ppermute | solution.py:220
  20.0 0.8 pad_maximum_fusion.2
  20.8 13.0 %collective-permute-start.2 = (bf16[4,128,128]{2,1,0:T(8,128)(2,1)S(1)}, bf16[4,128,128]{2,1,0:T(8,128)(2,1)S(1)}, u32[]{:S(2)}, u32[]{:S(2)}) collective-permute-start(bf16[4,128,128]{2,1,0:T(8,128)(2,1)S(1)} %pad_maximum_fusion.2), channel_id=1, source_target_pairs={{0,128},{128,0},{256,384},{384,256},{512,640},{640,512},{768,896},... | collective-permute-start | bytes 393224 | tf_op jit(solution)/shard_map/ppermute | solution.py:220
  33.8 2.9 %collective-permute-done.2 = bf16[4,128,128]{2,1,0:T(8,128)(2,1)S(1)} collective-permute-done((bf16[4,128,128]{2,1,0:T(8,128)(2,1)S(1)}, bf16[4,128,128]{2,1,0:T(8,128)(2,1)S(1)}, u32[]{:S(2)}, u32[]{:S(2)}) %collective-permute-start.2) | collective-permute-done | bytes 131104 | tf_op jit(solution)/shard_map/ppermute | solution.py:220
  36.7 0.8 fusion
  37.5 1.9 %collective-permute-start.3 = (bf16[8,128,128]{2,1,0:T(8,128)(2,1)S(1)}, bf16[8,128,128]{2,1,0:T(8,128)(2,1)S(1)}, u32[]{:S(2)}, u32[]{:S(2)}) collective-permute-start(bf16[8,128,128]{2,1,0:T(8,128)(2,1)S(1)} %get-tuple-element.3), channel_id=1, source_target_pairs={{0,32},{32,64},{64,96},{96,0},{1,33},{33,65},{65,97},{97,1},{2,34}... | collective-permute-start | bytes 786440 | tf_op jit(solution)/shard_map/ppermute | solution.py:224
  39.5 1.9 %collective-permute-start.4 = (bf16[8,128,128]{2,1,0:T(8,128)(2,1)S(1)}, bf16[8,128,128]{2,1,0:T(8,128)(2,1)S(1)}, u32[]{:S(2)}, u32[]{:S(2)}) collective-permute-start(bf16[8,128,128]{2,1,0:T(8,128)(2,1)S(1)} %get-tuple-element.3), channel_id=1, source_target_pairs={{0,64},{32,96},{64,0},{96,32},{1,65},{33,97},{65,1},{97,33},{2,66}... | collective-permute-start | bytes 786440 | tf_op jit(solution)/shard_map/ppermute | solution.py:224
  41.4 5.1 %collective-permute-start.5 = (bf16[8,128,128]{2,1,0:T(8,128)(2,1)S(1)}, bf16[8,128,128]{2,1,0:T(8,128)(2,1)S(1)}, u32[]{:S(2)}, u32[]{:S(2)}) collective-permute-start(bf16[8,128,128]{2,1,0:T(8,128)(2,1)S(1)} %get-tuple-element.3), channel_id=1, source_target_pairs={{0,96},{32,0},{64,32},{96,64},{1,97},{33,1},{65,33},{97,65},{2,98}... | collective-permute-start | bytes 786440 | tf_op jit(solution)/shard_map/ppermute | solution.py:224
  46.5 0.8 reshape.20
  47.3 0.6 copy.13
  48.0 0.6 stack.38.place_ref
  48.6 1.2 collective-permute-done.3
  49.8 0.0 collective-permute-done.4
  49.8 2.8 %collective-permute-done.5 = bf16[8,128,128]{2,1,0:T(8,128)(2,1)S(1)} collective-permute-done((bf16[8,128,128]{2,1,0:T(8,128)(2,1)S(1)}, bf16[8,128,128]{2,1,0:T(8,128)(2,1)S(1)}, u32[]{:S(2)}, u32[]{:S(2)}) %collective-permute-start.5) | collective-permute-done | bytes 262176 | tf_op jit(solution)/shard_map/ppermute | solution.py:224
  52.6 0.1 pad_maximum_fusion.refs_4_
  52.7 0.0 copy-start
  52.7 1.9 %collective-permute-start.6 = (bf16[4,8,128,128]{3,2,1,0:T(8,128)(2,1)S(1)}, bf16[4,8,128,128]{3,2,1,0:T(8,128)(2,1)S(1)}, u32[]{:S(2)}, u32[]{:S(2)}) collective-permute-start(bf16[4,8,128,128]{3,2,1,0:T(8,128)(2,1)S(1)} %pad_maximum_fusion.refs_4_), channel_id=1, source_target_pairs={{0,16},{16,0},{1,17},{17,1},{2,18},{18,2},{3,19},{19,3},{4,20},{20... | collective-permute-start | bytes 3145736 | tf_op jit(solution)/shard_map/ppermute | solution.py:226
  54.7 2.5 %shard_map.123 = f32[32,8,128]{2,1,0:T(8,128)} custom-call(s32[5]{0:T(128)} %stack.38.place_ref, s32[2]{0:T(128)} %lengths_ref.1, bf16[2,64,128]{2,1,0:T(8,128)(2,1)} %bitcast.27, bf16[2,2,128,1024]{3,2,1,0:T(8,128)(2,1)} %cache_ref.1), custom_call_target="tpu_custom_call" | custom-call | flops 1000000000 | bytes 1048576 | tf_op jit(solution)/shard_map/pallas_call | solution.py:241
  57.2 12.4 %all_to_all.20 = f32[32,8,128]{2,1,0:T(8,128)} all-to-all(f32[32,8,128]{2,1,0:T(8,128)} %shard_map.123), channel_id=1, replica_groups=mesh['z'=8,'x'=4,'c'=2,'y'=4,'w'=4] {'x','c','y'}, dimensions={0} | all-to-all | bytes 262144 | tf_op jit(solution)/shard_map/all_to_all | solution.py:23
  69.5 1.9 %shard_map.124 = bf16[8,4,8,128]{3,2,1,0:T(8,128)(2,1)} custom-call(f32[8,4,8,128]{3,2,1,0:T(8,128)} %bitcast.17), custom_call_target="tpu_custom_call" | custom-call | flops 10000000 | bytes 1048576 | tf_op jit(solution)/shard_map/pallas_call | solution.py:245
  71.4 47.1 %all_to_all.21 = bf16[32,8,128]{2,1,0:T(8,128)(2,1)} all-to-all(bf16[32,8,128]{2,1,0:T(8,128)(2,1)} %bitcast.22), channel_id=1, replica_groups=mesh['z'=8,'x'=4,'c'=2,'y'=4,'w'=4] {'z','w'}, dimensions={0} | all-to-all | bytes 131072 | tf_op jit(solution)/shard_map/all_to_all | solution.py:23
  118.5 1.7 shard_map.125
  120.2 3.4 %all-to-all-start.2 = ((f32[8,16,128]{2,1,0:T(8,128)}), f32[8,16,128]{2,1,0:T(8,128)S(1)}, u32[]{:S(2)}, u32[]{:S(2)}) async-start(f32[8,16,128]{2,1,0:T(8,128)} %shard_map.125), calls=%async_computation.2 | async-start | bytes 131072 | tf_op jit(solution)/shard_map/all_to_all | solution.py:23
  123.6 0.7 convert_element_type.6
  124.2 4.9 %all-to-all-done.2.heads_ref = f32[8,16,128]{2,1,0:T(8,128)S(1)} async-done(((f32[8,16,128]{2,1,0:T(8,128)}), f32[8,16,128]{2,1,0:T(8,128)S(1)}, u32[]{:S(2)}, u32[]{:S(2)}) %all-to-all-start.2) | async-done | bytes 65568 | tf_op jit(solution)/shard_map/all_to_all | solution.py:23
  129.1 0.0 copy-start.2
  129.1 0.6 copy-done.2
  129.8 1.7 %shard_map.126 = f32[16,2,128]{2,1,0:T(2,128)} custom-call(f32[8,16,128]{2,1,0:T(8,128)} %copy-done.2, bf16[512,128]{1,0:T(8,128)(2,1)} %weight_ref.1), custom_call_target="tpu_custom_call" | custom-call | flops 10000000 | bytes 1048576 | tf_op jit(solution)/shard_map/pallas_call | solution.py:253
  131.5 4.5 %all-to-all-start.3 = ((f32[16,2,128]{2,1,0:T(2,128)}), f32[16,2,128]{2,1,0:T(2,128)S(1)}, u32[]{:S(2)}, u32[]{:S(2)}) async-start(f32[16,2,128]{2,1,0:T(2,128)} %shard_map.126), calls=%async_computation.3 | async-start | bytes 32768 | tf_op jit(solution)/shard_map/all_to_all | solution.py:23
  136.0 0.8 multiply_cosine_fusion
  136.8 0.6 pad_maximum_fusion.4.refs_7_
  137.4 23.0 %all-to-all-done.3 = f32[16,2,128]{2,1,0:T(2,128)S(1)} async-done(((f32[16,2,128]{2,1,0:T(2,128)}), f32[16,2,128]{2,1,0:T(2,128)S(1)}, u32[]{:S(2)}, u32[]{:S(2)}) %all-to-all-start.3) | async-done | bytes 16416 | tf_op jit(solution)/shard_map/all_to_all | solution.py:23
  160.4 0.5 reduce_sum.9
  161.0 0.0 collective-permute-done.6.refs_5_
  161.0 0.0 copy-done
  161.0 0.0 copy-start.1
  161.0 1.0 copy-done.1
  162.0 11.1 %shard_map.122 = bf16[768,128]{1,0:T(8,128)(2,1)} custom-call(s32[5]{0:T(128)} %stack.38.place_ref, bf16[768,8192]{1,0:T(8,128)(2,1)} %refs_3_.1, bf16[768,8192]{1,0:T(8,128)(2,1)} %refs_3_.1, bf16[768,8192]{1,0:T(8,128)(2,1)} %refs_3_.1, bf16[768,8192]{1,0:T(8,128)(2,1)} %refs_3_.1, bf16[4,8,128,128]{3,2,1,0:T(8,128)(2,1)} %copy-done, ...), custom_call_target="tpu_custom_call" | custom-call | flops 2000000000 | bytes 12582912 | tf_op jit(solution)/shard_map/pallas_call | solution.py:173
Async XLA Ops:
  0.6 11.2 %collective-permute-start = (bf16[1,128,128]{2,1,0:T(8,128)(2,1)}, bf16[1,128,128]{2,1,0:T(8,128)(2,1)S(1)}, u32[]{:S(2)}, u32[]{:S(2)}) collective-permute-start(bf16[1,128,128]{2,1,0:T(8,128)(2,1)} %bitcast.18), channel_id=1, source_target_pairs={{0,512},{128,640},{256,768},{384,896},{512,0},{640,128},{768,256},... | collective-permute-start | bytes 98312 | tf_op jit(solution)/shard_map/ppermute | solution.py:220
  12.6 7.4 %collective-permute-start.1 = (bf16[2,128,128]{2,1,0:T(8,128)(2,1)S(1)}, bf16[2,128,128]{2,1,0:T(8,128)(2,1)S(1)}, u32[]{:S(2)}, u32[]{:S(2)}) collective-permute-start(bf16[2,128,128]{2,1,0:T(8,128)(2,1)S(1)} %pad_maximum_fusion.3), channel_id=1, source_target_pairs={{0,256},{128,384},{256,0},{384,128},{512,768},{640,896},{768,512},... | collective-permute-start | bytes 196616 | tf_op jit(solution)/shard_map/ppermute | solution.py:220
  20.8 16.0 %collective-permute-start.2 = (bf16[4,128,128]{2,1,0:T(8,128)(2,1)S(1)}, bf16[4,128,128]{2,1,0:T(8,128)(2,1)S(1)}, u32[]{:S(2)}, u32[]{:S(2)}) collective-permute-start(bf16[4,128,128]{2,1,0:T(8,128)(2,1)S(1)} %pad_maximum_fusion.2), channel_id=1, source_target_pairs={{0,128},{128,0},{256,384},{384,256},{512,640},{640,512},{768,896},... | collective-permute-start | bytes 393224 | tf_op jit(solution)/shard_map/ppermute | solution.py:220
  37.5 12.3 %collective-permute-start.3 = (bf16[8,128,128]{2,1,0:T(8,128)(2,1)S(1)}, bf16[8,128,128]{2,1,0:T(8,128)(2,1)S(1)}, u32[]{:S(2)}, u32[]{:S(2)}) collective-permute-start(bf16[8,128,128]{2,1,0:T(8,128)(2,1)S(1)} %get-tuple-element.3), channel_id=1, source_target_pairs={{0,32},{32,64},{64,96},{96,0},{1,33},{33,65},{65,97},{97,1},{2,34}... | collective-permute-start | bytes 786440 | tf_op jit(solution)/shard_map/ppermute | solution.py:224
  39.5 10.4 %collective-permute-start.4 = (bf16[8,128,128]{2,1,0:T(8,128)(2,1)S(1)}, bf16[8,128,128]{2,1,0:T(8,128)(2,1)S(1)}, u32[]{:S(2)}, u32[]{:S(2)}) collective-permute-start(bf16[8,128,128]{2,1,0:T(8,128)(2,1)S(1)} %get-tuple-element.3), channel_id=1, source_target_pairs={{0,64},{32,96},{64,0},{96,32},{1,65},{33,97},{65,1},{97,33},{2,66}... | collective-permute-start | bytes 786440 | tf_op jit(solution)/shard_map/ppermute | solution.py:224
  41.4 11.2 %collective-permute-start.5 = (bf16[8,128,128]{2,1,0:T(8,128)(2,1)S(1)}, bf16[8,128,128]{2,1,0:T(8,128)(2,1)S(1)}, u32[]{:S(2)}, u32[]{:S(2)}) collective-permute-start(bf16[8,128,128]{2,1,0:T(8,128)(2,1)S(1)} %get-tuple-element.3), channel_id=1, source_target_pairs={{0,96},{32,0},{64,32},{96,64},{1,97},{33,1},{65,33},{97,65},{2,98}... | collective-permute-start | bytes 786440 | tf_op jit(solution)/shard_map/ppermute | solution.py:224
  52.7 108.3 %copy-start = (bf16[4,8,128,128]{3,2,1,0:T(8,128)(2,1)}, bf16[4,8,128,128]{3,2,1,0:T(8,128)(2,1)S(1)}, u32[]{:S(2)}) copy-start(bf16[4,8,128,128]{3,2,1,0:T(8,128)(2,1)S(1)} %pad_maximum_fusion.refs_4_) | copy-start | bytes 3145732
  52.7 108.3 %collective-permute-start.6 = (bf16[4,8,128,128]{3,2,1,0:T(8,128)(2,1)S(1)}, bf16[4,8,128,128]{3,2,1,0:T(8,128)(2,1)S(1)}, u32[]{:S(2)}, u32[]{:S(2)}) collective-permute-start(bf16[4,8,128,128]{3,2,1,0:T(8,128)(2,1)S(1)} %pad_maximum_fusion.refs_4_), channel_id=1, source_target_pairs={{0,16},{16,0},{1,17},{17,1},{2,18},{18,2},{3,19},{19,3},{4,20},{20... | collective-permute-start | bytes 3145736 | tf_op jit(solution)/shard_map/ppermute | solution.py:226
  120.2 8.9 %all-to-all-start.2 = ((f32[8,16,128]{2,1,0:T(8,128)}), f32[8,16,128]{2,1,0:T(8,128)S(1)}, u32[]{:S(2)}, u32[]{:S(2)}) async-start(f32[8,16,128]{2,1,0:T(8,128)} %shard_map.125), calls=%async_computation.2 | async-start | bytes 131072 | tf_op jit(solution)/shard_map/all_to_all | solution.py:23
  129.1 0.6 copy-start.2
  131.5 28.9 %all-to-all-start.3 = ((f32[16,2,128]{2,1,0:T(2,128)}), f32[16,2,128]{2,1,0:T(2,128)S(1)}, u32[]{:S(2)}, u32[]{:S(2)}) async-start(f32[16,2,128]{2,1,0:T(2,128)} %shard_map.126), calls=%async_computation.3 | async-start | bytes 32768 | tf_op jit(solution)/shard_map/all_to_all | solution.py:23
  161.0 1.0 copy-start.1

commit v4 on v3

--- a/solution.py
+++ b/solution.py
@@ -34,11 +34,15 @@
     trajectories, positions = cache_ref.shape[1], cache_ref.shape[2]
     start = place_ref[4] * positions
     pairs = [(t, g) for t in range(trajectories) for g in range(KEY_VALUE_HEADS)]
-    columns = [slice(g * HEAD_SIZE, (g + 1) * HEAD_SIZE) for g in range(KEY_VALUE_HEADS)]
+    columns = [slice(h * HEAD_SIZE, (h + 1) * HEAD_SIZE) for h in range(QUERY_HEADS)]
+    queries = query_ref[...].astype(jnp.float32)
+    order = [i + 4 * side for i in range(4) for side in range(2)]
     scores = jnp.concatenate(
         [
             lax.dot_general(
-                query_ref[t, g * GROUP : (g + 1) * GROUP, :],
+                jnp.concatenate(
+                    [queries[t : t + 1, columns[g * GROUP + r]] for r in order], axis=0
+                ).astype(jnp.bfloat16),
                 cache_ref[0, t, :, columns[g]],
                 (((1,), (1,)), ((), ())),
                 preferred_element_type=jnp.float32,
@@ -67,42 +71,51 @@
             out_ref[owner, row + 4 : row + 6, :] = stats[rows][pair]
 
 
+PIECE = 5
+
+
 def merge_kernel(parts_ref, out_ref):
     ny = parts_ref.shape[1]
-    lane = lax.broadcasted_iota(jnp.int32, (4, HEAD_SIZE), 1)
+    lane = lax.broadcasted_iota(jnp.int32, (1, HEAD_SIZE), 1)
     merged = []
     for y in range(ny):
         numerator, stats = parts_ref[:, y, :4, :], parts_ref[:, y, 4:, :]
         peak, total = stats[:, :, :1], stats[:, :, HEAD_SIZE // 2 : HEAD_SIZE // 2 + 1]
         top = jnp.max(peak, axis=0)
         factor = jnp.exp(peak - top[None])
-        total = jnp.sum(total * factor, axis=0)
-        some = total > 0.0
-        safe = jnp.where(some, total, 1.0)
-        attention = jnp.sum(numerator * factor, axis=0) / safe
-        weight = jnp.where(some, top + jnp.log(safe), masked_score)
-        high = weight.astype(jnp.bfloat16).astype(jnp.float32)
-        middle = (weight - high).astype(jnp.bfloat16).astype(jnp.float32)
-        low = weight - high - middle
-        weight = jnp.where(lane < 32, high, jnp.where(lane < 64, middle, low))
-        merged.append((attention, weight))
+        merged.append(
+            (jnp.sum(numerator * factor, axis=0), top, jnp.sum(total * factor, axis=0))
+        )
+    copies = out_ref.shape[0] // (4 * PIECE)
     for w in range(4):
-        rows = [part[w : w + 1] for kind in range(2) for part in (pair[kind] for pair in merged)]
-        piece = jnp.concatenate(rows, axis=0).astype(jnp.bfloat16)
-        for z in range(out_ref.shape[0]):
-            out_ref[z, w] = piece
+        stats = jnp.zeros((1, HEAD_SIZE), jnp.float32)
+        for y, (_, top, total) in enumerate(merged):
+            stats = jnp.where(lane >= 32 * y, top[w : w + 1], stats)
+            stats = jnp.where(lane >= 32 * y + 16, total[w : w + 1], stats)
+        piece = jnp.concatenate([part[w : w + 1] for part, _, _ in merged] + [stats], axis=0)
+        for z in range(copies):
+            row = (z * 4 + w) * PIECE
+            out_ref[row : row + PIECE, :] = piece
 
 
 def finish_kernel(parts_ref, out_ref):
-    for w in range(parts_ref.shape[1]):
-        parts = parts_ref[:, w].astype(jnp.float32)
-        attention, stats = parts[:, :4, :], parts[:, 4:, :]
-        weight = stats[:, :, :1] + stats[:, :, 32:33] + stats[:, :, 64:65]
-        factor = jnp.exp(weight - jnp.max(weight, axis=0)[None])
-        rows = jnp.sum(attention * factor, axis=0) / jnp.sum(factor, axis=0)
-        rows = rows.astype(jnp.bfloat16).astype(jnp.float32)
-        for k in range(out_ref.shape[0]):
-            out_ref[k, pl.ds(w, 4, stride=4), :] = rows
+    blocks = parts_ref.shape[0] // (4 * PIECE)
+    rows = [None] * 16
+
+    def across(row):
+        return parts_ref[pl.ds(row, blocks, stride=4 * PIECE), :]
+
+    for w in range(4):
+        stats = across(w * PIECE + 4)
+        for y in range(4):
+            peak, total = stats[:, 32 * y : 32 * y + 1], stats[:, 32 * y + 16 : 32 * y + 17]
+            factor = jnp.exp(peak - jnp.max(peak, axis=0, keepdims=True))
+            total = jnp.sum(total * factor, axis=0, keepdims=True)
+            values = jnp.sum(across(w * PIECE + y) * factor, axis=0, keepdims=True)
+            rows[y * 4 + w] = values / total
+    attention = jnp.concatenate(rows, axis=0).astype(jnp.bfloat16).astype(jnp.float32)
+    for k in range(out_ref.shape[0]):
+        out_ref[k] = attention
 
 
 def out_kernel(heads_ref, weight_ref, out_ref):
@@ -191,10 +204,10 @@
 SMEM = pl.BlockSpec(memory_space=pltpu.SMEM)
 
 
-def whole_call(kernel, shape, in_specs=(VMEM,), flops=10**7, dtype=jnp.float32):
+def whole_call(kernel, shape, in_specs=(VMEM,), flops=10**7):
     return pl.pallas_call(
         kernel,
-        out_shape=jax.ShapeDtypeStruct(shape, dtype),
+        out_shape=jax.ShapeDtypeStruct(shape, jnp.float32),
         in_specs=list(in_specs),
         out_specs=VMEM,
         cost_estimate=pl.CostEstimate(flops=flops, bytes_accessed=2**20, transcendentals=0),
@@ -236,18 +249,16 @@
     )
 
     trajectories = queries.shape[0]
-    ordered = queries.reshape(trajectories, KEY_VALUE_HEADS, 2, 4, HEAD_SIZE)
-    ordered = ordered.swapaxes(2, 3).reshape(trajectories, QUERY_HEADS, HEAD_SIZE)
     parts = whole_call(
         block_kernel, (nxc * ny, 8, HEAD_SIZE), (SMEM, SMEM, VMEM, VMEM), flops=10**9
-    )(place, cache_lengths, ordered, key_value_cache)
+    )(place, cache_lengths, queries, key_value_cache)
     parts = swap(parts, ("x", "c", "y"))
-    parts = whole_call(merge_kernel, (nz, nw, 8, HEAD_SIZE), dtype=jnp.bfloat16)(
+    parts = whole_call(merge_kernel, (nz * nw * PIECE, HEAD_SIZE))(
         parts.reshape(nxc, ny, 8, HEAD_SIZE)
     )
-    parts = swap(parts.reshape(nz * nw, 8, HEAD_SIZE), ("z", "w"))
+    parts = swap(parts.reshape(nz * nw * PIECE, 1, HEAD_SIZE), ("z", "w"))
     attention = whole_call(finish_kernel, (nxc, ngy, HEAD_SIZE))(
-        parts.reshape(nz, nw, 8, HEAD_SIZE)
+        parts.reshape(nz * nw * PIECE, HEAD_SIZE)
     )
     heads = swap(attention, ("x", "c"))
     mixed = whole_call(out_kernel, (ngy, trajectories, columns), (VMEM, VMEM))(heads, out_weight)

time: 174 us -> 167 us (0.960)
  blocking collectives: 59.5 us -> 46.6 us
  starting transfers between devices: 46 us -> 51.6 us
    all_to_all x2 -> x1, blocking collectives: 59.5 us -> 46.6 us  [swap(): return lax.all_to_all(pieces, axis, 0, 0, tiled=True)]
    all_to_all x2 -> x3, waiting for transfers between devices: 27.9 us -> 33.4 us  [swap(): return lax.all_to_all(pieces, axis, 0, 0, tiled=True)]
    all_to_all x2 -> x3, starting transfers between devices: 7.87 us -> 13.2 us  [swap(): return lax.all_to_all(pieces, axis, 0, 0, tiled=True)]
    ppermute x3, waiting for transfers between devices: 3.99 us -> 0.01 us  [shards(): lax.ppermute(blocks, 'x', [(i, (i + k) % nx) for i in range(nx)])]
  transfers between devices with their start and end apart: 9 -> 10, of which waited for: 7 -> 6; matrix products, arithmetic and copies ran while one was open for 3% -> 2% of each run, Pallas kernels for 5% -> 5%
where the time goes in v4:
time: 167 us; the launch traced here: 166 us
  starting transfers between devices  51.6 us (31%)
  blocking collectives  46.6 us (28%)
  waiting for transfers between devices  40.6 us (24%)
  Pallas kernels  18.7 us (11%)
  other arithmetic  5.03 us (3%)
  local copies, waits for them, and re-layouts  2.95 us (2%)
    all_to_all x1, blocking collectives, swap(): return lax.all_to_all(pieces, axis, 0, 0, tiled=True)  46.6 us
    all_to_all x3, waiting for transfers between devices, swap(): return lax.all_to_all(pieces, axis, 0, 0, tiled=True)  33.4 us
    ppermute x3, starting transfers between devices, shards(): other = lax.ppermute(blocks, 'z', [(i, i ^ far) for i in range(nz)])  27.3 us
    all_to_all x3, starting transfers between devices, swap(): return lax.all_to_all(pieces, axis, 0, 0, tiled=True)  13.2 us
    pallas_call x1, Pallas kernels, prefill(): pl.pallas_call(prefill_kernel, out_shape=result, grid_spec=pltpu.Prefetch...  11.1 us
    ppermute x3, starting transfers between devices, shards(): lax.ppermute(blocks, 'x', [(i, (i + k) % nx) for i in range(nx)])  8.97 us
    ppermute x3, waiting for transfers between devices, shards(): other = lax.ppermute(blocks, 'z', [(i, i ^ far) for i in range(nz)])  7.25 us
  transfers between devices with their start and end apart: 10, of which 6 were waited for; matrix products, arithmetic and copies ran while one was open for 2% of the time, Pallas kernels for 5%

profile of v4, /device:TPU:32, one launch (start us, length us, event | category | flops | bytes accessed | tf_op | source)
XLA Modules:
  0.0 166.4 jit_solution(11467488393825438342)
XLA Ops:
  0.6 9.1 %collective-permute-start = (bf16[1,128,128]{2,1,0:T(8,128)(2,1)}, bf16[1,128,128]{2,1,0:T(8,128)(2,1)S(1)}, u32[]{:S(2)}, u32[]{:S(2)}) collective-permute-start(bf16[1,128,128]{2,1,0:T(8,128)(2,1)} %bitcast.19), channel_id=1, source_target_pairs={{0,512},{128,640},{256,768},{384,896},{512,0},{640,128},{768,256},... | collective-permute-start | bytes 98312 | tf_op jit(solution)/shard_map/ppermute | solution.py:233
  9.7 2.1 %collective-permute-done = bf16[1,128,128]{2,1,0:T(8,128)(2,1)S(1)} collective-permute-done((bf16[1,128,128]{2,1,0:T(8,128)(2,1)}, bf16[1,128,128]{2,1,0:T(8,128)(2,1)S(1)}, u32[]{:S(2)}, u32[]{:S(2)}) %collective-permute-start) | collective-permute-done | bytes 32800 | tf_op jit(solution)/shard_map/ppermute | solution.py:233
  11.8 0.8 pad_maximum_fusion.3
  12.6 5.2 %collective-permute-start.1 = (bf16[2,128,128]{2,1,0:T(8,128)(2,1)S(1)}, bf16[2,128,128]{2,1,0:T(8,128)(2,1)S(1)}, u32[]{:S(2)}, u32[]{:S(2)}) collective-permute-start(bf16[2,128,128]{2,1,0:T(8,128)(2,1)S(1)} %pad_maximum_fusion.3), channel_id=1, source_target_pairs={{0,256},{128,384},{256,0},{384,128},{512,768},{640,896},{768,512},... | collective-permute-start | bytes 196616 | tf_op jit(solution)/shard_map/ppermute | solution.py:233
  17.8 2.2 %collective-permute-done.1 = bf16[2,128,128]{2,1,0:T(8,128)(2,1)S(1)} collective-permute-done((bf16[2,128,128]{2,1,0:T(8,128)(2,1)S(1)}, bf16[2,128,128]{2,1,0:T(8,128)(2,1)S(1)}, u32[]{:S(2)}, u32[]{:S(2)}) %collective-permute-start.1) | collective-permute-done | bytes 65568 | tf_op jit(solution)/shard_map/ppermute | solution.py:233
  20.0 0.8 pad_maximum_fusion.2
  20.8 13.0 %collective-permute-start.2 = (bf16[4,128,128]{2,1,0:T(8,128)(2,1)S(1)}, bf16[4,128,128]{2,1,0:T(8,128)(2,1)S(1)}, u32[]{:S(2)}, u32[]{:S(2)}) collective-permute-start(bf16[4,128,128]{2,1,0:T(8,128)(2,1)S(1)} %pad_maximum_fusion.2), channel_id=1, source_target_pairs={{0,128},{128,0},{256,384},{384,256},{512,640},{640,512},{768,896},... | collective-permute-start | bytes 393224 | tf_op jit(solution)/shard_map/ppermute | solution.py:233
  33.8 2.9 %collective-permute-done.2 = bf16[4,128,128]{2,1,0:T(8,128)(2,1)S(1)} collective-permute-done((bf16[4,128,128]{2,1,0:T(8,128)(2,1)S(1)}, bf16[4,128,128]{2,1,0:T(8,128)(2,1)S(1)}, u32[]{:S(2)}, u32[]{:S(2)}) %collective-permute-start.2) | collective-permute-done | bytes 131104 | tf_op jit(solution)/shard_map/ppermute | solution.py:233
  36.7 0.8 fusion
  37.5 1.9 %collective-permute-start.3 = (bf16[8,128,128]{2,1,0:T(8,128)(2,1)S(1)}, bf16[8,128,128]{2,1,0:T(8,128)(2,1)S(1)}, u32[]{:S(2)}, u32[]{:S(2)}) collective-permute-start(bf16[8,128,128]{2,1,0:T(8,128)(2,1)S(1)} %get-tuple-element.3), channel_id=1, source_target_pairs={{0,32},{32,64},{64,96},{96,0},{1,33},{33,65},{65,97},{97,1},{2,34}... | collective-permute-start | bytes 786440 | tf_op jit(solution)/shard_map/ppermute | solution.py:237
  39.5 1.9 %collective-permute-start.4 = (bf16[8,128,128]{2,1,0:T(8,128)(2,1)S(1)}, bf16[8,128,128]{2,1,0:T(8,128)(2,1)S(1)}, u32[]{:S(2)}, u32[]{:S(2)}) collective-permute-start(bf16[8,128,128]{2,1,0:T(8,128)(2,1)S(1)} %get-tuple-element.3), channel_id=1, source_target_pairs={{0,64},{32,96},{64,0},{96,32},{1,65},{33,97},{65,1},{97,33},{2,66}... | collective-permute-start | bytes 786440 | tf_op jit(solution)/shard_map/ppermute | solution.py:237
  41.4 5.1 %collective-permute-start.5 = (bf16[8,128,128]{2,1,0:T(8,128)(2,1)S(1)}, bf16[8,128,128]{2,1,0:T(8,128)(2,1)S(1)}, u32[]{:S(2)}, u32[]{:S(2)}) collective-permute-start(bf16[8,128,128]{2,1,0:T(8,128)(2,1)S(1)} %get-tuple-element.3), channel_id=1, source_target_pairs={{0,96},{32,0},{64,32},{96,64},{1,97},{33,1},{65,33},{97,65},{2,98}... | collective-permute-start | bytes 786440 | tf_op jit(solution)/shard_map/ppermute | solution.py:237
  46.5 0.7 stack.38.place_ref
  47.2 2.5 %shard_map.123 = f32[32,8,128]{2,1,0:T(8,128)} custom-call(s32[5]{0:T(128)} %stack.38.place_ref, s32[2]{0:T(128)} %lengths_ref.1, bf16[2,8192]{1,0:T(2,128)(2,1)} %query_ref.1, bf16[2,2,128,1024]{3,2,1,0:T(8,128)(2,1)} %cache_ref.1), custom_call_target="tpu_custom_call" | custom-call | flops 1000000000 | bytes 1048576 | tf_op jit(solution)/shard_map/pallas_call | solution.py:252
  49.7 4.6 %all-to-all-start = ((f32[32,8,128]{2,1,0:T(8,128)}), f32[32,8,128]{2,1,0:T(8,128)S(1)}, u32[]{:S(2)}, u32[]{:S(2)}) async-start(f32[32,8,128]{2,1,0:T(8,128)} %shard_map.123), calls=%async_computation | async-start | bytes 262144 | tf_op jit(solution)/shard_map/all_to_all | solution.py:23
  54.3 0.0 collective-permute-done.3
  54.3 0.0 collective-permute-done.4
  54.3 0.0 collective-permute-done.5
  54.3 0.1 pad_maximum_fusion.refs_4_
  54.5 0.0 copy-start
  54.5 2.2 %collective-permute-start.6 = (bf16[4,8,128,128]{3,2,1,0:T(8,128)(2,1)S(1)}, bf16[4,8,128,128]{3,2,1,0:T(8,128)(2,1)S(1)}, u32[]{:S(2)}, u32[]{:S(2)}) collective-permute-start(bf16[4,8,128,128]{3,2,1,0:T(8,128)(2,1)S(1)} %pad_maximum_fusion.refs_4_), channel_id=1, source_target_pairs={{0,16},{16,0},{1,17},{17,1},{2,18},{18,2},{3,19},{19,3},{4,20},{20... | collective-permute-start | bytes 3145736 | tf_op jit(solution)/shard_map/ppermute | solution.py:239
  56.7 5.4 %all-to-all-done = f32[32,8,128]{2,1,0:T(8,128)S(1)} async-done(((f32[32,8,128]{2,1,0:T(8,128)}), f32[32,8,128]{2,1,0:T(8,128)S(1)}, u32[]{:S(2)}, u32[]{:S(2)}) %all-to-all-start) | async-done | bytes 131104 | tf_op jit(solution)/shard_map/all_to_all | solution.py:23
  62.1 0.0 copy-start.2
  62.1 0.7 copy-done.2
  62.8 1.7 %shard_map.124 = f32[160,128]{1,0:T(8,128)} custom-call(f32[8,4,8,128]{3,2,1,0:T(8,128)} %bitcast.16), custom_call_target="tpu_custom_call" | custom-call | flops 10000000 | bytes 1048576 | tf_op jit(solution)/shard_map/pallas_call | solution.py:256
  64.5 46.6 %all_to_all.20 = f32[160,1,128]{2,1,0:T(1,128)} all-to-all(f32[160,1,128]{2,1,0:T(1,128)} %bitcast.17), channel_id=1, replica_groups=mesh['z'=8,'x'=4,'c'=2,'y'=4,'w'=4] {'z','w'}, dimensions={0} | all-to-all | bytes 163840 | tf_op jit(solution)/shard_map/all_to_all | solution.py:23
  111.2 1.7 %shard_map.125 = f32[8,16,128]{2,1,0:T(8,128)} custom-call(f32[160,128]{1,0:T(8,128)} %bitcast.18), custom_call_target="tpu_custom_call" | custom-call | flops 10000000 | bytes 1048576 | tf_op jit(solution)/shard_map/pallas_call | solution.py:260
  112.9 3.4 %all-to-all-start.2 = ((f32[8,16,128]{2,1,0:T(8,128)}), f32[8,16,128]{2,1,0:T(8,128)S(1)}, u32[]{:S(2)}, u32[]{:S(2)}) async-start(f32[8,16,128]{2,1,0:T(8,128)} %shard_map.125), calls=%async_computation.2 | async-start | bytes 131072 | tf_op jit(solution)/shard_map/all_to_all | solution.py:23
  116.2 0.7 convert_element_type.6
  116.9 4.9 %all-to-all-done.2.heads_ref = f32[8,16,128]{2,1,0:T(8,128)S(1)} async-done(((f32[8,16,128]{2,1,0:T(8,128)}), f32[8,16,128]{2,1,0:T(8,128)S(1)}, u32[]{:S(2)}, u32[]{:S(2)}) %all-to-all-start.2) | async-done | bytes 65568 | tf_op jit(solution)/shard_map/all_to_all | solution.py:23
  121.8 0.0 copy-start.3
  121.8 0.6 copy-done.3
  122.4 1.7 %shard_map.126 = f32[16,2,128]{2,1,0:T(2,128)} custom-call(f32[8,16,128]{2,1,0:T(8,128)} %copy-done.3, bf16[512,128]{1,0:T(8,128)(2,1)} %weight_ref.1), custom_call_target="tpu_custom_call" | custom-call | flops 10000000 | bytes 1048576 | tf_op jit(solution)/shard_map/pallas_call | solution.py:264
  124.1 5.2 %all-to-all-start.3 = ((f32[16,2,128]{2,1,0:T(2,128)}), f32[16,2,128]{2,1,0:T(2,128)S(1)}, u32[]{:S(2)}, u32[]{:S(2)}) async-start(f32[16,2,128]{2,1,0:T(2,128)} %shard_map.126), calls=%async_computation.3 | async-start | bytes 32768 | tf_op jit(solution)/shard_map/all_to_all | solution.py:23
  129.4 0.8 multiply_cosine_fusion
  130.2 0.6 pad_maximum_fusion.4.refs_7_
  130.8 23.0 %all-to-all-done.3 = f32[16,2,128]{2,1,0:T(2,128)S(1)} async-done(((f32[16,2,128]{2,1,0:T(2,128)}), f32[16,2,128]{2,1,0:T(2,128)S(1)}, u32[]{:S(2)}, u32[]{:S(2)}) %all-to-all-start.3) | async-done | bytes 16416 | tf_op jit(solution)/shard_map/all_to_all | solution.py:23
  153.8 0.5 reduce_sum.9
  154.3 0.0 collective-permute-done.6.refs_5_
  154.3 0.0 copy-done
  154.3 0.0 copy-start.1
  154.4 1.0 copy-done.1
  155.3 11.1 %shard_map.122 = bf16[768,128]{1,0:T(8,128)(2,1)} custom-call(s32[5]{0:T(128)} %stack.38.place_ref, bf16[768,8192]{1,0:T(8,128)(2,1)} %refs_3_.1, bf16[768,8192]{1,0:T(8,128)(2,1)} %refs_3_.1, bf16[768,8192]{1,0:T(8,128)(2,1)} %refs_3_.1, bf16[768,8192]{1,0:T(8,128)(2,1)} %refs_3_.1, bf16[4,8,128,128]{3,2,1,0:T(8,128)(2,1)} %copy-done, ...), custom_call_target="tpu_custom_call" | custom-call | flops 2000000000 | bytes 12582912 | tf_op jit(solution)/shard_map/pallas_call | solution.py:186
Async XLA Ops:
  0.6 11.2 %collective-permute-start = (bf16[1,128,128]{2,1,0:T(8,128)(2,1)}, bf16[1,128,128]{2,1,0:T(8,128)(2,1)S(1)}, u32[]{:S(2)}, u32[]{:S(2)}) collective-permute-start(bf16[1,128,128]{2,1,0:T(8,128)(2,1)} %bitcast.19), channel_id=1, source_target_pairs={{0,512},{128,640},{256,768},{384,896},{512,0},{640,128},{768,256},... | collective-permute-start | bytes 98312 | tf_op jit(solution)/shard_map/ppermute | solution.py:233
  12.6 7.4 %collective-permute-start.1 = (bf16[2,128,128]{2,1,0:T(8,128)(2,1)S(1)}, bf16[2,128,128]{2,1,0:T(8,128)(2,1)S(1)}, u32[]{:S(2)}, u32[]{:S(2)}) collective-permute-start(bf16[2,128,128]{2,1,0:T(8,128)(2,1)S(1)} %pad_maximum_fusion.3), channel_id=1, source_target_pairs={{0,256},{128,384},{256,0},{384,128},{512,768},{640,896},{768,512},... | collective-permute-start | bytes 196616 | tf_op jit(solution)/shard_map/ppermute | solution.py:233
  20.8 16.0 %collective-permute-start.2 = (bf16[4,128,128]{2,1,0:T(8,128)(2,1)S(1)}, bf16[4,128,128]{2,1,0:T(8,128)(2,1)S(1)}, u32[]{:S(2)}, u32[]{:S(2)}) collective-permute-start(bf16[4,128,128]{2,1,0:T(8,128)(2,1)S(1)} %pad_maximum_fusion.2), channel_id=1, source_target_pairs={{0,128},{128,0},{256,384},{384,256},{512,640},{640,512},{768,896},... | collective-permute-start | bytes 393224 | tf_op jit(solution)/shard_map/ppermute | solution.py:233
  37.5 16.8 %collective-permute-start.3 = (bf16[8,128,128]{2,1,0:T(8,128)(2,1)S(1)}, bf16[8,128,128]{2,1,0:T(8,128)(2,1)S(1)}, u32[]{:S(2)}, u32[]{:S(2)}) collective-permute-start(bf16[8,128,128]{2,1,0:T(8,128)(2,1)S(1)} %get-tuple-element.3), channel_id=1, source_target_pairs={{0,32},{32,64},{64,96},{96,0},{1,33},{33,65},{65,97},{97,1},{2,34}... | collective-permute-start | bytes 786440 | tf_op jit(solution)/shard_map/ppermute | solution.py:237
  39.5 14.9 %collective-permute-start.4 = (bf16[8,128,128]{2,1,0:T(8,128)(2,1)S(1)}, bf16[8,128,128]{2,1,0:T(8,128)(2,1)S(1)}, u32[]{:S(2)}, u32[]{:S(2)}) collective-permute-start(bf16[8,128,128]{2,1,0:T(8,128)(2,1)S(1)} %get-tuple-element.3), channel_id=1, source_target_pairs={{0,64},{32,96},{64,0},{96,32},{1,65},{33,97},{65,1},{97,33},{2,66}... | collective-permute-start | bytes 786440 | tf_op jit(solution)/shard_map/ppermute | solution.py:237
  41.4 12.9 %collective-permute-start.5 = (bf16[8,128,128]{2,1,0:T(8,128)(2,1)S(1)}, bf16[8,128,128]{2,1,0:T(8,128)(2,1)S(1)}, u32[]{:S(2)}, u32[]{:S(2)}) collective-permute-start(bf16[8,128,128]{2,1,0:T(8,128)(2,1)S(1)} %get-tuple-element.3), channel_id=1, source_target_pairs={{0,96},{32,0},{64,32},{96,64},{1,97},{33,1},{65,33},{97,65},{2,98}... | collective-permute-start | bytes 786440 | tf_op jit(solution)/shard_map/ppermute | solution.py:237
  49.7 12.4 %all-to-all-start = ((f32[32,8,128]{2,1,0:T(8,128)}), f32[32,8,128]{2,1,0:T(8,128)S(1)}, u32[]{:S(2)}, u32[]{:S(2)}) async-start(f32[32,8,128]{2,1,0:T(8,128)} %shard_map.123), calls=%async_computation | async-start | bytes 262144 | tf_op jit(solution)/shard_map/all_to_all | solution.py:23
  54.5 99.9 %copy-start = (bf16[4,8,128,128]{3,2,1,0:T(8,128)(2,1)}, bf16[4,8,128,128]{3,2,1,0:T(8,128)(2,1)S(1)}, u32[]{:S(2)}) copy-start(bf16[4,8,128,128]{3,2,1,0:T(8,128)(2,1)S(1)} %pad_maximum_fusion.refs_4_) | copy-start | bytes 3145732
  54.5 99.9 %collective-permute-start.6 = (bf16[4,8,128,128]{3,2,1,0:T(8,128)(2,1)S(1)}, bf16[4,8,128,128]{3,2,1,0:T(8,128)(2,1)S(1)}, u32[]{:S(2)}, u32[]{:S(2)}) collective-permute-start(bf16[4,8,128,128]{3,2,1,0:T(8,128)(2,1)S(1)} %pad_maximum_fusion.refs_4_), channel_id=1, source_target_pairs={{0,16},{16,0},{1,17},{17,1},{2,18},{18,2},{3,19},{19,3},{4,20},{20... | collective-permute-start | bytes 3145736 | tf_op jit(solution)/shard_map/ppermute | solution.py:239
  62.1 0.7 copy-start.2
  112.9 8.9 %all-to-all-start.2 = ((f32[8,16,128]{2,1,0:T(8,128)}), f32[8,16,128]{2,1,0:T(8,128)S(1)}, u32[]{:S(2)}, u32[]{:S(2)}) async-start(f32[8,16,128]{2,1,0:T(8,128)} %shard_map.125), calls=%async_computation.2 | async-start | bytes 131072 | tf_op jit(solution)/shard_map/all_to_all | solution.py:23
  121.8 0.6 copy-start.3
  124.1 29.7 %all-to-all-start.3 = ((f32[16,2,128]{2,1,0:T(2,128)}), f32[16,2,128]{2,1,0:T(2,128)S(1)}, u32[]{:S(2)}, u32[]{:S(2)}) async-start(f32[16,2,128]{2,1,0:T(2,128)} %shard_map.126), calls=%async_computation.3 | async-start | bytes 32768 | tf_op jit(solution)/shard_map/all_to_all | solution.py:23
  154.3 1.0 copy-start.1

commit v5 on v4

--- a/solution.py
+++ b/solution.py
@@ -173,8 +173,7 @@
 
     def token_block(k):
         def index(step, place):
-            flipped = (step & 1) * 4 + (step & 2) + (step >> 2)
-            return 0, (place[0] ^ flipped) * nx + ((place[1] + nx - k) & (nx - 1))
+            return 0, (place[0] ^ step) * nx + ((place[1] + nx - k) & (nx - 1))
 
         return index
 
@@ -229,9 +228,11 @@
     nxc, ngy = nx * nc, ny * nw
 
     blocks = key_value_weight[None]
-    for far in (4, 2, 1):
-        other = lax.ppermute(blocks, "z", [(i, i ^ far) for i in range(nz)])
-        blocks = jnp.concatenate([blocks, other], axis=0)
+    other = lax.ppermute(blocks, "z", [(i, i ^ 1) for i in range(nz)])
+    pairs = [jnp.concatenate([blocks, other], axis=0)]
+    for far in (4, 6, 2):
+        pairs.append(lax.ppermute(pairs[0], "z", [(i, i ^ far) for i in range(nz)]))
+    blocks = jnp.stack([pairs[k] for k in (0, 3, 1, 2)]).reshape(nz, *key_value_weight.shape)
     sides = [blocks]
     for k in range(1, nx):
         sides.append(lax.ppermute(blocks, "x", [(i, (i + k) % nx) for i in range(nx)]))

time: 167 us -> 167 us (level)
  starting transfers between devices: 51.6 us -> 54.9 us
  waiting for transfers between devices: 40.6 us -> 37.7 us
    ppermute x3 -> x4, waiting for transfers between devices: 7.25 us -> 4.32 us  [the longest x3 2.23 us: shards(): pairs.append(lax.ppermute(pairs[0], 'z', [(i, i ^ far) for i in range(nz)]))]
    ppermute x3 -> x4, starting transfers between devices: 27.3 us -> 28.7 us  [the longest x1 14.6 us: shards(): other = lax.ppermute(blocks, 'z', [(i, i ^ 1) for i in range(nz)])]
  transfers between devices with their start and end apart: 10 -> 11, of which waited for: 6 -> 5; matrix products, arithmetic and copies ran while one was open for 2% -> 2% of each run, Pallas kernels for 5% -> 5%
where the time goes in v5:
time: 167 us; the launch traced here: 166 us
  starting transfers between devices  54.9 us (33%)
  blocking collectives  47.4 us (28%)
  waiting for transfers between devices  37.7 us (23%)
  Pallas kernels  18.7 us (11%)
  other arithmetic  3.51 us (2%)
  local copies, waits for them, and re-layouts  2.89 us (2%)
    all_to_all x1, blocking collectives, swap(): return lax.all_to_all(pieces, axis, 0, 0, tiled=True)  47.4 us
    all_to_all x3, waiting for transfers between devices, swap(): return lax.all_to_all(pieces, axis, 0, 0, tiled=True)  33.4 us
    ppermute x1, starting transfers between devices, shards(): other = lax.ppermute(blocks, 'z', [(i, i ^ 1) for i in range(nz)])  14.6 us
    ppermute x3, starting transfers between devices, shards(): pairs.append(lax.ppermute(pairs[0], 'z', [(i, i ^ far) for i in range(nz)]))  14 us
    all_to_all x3, starting transfers between devices, swap(): return lax.all_to_all(pieces, axis, 0, 0, tiled=True)  13.5 us
    pallas_call x1, Pallas kernels, prefill(): pl.pallas_call(prefill_kernel, out_shape=result, grid_spec=pltpu.Prefetch...  11 us
    ppermute x3, starting transfers between devices, shards(): lax.ppermute(blocks, 'x', [(i, (i + k) % nx) for i in range(nx)])  10.5 us
  transfers between devices with their start and end apart: 11, of which 5 were waited for; matrix products, arithmetic and copies ran while one was open for 2% of the time, Pallas kernels for 5%

profile of v5, /device:TPU:32, one launch (start us, length us, event | category | flops | bytes accessed | tf_op | source)
XLA Modules:
  0.0 165.8 jit_solution(9661046022867700599)
XLA Ops:
  0.6 14.6 %collective-permute-start = (bf16[1,128,128]{2,1,0:T(8,128)(2,1)}, bf16[1,128,128]{2,1,0:T(8,128)(2,1)S(1)}, u32[]{:S(2)}, u32[]{:S(2)}) collective-permute-start(bf16[1,128,128]{2,1,0:T(8,128)(2,1)} %bitcast.34), channel_id=1, source_target_pairs={{0,128},{128,0},{256,384},{384,256},{512,640},{640,512},{768,896},... | collective-permute-start | bytes 98312 | tf_op jit(solution)/shard_map/ppermute | solution.py:231
  15.3 2.1 %collective-permute-done = bf16[1,128,128]{2,1,0:T(8,128)(2,1)S(1)} collective-permute-done((bf16[1,128,128]{2,1,0:T(8,128)(2,1)}, bf16[1,128,128]{2,1,0:T(8,128)(2,1)S(1)}, u32[]{:S(2)}, u32[]{:S(2)}) %collective-permute-start) | collective-permute-done | bytes 32800 | tf_op jit(solution)/shard_map/ppermute | solution.py:231
  17.4 0.8 fusion
  18.1 1.9 %collective-permute-start.1 = (bf16[2,128,128]{2,1,0:T(8,128)(2,1)S(1)}, bf16[2,128,128]{2,1,0:T(8,128)(2,1)S(1)}, u32[]{:S(2)}, u32[]{:S(2)}) collective-permute-start(bf16[2,128,128]{2,1,0:T(8,128)(2,1)S(1)} %get-tuple-element.3), channel_id=1, source_target_pairs={{0,256},{128,384},{256,0},{384,128},{512,768},{640,896},{768,512},... | collective-permute-start | bytes 196616 | tf_op jit(solution)/shard_map/ppermute | solution.py:234
  20.1 1.9 %collective-permute-start.2 = (bf16[2,128,128]{2,1,0:T(8,128)(2,1)S(1)}, bf16[2,128,128]{2,1,0:T(8,128)(2,1)S(1)}, u32[]{:S(2)}, u32[]{:S(2)}) collective-permute-start(bf16[2,128,128]{2,1,0:T(8,128)(2,1)S(1)} %get-tuple-element.3), channel_id=1, source_target_pairs={{0,512},{128,640},{256,768},{384,896},{512,0},{640,128},{768,256},... | collective-permute-start | bytes 196616 | tf_op jit(solution)/shard_map/ppermute | solution.py:234
  22.0 10.2 %collective-permute-start.3 = (bf16[2,128,128]{2,1,0:T(8,128)(2,1)S(1)}, bf16[2,128,128]{2,1,0:T(8,128)(2,1)S(1)}, u32[]{:S(2)}, u32[]{:S(2)}) collective-permute-start(bf16[2,128,128]{2,1,0:T(8,128)(2,1)S(1)} %get-tuple-element.3), channel_id=1, source_target_pairs={{0,768},{128,896},{256,512},{384,640},{512,256},{640,384},{768,0},... | collective-permute-start | bytes 196616 | tf_op jit(solution)/shard_map/ppermute | solution.py:234
  32.2 0.0 collective-permute-done.1
  32.2 0.0 collective-permute-done.2
  32.2 2.2 %collective-permute-done.3 = bf16[2,128,128]{2,1,0:T(8,128)(2,1)S(1)} collective-permute-done((bf16[2,128,128]{2,1,0:T(8,128)(2,1)S(1)}, bf16[2,128,128]{2,1,0:T(8,128)(2,1)S(1)}, u32[]{:S(2)}, u32[]{:S(2)}) %collective-permute-start.3) | collective-permute-done | bytes 65568 | tf_op jit(solution)/shard_map/ppermute | solution.py:234
  34.5 2.6 %collective-permute-start.4 = (bf16[8,128,128]{2,1,0:T(8,128)(2,1)S(1)}, bf16[8,128,128]{2,1,0:T(8,128)(2,1)S(1)}, u32[]{:S(2)}, u32[]{:S(2)}) collective-permute-start(bf16[8,128,128]{2,1,0:T(8,128)(2,1)S(1)} %bitcast.21), channel_id=1, source_target_pairs={{0,32},{32,64},{64,96},{96,0},{1,33},{33,65},{65,97},{97,1},{2,34}... | collective-permute-start | bytes 786440 | tf_op jit(solution)/shard_map/ppermute | solution.py:238
  37.0 4.6 %collective-permute-start.5 = (bf16[8,128,128]{2,1,0:T(8,128)(2,1)S(1)}, bf16[8,128,128]{2,1,0:T(8,128)(2,1)S(1)}, u32[]{:S(2)}, u32[]{:S(2)}) collective-permute-start(bf16[8,128,128]{2,1,0:T(8,128)(2,1)S(1)} %bitcast.22), channel_id=1, source_target_pairs={{0,64},{32,96},{64,0},{96,32},{1,65},{33,97},{65,1},{97,33},{2,66}... | collective-permute-start | bytes 786440 | tf_op jit(solution)/shard_map/ppermute | solution.py:238
  41.7 3.3 %collective-permute-start.6 = (bf16[8,128,128]{2,1,0:T(8,128)(2,1)S(1)}, bf16[8,128,128]{2,1,0:T(8,128)(2,1)S(1)}, u32[]{:S(2)}, u32[]{:S(2)}) collective-permute-start(bf16[8,128,128]{2,1,0:T(8,128)(2,1)S(1)} %bitcast.23), channel_id=1, source_target_pairs={{0,96},{32,0},{64,32},{96,64},{1,97},{33,1},{65,33},{97,65},{2,98}... | collective-permute-start | bytes 786440 | tf_op jit(solution)/shard_map/ppermute | solution.py:238
  45.0 0.6 stack.50.place_ref
  45.6 2.5 %shard_map.123 = f32[32,8,128]{2,1,0:T(8,128)} custom-call(s32[5]{0:T(128)} %stack.50.place_ref, s32[2]{0:T(128)} %lengths_ref.1, bf16[2,8192]{1,0:T(2,128)(2,1)} %query_ref.1, bf16[2,2,128,1024]{3,2,1,0:T(8,128)(2,1)} %cache_ref.1), custom_call_target="tpu_custom_call" | custom-call | flops 1000000000 | bytes 1048576 | tf_op jit(solution)/shard_map/pallas_call | solution.py:253
  48.1 4.9 %all-to-all-start = ((f32[32,8,128]{2,1,0:T(8,128)}), f32[32,8,128]{2,1,0:T(8,128)S(1)}, u32[]{:S(2)}, u32[]{:S(2)}) async-start(f32[32,8,128]{2,1,0:T(8,128)} %shard_map.123), calls=%async_computation | async-start | bytes 262144 | tf_op jit(solution)/shard_map/all_to_all | solution.py:23
  53.0 0.0 collective-permute-done.4
  53.0 0.0 collective-permute-done.5
  53.0 0.0 collective-permute-done.6
  53.1 0.1 pad_maximum_fusion.refs_4_
  53.2 0.0 copy-start
  53.2 2.2 %collective-permute-start.7 = (bf16[4,8,128,128]{3,2,1,0:T(8,128)(2,1)S(1)}, bf16[4,8,128,128]{3,2,1,0:T(8,128)(2,1)S(1)}, u32[]{:S(2)}, u32[]{:S(2)}) collective-permute-start(bf16[4,8,128,128]{3,2,1,0:T(8,128)(2,1)S(1)} %pad_maximum_fusion.refs_4_), channel_id=1, source_target_pairs={{0,16},{16,0},{1,17},{17,1},{2,18},{18,2},{3,19},{19,3},{4,20},{20... | collective-permute-start | bytes 3145736 | tf_op jit(solution)/shard_map/ppermute | solution.py:240
  55.4 5.4 %all-to-all-done = f32[32,8,128]{2,1,0:T(8,128)S(1)} async-done(((f32[32,8,128]{2,1,0:T(8,128)}), f32[32,8,128]{2,1,0:T(8,128)S(1)}, u32[]{:S(2)}, u32[]{:S(2)}) %all-to-all-start) | async-done | bytes 131104 | tf_op jit(solution)/shard_map/all_to_all | solution.py:23
  60.8 0.0 copy-start.2
  60.8 0.7 copy-done.2
  61.5 1.7 %shard_map.124 = f32[160,128]{1,0:T(8,128)} custom-call(f32[8,4,8,128]{3,2,1,0:T(8,128)} %bitcast.25), custom_call_target="tpu_custom_call" | custom-call | flops 10000000 | bytes 1048576 | tf_op jit(solution)/shard_map/pallas_call | solution.py:257
  63.2 47.4 %all_to_all.20 = f32[160,1,128]{2,1,0:T(1,128)} all-to-all(f32[160,1,128]{2,1,0:T(1,128)} %bitcast.26), channel_id=1, replica_groups=mesh['z'=8,'x'=4,'c'=2,'y'=4,'w'=4] {'z','w'}, dimensions={0} | all-to-all | bytes 163840 | tf_op jit(solution)/shard_map/all_to_all | solution.py:23
  110.6 1.7 %shard_map.125 = f32[8,16,128]{2,1,0:T(8,128)} custom-call(f32[160,128]{1,0:T(8,128)} %bitcast.27), custom_call_target="tpu_custom_call" | custom-call | flops 10000000 | bytes 1048576 | tf_op jit(solution)/shard_map/pallas_call | solution.py:261
  112.3 3.4 %all-to-all-start.2 = ((f32[8,16,128]{2,1,0:T(8,128)}), f32[8,16,128]{2,1,0:T(8,128)S(1)}, u32[]{:S(2)}, u32[]{:S(2)}) async-start(f32[8,16,128]{2,1,0:T(8,128)} %shard_map.125), calls=%async_computation.2 | async-start | bytes 131072 | tf_op jit(solution)/shard_map/all_to_all | solution.py:23
  115.7 0.7 convert_element_type.6
  116.3 4.9 %all-to-all-done.2.heads_ref = f32[8,16,128]{2,1,0:T(8,128)S(1)} async-done(((f32[8,16,128]{2,1,0:T(8,128)}), f32[8,16,128]{2,1,0:T(8,128)S(1)}, u32[]{:S(2)}, u32[]{:S(2)}) %all-to-all-start.2) | async-done | bytes 65568 | tf_op jit(solution)/shard_map/all_to_all | solution.py:23
  121.2 0.0 copy-start.3
  121.2 0.6 copy-done.3
  121.9 1.7 %shard_map.126 = f32[16,2,128]{2,1,0:T(2,128)} custom-call(f32[8,16,128]{2,1,0:T(8,128)} %copy-done.3, bf16[512,128]{1,0:T(8,128)(2,1)} %weight_ref.1), custom_call_target="tpu_custom_call" | custom-call | flops 10000000 | bytes 1048576 | tf_op jit(solution)/shard_map/pallas_call | solution.py:265
  123.6 5.2 %all-to-all-start.3 = ((f32[16,2,128]{2,1,0:T(2,128)}), f32[16,2,128]{2,1,0:T(2,128)S(1)}, u32[]{:S(2)}, u32[]{:S(2)}) async-start(f32[16,2,128]{2,1,0:T(2,128)} %shard_map.126), calls=%async_computation.3 | async-start | bytes 32768 | tf_op jit(solution)/shard_map/all_to_all | solution.py:23
  128.9 0.8 multiply_cosine_fusion
  129.6 0.6 pad_maximum_fusion.3.refs_7_
  130.2 23.0 %all-to-all-done.3 = f32[16,2,128]{2,1,0:T(2,128)S(1)} async-done(((f32[16,2,128]{2,1,0:T(2,128)}), f32[16,2,128]{2,1,0:T(2,128)S(1)}, u32[]{:S(2)}, u32[]{:S(2)}) %all-to-all-start.3) | async-done | bytes 16416 | tf_op jit(solution)/shard_map/all_to_all | solution.py:23
  153.3 0.5 reduce_sum.9
  153.8 0.0 collective-permute-done.7.refs_5_
  153.8 0.0 copy-done
  153.8 0.0 copy-start.1
  153.8 1.0 copy-done.1
  154.8 11.0 %shard_map.122 = bf16[768,128]{1,0:T(8,128)(2,1)} custom-call(s32[5]{0:T(128)} %stack.50.place_ref, bf16[768,8192]{1,0:T(8,128)(2,1)} %refs_3_.1, bf16[768,8192]{1,0:T(8,128)(2,1)} %refs_3_.1, bf16[768,8192]{1,0:T(8,128)(2,1)} %refs_3_.1, bf16[768,8192]{1,0:T(8,128)(2,1)} %refs_3_.1, bf16[4,8,128,128]{3,2,1,0:T(8,128)(2,1)} %copy-done, ...), custom_call_target="tpu_custom_call" | custom-call | flops 2000000000 | bytes 12582912 | tf_op jit(solution)/shard_map/pallas_call | solution.py:185
  (1 shorter events, 0.0 us)
Async XLA Ops:
  0.6 16.7 %collective-permute-start = (bf16[1,128,128]{2,1,0:T(8,128)(2,1)}, bf16[1,128,128]{2,1,0:T(8,128)(2,1)S(1)}, u32[]{:S(2)}, u32[]{:S(2)}) collective-permute-start(bf16[1,128,128]{2,1,0:T(8,128)(2,1)} %bitcast.34), channel_id=1, source_target_pairs={{0,128},{128,0},{256,384},{384,256},{512,640},{640,512},{768,896},... | collective-permute-start | bytes 98312 | tf_op jit(solution)/shard_map/ppermute | solution.py:231
  18.1 14.0 %collective-permute-start.1 = (bf16[2,128,128]{2,1,0:T(8,128)(2,1)S(1)}, bf16[2,128,128]{2,1,0:T(8,128)(2,1)S(1)}, u32[]{:S(2)}, u32[]{:S(2)}) collective-permute-start(bf16[2,128,128]{2,1,0:T(8,128)(2,1)S(1)} %get-tuple-element.3), channel_id=1, source_target_pairs={{0,256},{128,384},{256,0},{384,128},{512,768},{640,896},{768,512},... | collective-permute-start | bytes 196616 | tf_op jit(solution)/shard_map/ppermute | solution.py:234
  20.1 12.1 %collective-permute-start.2 = (bf16[2,128,128]{2,1,0:T(8,128)(2,1)S(1)}, bf16[2,128,128]{2,1,0:T(8,128)(2,1)S(1)}, u32[]{:S(2)}, u32[]{:S(2)}) collective-permute-start(bf16[2,128,128]{2,1,0:T(8,128)(2,1)S(1)} %get-tuple-element.3), channel_id=1, source_target_pairs={{0,512},{128,640},{256,768},{384,896},{512,0},{640,128},{768,256},... | collective-permute-start | bytes 196616 | tf_op jit(solution)/shard_map/ppermute | solution.py:234
  22.0 12.4 %collective-permute-start.3 = (bf16[2,128,128]{2,1,0:T(8,128)(2,1)S(1)}, bf16[2,128,128]{2,1,0:T(8,128)(2,1)S(1)}, u32[]{:S(2)}, u32[]{:S(2)}) collective-permute-start(bf16[2,128,128]{2,1,0:T(8,128)(2,1)S(1)} %get-tuple-element.3), channel_id=1, source_target_pairs={{0,768},{128,896},{256,512},{384,640},{512,256},{640,384},{768,0},... | collective-permute-start | bytes 196616 | tf_op jit(solution)/shard_map/ppermute | solution.py:234
  34.5 18.6 %collective-permute-start.4 = (bf16[8,128,128]{2,1,0:T(8,128)(2,1)S(1)}, bf16[8,128,128]{2,1,0:T(8,128)(2,1)S(1)}, u32[]{:S(2)}, u32[]{:S(2)}) collective-permute-start(bf16[8,128,128]{2,1,0:T(8,128)(2,1)S(1)} %bitcast.21), channel_id=1, source_target_pairs={{0,32},{32,64},{64,96},{96,0},{1,33},{33,65},{65,97},{97,1},{2,34}... | collective-permute-start | bytes 786440 | tf_op jit(solution)/shard_map/ppermute | solution.py:238
  37.0 16.0 %collective-permute-start.5 = (bf16[8,128,128]{2,1,0:T(8,128)(2,1)S(1)}, bf16[8,128,128]{2,1,0:T(8,128)(2,1)S(1)}, u32[]{:S(2)}, u32[]{:S(2)}) collective-permute-start(bf16[8,128,128]{2,1,0:T(8,128)(2,1)S(1)} %bitcast.22), channel_id=1, source_target_pairs={{0,64},{32,96},{64,0},{96,32},{1,65},{33,97},{65,1},{97,33},{2,66}... | collective-permute-start | bytes 786440 | tf_op jit(solution)/shard_map/ppermute | solution.py:238
  41.7 11.4 %collective-permute-start.6 = (bf16[8,128,128]{2,1,0:T(8,128)(2,1)S(1)}, bf16[8,128,128]{2,1,0:T(8,128)(2,1)S(1)}, u32[]{:S(2)}, u32[]{:S(2)}) collective-permute-start(bf16[8,128,128]{2,1,0:T(8,128)(2,1)S(1)} %bitcast.23), channel_id=1, source_target_pairs={{0,96},{32,0},{64,32},{96,64},{1,97},{33,1},{65,33},{97,65},{2,98}... | collective-permute-start | bytes 786440 | tf_op jit(solution)/shard_map/ppermute | solution.py:238
  48.1 12.7 %all-to-all-start = ((f32[32,8,128]{2,1,0:T(8,128)}), f32[32,8,128]{2,1,0:T(8,128)S(1)}, u32[]{:S(2)}, u32[]{:S(2)}) async-start(f32[32,8,128]{2,1,0:T(8,128)} %shard_map.123), calls=%async_computation | async-start | bytes 262144 | tf_op jit(solution)/shard_map/all_to_all | solution.py:23
  53.2 100.6 %copy-start = (bf16[4,8,128,128]{3,2,1,0:T(8,128)(2,1)}, bf16[4,8,128,128]{3,2,1,0:T(8,128)(2,1)S(1)}, u32[]{:S(2)}) copy-start(bf16[4,8,128,128]{3,2,1,0:T(8,128)(2,1)S(1)} %pad_maximum_fusion.refs_4_) | copy-start | bytes 3145732
  53.2 100.6 %collective-permute-start.7 = (bf16[4,8,128,128]{3,2,1,0:T(8,128)(2,1)S(1)}, bf16[4,8,128,128]{3,2,1,0:T(8,128)(2,1)S(1)}, u32[]{:S(2)}, u32[]{:S(2)}) collective-permute-start(bf16[4,8,128,128]{3,2,1,0:T(8,128)(2,1)S(1)} %pad_maximum_fusion.refs_4_), channel_id=1, source_target_pairs={{0,16},{16,0},{1,17},{17,1},{2,18},{18,2},{3,19},{19,3},{4,20},{20... | collective-permute-start | bytes 3145736 | tf_op jit(solution)/shard_map/ppermute | solution.py:240
  60.8 0.7 copy-start.2
  112.3 8.9 %all-to-all-start.2 = ((f32[8,16,128]{2,1,0:T(8,128)}), f32[8,16,128]{2,1,0:T(8,128)S(1)}, u32[]{:S(2)}, u32[]{:S(2)}) async-start(f32[8,16,128]{2,1,0:T(8,128)} %shard_map.125), calls=%async_computation.2 | async-start | bytes 131072 | tf_op jit(solution)/shard_map/all_to_all | solution.py:23
  121.2 0.6 copy-start.3
  123.6 29.7 %all-to-all-start.3 = ((f32[16,2,128]{2,1,0:T(2,128)}), f32[16,2,128]{2,1,0:T(2,128)S(1)}, u32[]{:S(2)}, u32[]{:S(2)}) async-start(f32[16,2,128]{2,1,0:T(2,128)} %shard_map.126), calls=%async_computation.3 | async-start | bytes 32768 | tf_op jit(solution)/shard_map/all_to_all | solution.py:23
  153.8 1.0 copy-start.1

commit v6 on v5

--- a/solution.py
+++ b/solution.py
@@ -173,7 +173,7 @@
 
     def token_block(k):
         def index(step, place):
-            return 0, (place[0] ^ step) * nx + ((place[1] + nx - k) & (nx - 1))
+            return 0, (place[0] ^ ((step >> 1) + (step & 1) * 4)) * nx + ((place[1] + nx - k) & (nx - 1))
 
         return index
 
@@ -228,11 +228,11 @@
     nxc, ngy = nx * nc, ny * nw
 
     blocks = key_value_weight[None]
-    other = lax.ppermute(blocks, "z", [(i, i ^ 1) for i in range(nz)])
+    other = lax.ppermute(blocks, "z", [(i, i ^ 4) for i in range(nz)])
     pairs = [jnp.concatenate([blocks, other], axis=0)]
-    for far in (4, 6, 2):
+    for far in (1, 2, 3):
         pairs.append(lax.ppermute(pairs[0], "z", [(i, i ^ far) for i in range(nz)]))
-    blocks = jnp.stack([pairs[k] for k in (0, 3, 1, 2)]).reshape(nz, *key_value_weight.shape)
+    blocks = jnp.stack(pairs).reshape(nz, *key_value_weight.shape)
     sides = [blocks]
     for k in range(1, nx):
         sides.append(lax.ppermute(blocks, "x", [(i, (i + k) % nx) for i in range(nx)]))

time: 167 us -> 165 us (0.988)
  starting transfers between devices: 54.9 us -> 52.1 us
    ppermute x1, starting transfers between devices: 14.6 us -> 9.1 us  [shards(): other = lax.ppermute(blocks, 'z', [(i, i ^ 4) for i in range(nz)])]
    ppermute x3, starting transfers between devices: 14 us -> 18.7 us  [shards(): pairs.append(lax.ppermute(pairs[0], 'z', [(i, i ^ far) for i in range(nz)]))]
  transfers between devices with their start and end apart: 11 -> 11, of which waited for: 5 -> 6; matrix products, arithmetic and copies ran while one was open for 2% -> 2% of each run, Pallas kernels for 5% -> 5%
where the time goes in v6:
time: 165 us; the launch traced here: 164 us
  starting transfers between devices  52.1 us (32%)
  blocking collectives  47.4 us (29%)
  waiting for transfers between devices  38.2 us (23%)
  Pallas kernels  18.7 us (11%)
  other arithmetic  3.51 us (2%)
  local copies, waits for them, and re-layouts  2.89 us (2%)
    all_to_all x1, blocking collectives, swap(): return lax.all_to_all(pieces, axis, 0, 0, tiled=True)  47.4 us
    all_to_all x3, waiting for transfers between devices, swap(): return lax.all_to_all(pieces, axis, 0, 0, tiled=True)  33.4 us
    ppermute x3, starting transfers between devices, shards(): pairs.append(lax.ppermute(pairs[0], 'z', [(i, i ^ far) for i in range(nz)]))  18.7 us
    all_to_all x3, starting transfers between devices, swap(): return lax.all_to_all(pieces, axis, 0, 0, tiled=True)  13.2 us
    pallas_call x1, Pallas kernels, prefill(): pl.pallas_call(prefill_kernel, out_shape=result, grid_spec=pltpu.Prefetch...  11 us
    ppermute x1, starting transfers between devices, shards(): other = lax.ppermute(blocks, 'z', [(i, i ^ 4) for i in range(nz)])  9.1 us
    ppermute x3, starting transfers between devices, shards(): lax.ppermute(blocks, 'x', [(i, (i + k) % nx) for i in range(nx)])  8.97 us
  transfers between devices with their start and end apart: 11, of which 6 were waited for; matrix products, arithmetic and copies ran while one was open for 2% of the time, Pallas kernels for 5%

profile of v6, /device:TPU:32, one launch (start us, length us, event | category | flops | bytes accessed | tf_op | source)
XLA Modules:
  0.0 163.7 jit_solution(17814112893255020236)
XLA Ops:
  0.6 9.1 %collective-permute-start = (bf16[1,128,128]{2,1,0:T(8,128)(2,1)}, bf16[1,128,128]{2,1,0:T(8,128)(2,1)S(1)}, u32[]{:S(2)}, u32[]{:S(2)}) collective-permute-start(bf16[1,128,128]{2,1,0:T(8,128)(2,1)} %bitcast.34), channel_id=1, source_target_pairs={{0,512},{128,640},{256,768},{384,896},{512,0},{640,128},{768,256},... | collective-permute-start | bytes 98312 | tf_op jit(solution)/shard_map/ppermute | solution.py:231
  9.7 2.1 %collective-permute-done = bf16[1,128,128]{2,1,0:T(8,128)(2,1)S(1)} collective-permute-done((bf16[1,128,128]{2,1,0:T(8,128)(2,1)}, bf16[1,128,128]{2,1,0:T(8,128)(2,1)S(1)}, u32[]{:S(2)}, u32[]{:S(2)}) %collective-permute-start) | collective-permute-done | bytes 32800 | tf_op jit(solution)/shard_map/ppermute | solution.py:231
  11.8 0.8 fusion
  12.6 13.4 %collective-permute-start.1 = (bf16[2,128,128]{2,1,0:T(8,128)(2,1)S(1)}, bf16[2,128,128]{2,1,0:T(8,128)(2,1)S(1)}, u32[]{:S(2)}, u32[]{:S(2)}) collective-permute-start(bf16[2,128,128]{2,1,0:T(8,128)(2,1)S(1)} %get-tuple-element.3), channel_id=1, source_target_pairs={{0,128},{128,0},{256,384},{384,256},{512,640},{640,512},{768,896},... | collective-permute-start | bytes 196616 | tf_op jit(solution)/shard_map/ppermute | solution.py:234
  26.0 1.9 %collective-permute-start.2 = (bf16[2,128,128]{2,1,0:T(8,128)(2,1)S(1)}, bf16[2,128,128]{2,1,0:T(8,128)(2,1)S(1)}, u32[]{:S(2)}, u32[]{:S(2)}) collective-permute-start(bf16[2,128,128]{2,1,0:T(8,128)(2,1)S(1)} %get-tuple-element.3), channel_id=1, source_target_pairs={{0,256},{128,384},{256,0},{384,128},{512,768},{640,896},{768,512},... | collective-permute-start | bytes 196616 | tf_op jit(solution)/shard_map/ppermute | solution.py:234
  27.9 3.4 %collective-permute-start.3 = (bf16[2,128,128]{2,1,0:T(8,128)(2,1)S(1)}, bf16[2,128,128]{2,1,0:T(8,128)(2,1)S(1)}, u32[]{:S(2)}, u32[]{:S(2)}) collective-permute-start(bf16[2,128,128]{2,1,0:T(8,128)(2,1)S(1)} %get-tuple-element.3), channel_id=1, source_target_pairs={{0,384},{128,256},{256,128},{384,0},{512,896},{640,768},{768,640},... | collective-permute-start | bytes 196616 | tf_op jit(solution)/shard_map/ppermute | solution.py:234
  31.3 0.0 collective-permute-done.1
  31.3 1.7 %collective-permute-done.2 = bf16[2,128,128]{2,1,0:T(8,128)(2,1)S(1)} collective-permute-done((bf16[2,128,128]{2,1,0:T(8,128)(2,1)S(1)}, bf16[2,128,128]{2,1,0:T(8,128)(2,1)S(1)}, u32[]{:S(2)}, u32[]{:S(2)}) %collective-permute-start.2) | collective-permute-done | bytes 65568 | tf_op jit(solution)/shard_map/ppermute | solution.py:234
  33.0 1.0 collective-permute-done.3
  34.1 1.9 %collective-permute-start.4 = (bf16[8,128,128]{2,1,0:T(8,128)(2,1)S(1)}, bf16[8,128,128]{2,1,0:T(8,128)(2,1)S(1)}, u32[]{:S(2)}, u32[]{:S(2)}) collective-permute-start(bf16[8,128,128]{2,1,0:T(8,128)(2,1)S(1)} %bitcast.21), channel_id=1, source_target_pairs={{0,32},{32,64},{64,96},{96,0},{1,33},{33,65},{65,97},{97,1},{2,34}... | collective-permute-start | bytes 786440 | tf_op jit(solution)/shard_map/ppermute | solution.py:238
  36.0 1.9 %collective-permute-start.5 = (bf16[8,128,128]{2,1,0:T(8,128)(2,1)S(1)}, bf16[8,128,128]{2,1,0:T(8,128)(2,1)S(1)}, u32[]{:S(2)}, u32[]{:S(2)}) collective-permute-start(bf16[8,128,128]{2,1,0:T(8,128)(2,1)S(1)} %bitcast.22), channel_id=1, source_target_pairs={{0,64},{32,96},{64,0},{96,32},{1,65},{33,97},{65,1},{97,33},{2,66}... | collective-permute-start | bytes 786440 | tf_op jit(solution)/shard_map/ppermute | solution.py:238
  38.0 5.1 %collective-permute-start.6 = (bf16[8,128,128]{2,1,0:T(8,128)(2,1)S(1)}, bf16[8,128,128]{2,1,0:T(8,128)(2,1)S(1)}, u32[]{:S(2)}, u32[]{:S(2)}) collective-permute-start(bf16[8,128,128]{2,1,0:T(8,128)(2,1)S(1)} %bitcast.23), channel_id=1, source_target_pairs={{0,96},{32,0},{64,32},{96,64},{1,97},{33,1},{65,33},{97,65},{2,98}... | collective-permute-start | bytes 786440 | tf_op jit(solution)/shard_map/ppermute | solution.py:238
  43.1 0.6 stack.50.place_ref
  43.7 2.5 %shard_map.123 = f32[32,8,128]{2,1,0:T(8,128)} custom-call(s32[5]{0:T(128)} %stack.50.place_ref, s32[2]{0:T(128)} %lengths_ref.1, bf16[2,8192]{1,0:T(2,128)(2,1)} %query_ref.1, bf16[2,2,128,1024]{3,2,1,0:T(8,128)(2,1)} %cache_ref.1), custom_call_target="tpu_custom_call" | custom-call | flops 1000000000 | bytes 1048576 | tf_op jit(solution)/shard_map/pallas_call | solution.py:253
  46.2 4.6 %all-to-all-start = ((f32[32,8,128]{2,1,0:T(8,128)}), f32[32,8,128]{2,1,0:T(8,128)S(1)}, u32[]{:S(2)}, u32[]{:S(2)}) async-start(f32[32,8,128]{2,1,0:T(8,128)} %shard_map.123), calls=%async_computation | async-start | bytes 262144 | tf_op jit(solution)/shard_map/all_to_all | solution.py:23
  50.8 0.0 collective-permute-done.4
  50.8 0.0 collective-permute-done.5
  50.8 0.0 collective-permute-done.6
  50.8 0.1 pad_maximum_fusion.refs_4_
  51.0 0.0 copy-start
  51.0 2.2 %collective-permute-start.7 = (bf16[4,8,128,128]{3,2,1,0:T(8,128)(2,1)S(1)}, bf16[4,8,128,128]{3,2,1,0:T(8,128)(2,1)S(1)}, u32[]{:S(2)}, u32[]{:S(2)}) collective-permute-start(bf16[4,8,128,128]{3,2,1,0:T(8,128)(2,1)S(1)} %pad_maximum_fusion.refs_4_), channel_id=1, source_target_pairs={{0,16},{16,0},{1,17},{17,1},{2,18},{18,2},{3,19},{19,3},{4,20},{20... | collective-permute-start | bytes 3145736 | tf_op jit(solution)/shard_map/ppermute | solution.py:240
  53.2 5.4 %all-to-all-done = f32[32,8,128]{2,1,0:T(8,128)S(1)} async-done(((f32[32,8,128]{2,1,0:T(8,128)}), f32[32,8,128]{2,1,0:T(8,128)S(1)}, u32[]{:S(2)}, u32[]{:S(2)}) %all-to-all-start) | async-done | bytes 131104 | tf_op jit(solution)/shard_map/all_to_all | solution.py:23
  58.6 0.0 copy-start.2
  58.6 0.7 copy-done.2
  59.3 1.7 %shard_map.124 = f32[160,128]{1,0:T(8,128)} custom-call(f32[8,4,8,128]{3,2,1,0:T(8,128)} %bitcast.25), custom_call_target="tpu_custom_call" | custom-call | flops 10000000 | bytes 1048576 | tf_op jit(solution)/shard_map/pallas_call | solution.py:257
  61.0 47.4 %all_to_all.20 = f32[160,1,128]{2,1,0:T(1,128)} all-to-all(f32[160,1,128]{2,1,0:T(1,128)} %bitcast.26), channel_id=1, replica_groups=mesh['z'=8,'x'=4,'c'=2,'y'=4,'w'=4] {'z','w'}, dimensions={0} | all-to-all | bytes 163840 | tf_op jit(solution)/shard_map/all_to_all | solution.py:23
  108.5 1.7 %shard_map.125 = f32[8,16,128]{2,1,0:T(8,128)} custom-call(f32[160,128]{1,0:T(8,128)} %bitcast.27), custom_call_target="tpu_custom_call" | custom-call | flops 10000000 | bytes 1048576 | tf_op jit(solution)/shard_map/pallas_call | solution.py:261
  110.2 3.4 %all-to-all-start.2 = ((f32[8,16,128]{2,1,0:T(8,128)}), f32[8,16,128]{2,1,0:T(8,128)S(1)}, u32[]{:S(2)}, u32[]{:S(2)}) async-start(f32[8,16,128]{2,1,0:T(8,128)} %shard_map.125), calls=%async_computation.2 | async-start | bytes 131072 | tf_op jit(solution)/shard_map/all_to_all | solution.py:23
  113.5 0.7 convert_element_type.6
  114.2 4.9 %all-to-all-done.2.heads_ref = f32[8,16,128]{2,1,0:T(8,128)S(1)} async-done(((f32[8,16,128]{2,1,0:T(8,128)}), f32[8,16,128]{2,1,0:T(8,128)S(1)}, u32[]{:S(2)}, u32[]{:S(2)}) %all-to-all-start.2) | async-done | bytes 65568 | tf_op jit(solution)/shard_map/all_to_all | solution.py:23
  119.1 0.0 copy-start.3
  119.1 0.6 copy-done.3
  119.7 1.7 %shard_map.126 = f32[16,2,128]{2,1,0:T(2,128)} custom-call(f32[8,16,128]{2,1,0:T(8,128)} %copy-done.3, bf16[512,128]{1,0:T(8,128)(2,1)} %weight_ref.1), custom_call_target="tpu_custom_call" | custom-call | flops 10000000 | bytes 1048576 | tf_op jit(solution)/shard_map/pallas_call | solution.py:265
  121.4 5.2 %all-to-all-start.3 = ((f32[16,2,128]{2,1,0:T(2,128)}), f32[16,2,128]{2,1,0:T(2,128)S(1)}, u32[]{:S(2)}, u32[]{:S(2)}) async-start(f32[16,2,128]{2,1,0:T(2,128)} %shard_map.126), calls=%async_computation.3 | async-start | bytes 32768 | tf_op jit(solution)/shard_map/all_to_all | solution.py:23
  126.7 0.8 multiply_cosine_fusion
  127.5 0.6 pad_maximum_fusion.3.refs_7_
  128.1 23.0 %all-to-all-done.3 = f32[16,2,128]{2,1,0:T(2,128)S(1)} async-done(((f32[16,2,128]{2,1,0:T(2,128)}), f32[16,2,128]{2,1,0:T(2,128)S(1)}, u32[]{:S(2)}, u32[]{:S(2)}) %all-to-all-start.3) | async-done | bytes 16416 | tf_op jit(solution)/shard_map/all_to_all | solution.py:23
  151.1 0.5 reduce_sum.9
  151.6 0.0 collective-permute-done.7.refs_5_
  151.6 0.0 copy-done
  151.6 0.0 copy-start.1
  151.6 1.0 copy-done.1
  152.7 11.0 %shard_map.122 = bf16[768,128]{1,0:T(8,128)(2,1)} custom-call(s32[5]{0:T(128)} %stack.50.place_ref, bf16[768,8192]{1,0:T(8,128)(2,1)} %refs_3_.1, bf16[768,8192]{1,0:T(8,128)(2,1)} %refs_3_.1, bf16[768,8192]{1,0:T(8,128)(2,1)} %refs_3_.1, bf16[768,8192]{1,0:T(8,128)(2,1)} %refs_3_.1, bf16[4,8,128,128]{3,2,1,0:T(8,128)(2,1)} %copy-done, ...), custom_call_target="tpu_custom_call" | custom-call | flops 2000000000 | bytes 12582912 | tf_op jit(solution)/shard_map/pallas_call | solution.py:185
  (1 shorter events, 0.0 us)
Async XLA Ops:
  0.6 11.2 %collective-permute-start = (bf16[1,128,128]{2,1,0:T(8,128)(2,1)}, bf16[1,128,128]{2,1,0:T(8,128)(2,1)S(1)}, u32[]{:S(2)}, u32[]{:S(2)}) collective-permute-start(bf16[1,128,128]{2,1,0:T(8,128)(2,1)} %bitcast.34), channel_id=1, source_target_pairs={{0,512},{128,640},{256,768},{384,896},{512,0},{640,128},{768,256},... | collective-permute-start | bytes 98312 | tf_op jit(solution)/shard_map/ppermute | solution.py:231
  12.6 18.7 %collective-permute-start.1 = (bf16[2,128,128]{2,1,0:T(8,128)(2,1)S(1)}, bf16[2,128,128]{2,1,0:T(8,128)(2,1)S(1)}, u32[]{:S(2)}, u32[]{:S(2)}) collective-permute-start(bf16[2,128,128]{2,1,0:T(8,128)(2,1)S(1)} %get-tuple-element.3), channel_id=1, source_target_pairs={{0,128},{128,0},{256,384},{384,256},{512,640},{640,512},{768,896},... | collective-permute-start | bytes 196616 | tf_op jit(solution)/shard_map/ppermute | solution.py:234
  26.0 7.1 %collective-permute-start.2 = (bf16[2,128,128]{2,1,0:T(8,128)(2,1)S(1)}, bf16[2,128,128]{2,1,0:T(8,128)(2,1)S(1)}, u32[]{:S(2)}, u32[]{:S(2)}) collective-permute-start(bf16[2,128,128]{2,1,0:T(8,128)(2,1)S(1)} %get-tuple-element.3), channel_id=1, source_target_pairs={{0,256},{128,384},{256,0},{384,128},{512,768},{640,896},{768,512},... | collective-permute-start | bytes 196616 | tf_op jit(solution)/shard_map/ppermute | solution.py:234
  27.9 6.2 %collective-permute-start.3 = (bf16[2,128,128]{2,1,0:T(8,128)(2,1)S(1)}, bf16[2,128,128]{2,1,0:T(8,128)(2,1)S(1)}, u32[]{:S(2)}, u32[]{:S(2)}) collective-permute-start(bf16[2,128,128]{2,1,0:T(8,128)(2,1)S(1)} %get-tuple-element.3), channel_id=1, source_target_pairs={{0,384},{128,256},{256,128},{384,0},{512,896},{640,768},{768,640},... | collective-permute-start | bytes 196616 | tf_op jit(solution)/shard_map/ppermute | solution.py:234
  34.1 16.7 %collective-permute-start.4 = (bf16[8,128,128]{2,1,0:T(8,128)(2,1)S(1)}, bf16[8,128,128]{2,1,0:T(8,128)(2,1)S(1)}, u32[]{:S(2)}, u32[]{:S(2)}) collective-permute-start(bf16[8,128,128]{2,1,0:T(8,128)(2,1)S(1)} %bitcast.21), channel_id=1, source_target_pairs={{0,32},{32,64},{64,96},{96,0},{1,33},{33,65},{65,97},{97,1},{2,34}... | collective-permute-start | bytes 786440 | tf_op jit(solution)/shard_map/ppermute | solution.py:238
  36.0 14.8 %collective-permute-start.5 = (bf16[8,128,128]{2,1,0:T(8,128)(2,1)S(1)}, bf16[8,128,128]{2,1,0:T(8,128)(2,1)S(1)}, u32[]{:S(2)}, u32[]{:S(2)}) collective-permute-start(bf16[8,128,128]{2,1,0:T(8,128)(2,1)S(1)} %bitcast.22), channel_id=1, source_target_pairs={{0,64},{32,96},{64,0},{96,32},{1,65},{33,97},{65,1},{97,33},{2,66}... | collective-permute-start | bytes 786440 | tf_op jit(solution)/shard_map/ppermute | solution.py:238
  38.0 12.9 %collective-permute-start.6 = (bf16[8,128,128]{2,1,0:T(8,128)(2,1)S(1)}, bf16[8,128,128]{2,1,0:T(8,128)(2,1)S(1)}, u32[]{:S(2)}, u32[]{:S(2)}) collective-permute-start(bf16[8,128,128]{2,1,0:T(8,128)(2,1)S(1)} %bitcast.23), channel_id=1, source_target_pairs={{0,96},{32,0},{64,32},{96,64},{1,97},{33,1},{65,33},{97,65},{2,98}... | collective-permute-start | bytes 786440 | tf_op jit(solution)/shard_map/ppermute | solution.py:238
  46.2 12.4 %all-to-all-start = ((f32[32,8,128]{2,1,0:T(8,128)}), f32[32,8,128]{2,1,0:T(8,128)S(1)}, u32[]{:S(2)}, u32[]{:S(2)}) async-start(f32[32,8,128]{2,1,0:T(8,128)} %shard_map.123), calls=%async_computation | async-start | bytes 262144 | tf_op jit(solution)/shard_map/all_to_all | solution.py:23
  51.0 100.7 %copy-start = (bf16[4,8,128,128]{3,2,1,0:T(8,128)(2,1)}, bf16[4,8,128,128]{3,2,1,0:T(8,128)(2,1)S(1)}, u32[]{:S(2)}) copy-start(bf16[4,8,128,128]{3,2,1,0:T(8,128)(2,1)S(1)} %pad_maximum_fusion.refs_4_) | copy-start | bytes 3145732
  51.0 100.7 %collective-permute-start.7 = (bf16[4,8,128,128]{3,2,1,0:T(8,128)(2,1)S(1)}, bf16[4,8,128,128]{3,2,1,0:T(8,128)(2,1)S(1)}, u32[]{:S(2)}, u32[]{:S(2)}) collective-permute-start(bf16[4,8,128,128]{3,2,1,0:T(8,128)(2,1)S(1)} %pad_maximum_fusion.refs_4_), channel_id=1, source_target_pairs={{0,16},{16,0},{1,17},{17,1},{2,18},{18,2},{3,19},{19,3},{4,20},{20... | collective-permute-start | bytes 3145736 | tf_op jit(solution)/shard_map/ppermute | solution.py:240
  58.6 0.7 copy-start.2
  110.2 8.9 %all-to-all-start.2 = ((f32[8,16,128]{2,1,0:T(8,128)}), f32[8,16,128]{2,1,0:T(8,128)S(1)}, u32[]{:S(2)}, u32[]{:S(2)}) async-start(f32[8,16,128]{2,1,0:T(8,128)} %shard_map.125), calls=%async_computation.2 | async-start | bytes 131072 | tf_op jit(solution)/shard_map/all_to_all | solution.py:23
  119.1 0.6 copy-start.3
  121.4 29.7 %all-to-all-start.3 = ((f32[16,2,128]{2,1,0:T(2,128)}), f32[16,2,128]{2,1,0:T(2,128)S(1)}, u32[]{:S(2)}, u32[]{:S(2)}) async-start(f32[16,2,128]{2,1,0:T(2,128)} %shard_map.126), calls=%async_computation.3 | async-start | bytes 32768 | tf_op jit(solution)/shard_map/all_to_all | solution.py:23
  151.6 1.0 copy-start.1

commit v7 on v6

--- a/solution.py
+++ b/solution.py
@@ -71,10 +71,10 @@
             out_ref[owner, row + 4 : row + 6, :] = stats[rows][pair]
 
 
-PIECE = 5
-
-
-def merge_kernel(parts_ref, out_ref):
+PIECE = 6
+
+
+def merge_kernel(parts_ref, out_ref, rows_ref):
     ny = parts_ref.shape[1]
     lane = lax.broadcasted_iota(jnp.int32, (1, HEAD_SIZE), 1)
     merged = []
@@ -83,34 +83,43 @@
         peak, total = stats[:, :, :1], stats[:, :, HEAD_SIZE // 2 : HEAD_SIZE // 2 + 1]
         top = jnp.max(peak, axis=0)
         factor = jnp.exp(peak - top[None])
-        merged.append(
-            (jnp.sum(numerator * factor, axis=0), top, jnp.sum(total * factor, axis=0))
-        )
+        total = jnp.sum(total * factor, axis=0)
+        some = total > 0.0
+        safe = jnp.where(some, total, 1.0)
+        weight = jnp.where(some, top + jnp.log(safe), masked_score)
+        high = weight.astype(jnp.bfloat16).astype(jnp.float32)
+        middle = (weight - high).astype(jnp.bfloat16).astype(jnp.float32)
+        low = weight - high - middle
+        merged.append((jnp.sum(numerator * factor, axis=0) / safe, (high, middle, low)))
     copies = out_ref.shape[0] // (4 * PIECE)
     for w in range(4):
         stats = jnp.zeros((1, HEAD_SIZE), jnp.float32)
-        for y, (_, top, total) in enumerate(merged):
-            stats = jnp.where(lane >= 32 * y, top[w : w + 1], stats)
-            stats = jnp.where(lane >= 32 * y + 16, total[w : w + 1], stats)
-        piece = jnp.concatenate([part[w : w + 1] for part, _, _ in merged] + [stats], axis=0)
+        for y, (_, split) in enumerate(merged):
+            for k, part in enumerate(split):
+                stats = jnp.where(lane >= 32 * y + 8 * k, part[w : w + 1], stats)
+        rows = [part[w : w + 1] for part, _ in merged] + [stats, stats]
+        piece = jnp.concatenate(rows, axis=0)
         for z in range(copies):
             row = (z * 4 + w) * PIECE
-            out_ref[row : row + PIECE, :] = piece
-
-
-def finish_kernel(parts_ref, out_ref):
+            rows_ref[row : row + PIECE, :] = piece
+    out_ref[...] = rows_ref[...].astype(jnp.bfloat16)
+
+
+def finish_kernel(parts_ref, out_ref, rows_ref):
     blocks = parts_ref.shape[0] // (4 * PIECE)
     rows = [None] * 16
+    rows_ref[...] = parts_ref[...].astype(jnp.float32)
 
     def across(row):
-        return parts_ref[pl.ds(row, blocks, stride=4 * PIECE), :]
+        return rows_ref[pl.ds(row, blocks, stride=4 * PIECE), :]
 
     for w in range(4):
         stats = across(w * PIECE + 4)
         for y in range(4):
-            peak, total = stats[:, 32 * y : 32 * y + 1], stats[:, 32 * y + 16 : 32 * y + 17]
-            factor = jnp.exp(peak - jnp.max(peak, axis=0, keepdims=True))
-            total = jnp.sum(total * factor, axis=0, keepdims=True)
+            high, middle, low = (stats[:, 32 * y + 8 * k : 32 * y + 8 * k + 1] for k in range(3))
+            weight = high + middle + low
+            factor = jnp.exp(weight - jnp.max(weight, axis=0, keepdims=True))
+            total = jnp.sum(factor, axis=0, keepdims=True)
             values = jnp.sum(across(w * PIECE + y) * factor, axis=0, keepdims=True)
             rows[y * 4 + w] = values / total
     attention = jnp.concatenate(rows, axis=0).astype(jnp.bfloat16).astype(jnp.float32)
@@ -203,10 +212,11 @@
 SMEM = pl.BlockSpec(memory_space=pltpu.SMEM)
 
 
-def whole_call(kernel, shape, in_specs=(VMEM,), flops=10**7):
+def whole_call(kernel, shape, in_specs=(VMEM,), flops=10**7, dtype=jnp.float32, scratch=()):
     return pl.pallas_call(
         kernel,
-        out_shape=jax.ShapeDtypeStruct(shape, jnp.float32),
+        out_shape=jax.ShapeDtypeStruct(shape, dtype),
+        scratch_shapes=list(scratch),
         in_specs=list(in_specs),
         out_specs=VMEM,
         cost_estimate=pl.CostEstimate(flops=flops, bytes_accessed=2**20, transcendentals=0),
@@ -254,12 +264,14 @@
         block_kernel, (nxc * ny, 8, HEAD_SIZE), (SMEM, SMEM, VMEM, VMEM), flops=10**9
     )(place, cache_lengths, queries, key_value_cache)
     parts = swap(parts, ("x", "c", "y"))
-    parts = whole_call(merge_kernel, (nz * nw * PIECE, HEAD_SIZE))(
+    pieces = (nz * nw * PIECE, HEAD_SIZE)
+    rows = (pltpu.VMEM(pieces, jnp.float32),)
+    parts = whole_call(merge_kernel, pieces, dtype=jnp.bfloat16, scratch=rows)(
         parts.reshape(nxc, ny, 8, HEAD_SIZE)
     )
-    parts = swap(parts.reshape(nz * nw * PIECE, 1, HEAD_SIZE), ("z", "w"))
-    attention = whole_call(finish_kernel, (nxc, ngy, HEAD_SIZE))(
-        parts.reshape(nz * nw * PIECE, HEAD_SIZE)
+    parts = swap(parts.reshape(nz * nw * PIECE // 2, 2, HEAD_SIZE), ("z", "w"))
+    attention = whole_call(finish_kernel, (nxc, ngy, HEAD_SIZE), scratch=rows)(
+        parts.reshape(pieces)
     )
     heads = swap(attention, ("x", "c"))
     mixed = whole_call(out_kernel, (ngy, trajectories, columns), (VMEM, VMEM))(heads, out_weight)

time: 165 us -> 172 us (1.042)
  blocking collectives: 47.4 us -> 60.2 us
  starting transfers between devices: 52.1 us -> 46.3 us
    all_to_all x1 -> x2, blocking collectives: 47.4 us -> 60.2 us  [swap(): return lax.all_to_all(pieces, axis, 0, 0, tiled=True)]
    ppermute x3, waiting for transfers between devices: 0.01 us -> 6.06 us  [shards(): lax.ppermute(blocks, 'x', [(i, (i + k) % nx) for i in range(nx)])]
    all_to_all x3 -> x2, starting transfers between devices: 13.2 us -> 7.66 us  [swap(): return lax.all_to_all(pieces, axis, 0, 0, tiled=True)]
    all_to_all x3 -> x2, waiting for transfers between devices: 33.4 us -> 27.9 us  [swap(): return lax.all_to_all(pieces, axis, 0, 0, tiled=True)]
  transfers between devices with their start and end apart: 11 -> 10, of which waited for: 6 -> 7; matrix products, arithmetic and copies ran while one was open for 2% -> 2% of each run, Pallas kernels for 5% -> 5%
where the time goes in v7:
time: 172 us; the launch traced here: 171 us
  blocking collectives  60.2 us (35%)
  starting transfers between devices  46.3 us (27%)
  waiting for transfers between devices  38.8 us (23%)
  Pallas kernels  18.8 us (11%)
  other arithmetic  3.51 us (2%)
  local copies, waits for them, and re-layouts  2.22 us (1%)
    all_to_all x2, blocking collectives, swap(): return lax.all_to_all(pieces, axis, 0, 0, tiled=True)  60.2 us
    all_to_all x2, waiting for transfers between devices, swap(): return lax.all_to_all(pieces, axis, 0, 0, tiled=True)  27.9 us
    ppermute x3, starting transfers between devices, shards(): pairs.append(lax.ppermute(pairs[0], 'z', [(i, i ^ far) for i in range(nz)]))  18.7 us
    pallas_call x1, Pallas kernels, prefill(): pl.pallas_call(prefill_kernel, out_shape=result, grid_spec=pltpu.Prefetch...  11 us
    ppermute x1, starting transfers between devices, shards(): other = lax.ppermute(blocks, 'z', [(i, i ^ 4) for i in range(nz)])  9.1 us
    ppermute x3, starting transfers between devices, shards(): lax.ppermute(blocks, 'x', [(i, (i + k) % nx) for i in range(nx)])  8.97 us
    all_to_all x2, starting transfers between devices, swap(): return lax.all_to_all(pieces, axis, 0, 0, tiled=True)  7.66 us
    ppermute x3, waiting for transfers between devices, shards(): lax.ppermute(blocks, 'x', [(i, (i + k) % nx) for i in range(nx)])  6.06 us
  transfers between devices with their start and end apart: 10, of which 7 were waited for; matrix products, arithmetic and copies ran while one was open for 2% of the time, Pallas kernels for 5%

profile of v7, /device:TPU:32, one launch (start us, length us, event | category | flops | bytes accessed | tf_op | source)
XLA Modules:
  0.0 170.7 jit_solution(5507966936077813591)
XLA Ops:
  0.6 9.1 %collective-permute-start = (bf16[1,128,128]{2,1,0:T(8,128)(2,1)}, bf16[1,128,128]{2,1,0:T(8,128)(2,1)S(1)}, u32[]{:S(2)}, u32[]{:S(2)}) collective-permute-start(bf16[1,128,128]{2,1,0:T(8,128)(2,1)} %bitcast.32), channel_id=1, source_target_pairs={{0,512},{128,640},{256,768},{384,896},{512,0},{640,128},{768,256},... | collective-permute-start | bytes 98312 | tf_op jit(solution)/shard_map/ppermute | solution.py:241
  9.7 2.1 %collective-permute-done = bf16[1,128,128]{2,1,0:T(8,128)(2,1)S(1)} collective-permute-done((bf16[1,128,128]{2,1,0:T(8,128)(2,1)}, bf16[1,128,128]{2,1,0:T(8,128)(2,1)S(1)}, u32[]{:S(2)}, u32[]{:S(2)}) %collective-permute-start) | collective-permute-done | bytes 32800 | tf_op jit(solution)/shard_map/ppermute | solution.py:241
  11.8 0.8 fusion
  12.6 13.4 %collective-permute-start.1 = (bf16[2,128,128]{2,1,0:T(8,128)(2,1)S(1)}, bf16[2,128,128]{2,1,0:T(8,128)(2,1)S(1)}, u32[]{:S(2)}, u32[]{:S(2)}) collective-permute-start(bf16[2,128,128]{2,1,0:T(8,128)(2,1)S(1)} %get-tuple-element.3), channel_id=1, source_target_pairs={{0,128},{128,0},{256,384},{384,256},{512,640},{640,512},{768,896},... | collective-permute-start | bytes 196616 | tf_op jit(solution)/shard_map/ppermute | solution.py:244
  26.0 1.9 %collective-permute-start.2 = (bf16[2,128,128]{2,1,0:T(8,128)(2,1)S(1)}, bf16[2,128,128]{2,1,0:T(8,128)(2,1)S(1)}, u32[]{:S(2)}, u32[]{:S(2)}) collective-permute-start(bf16[2,128,128]{2,1,0:T(8,128)(2,1)S(1)} %get-tuple-element.3), channel_id=1, source_target_pairs={{0,256},{128,384},{256,0},{384,128},{512,768},{640,896},{768,512},... | collective-permute-start | bytes 196616 | tf_op jit(solution)/shard_map/ppermute | solution.py:244
  27.9 3.4 %collective-permute-start.3 = (bf16[2,128,128]{2,1,0:T(8,128)(2,1)S(1)}, bf16[2,128,128]{2,1,0:T(8,128)(2,1)S(1)}, u32[]{:S(2)}, u32[]{:S(2)}) collective-permute-start(bf16[2,128,128]{2,1,0:T(8,128)(2,1)S(1)} %get-tuple-element.3), channel_id=1, source_target_pairs={{0,384},{128,256},{256,128},{384,0},{512,896},{640,768},{768,640},... | collective-permute-start | bytes 196616 | tf_op jit(solution)/shard_map/ppermute | solution.py:244
  31.3 0.0 collective-permute-done.1
  31.3 1.7 %collective-permute-done.2 = bf16[2,128,128]{2,1,0:T(8,128)(2,1)S(1)} collective-permute-done((bf16[2,128,128]{2,1,0:T(8,128)(2,1)S(1)}, bf16[2,128,128]{2,1,0:T(8,128)(2,1)S(1)}, u32[]{:S(2)}, u32[]{:S(2)}) %collective-permute-start.2) | collective-permute-done | bytes 65568 | tf_op jit(solution)/shard_map/ppermute | solution.py:244
  33.0 1.0 collective-permute-done.3
  34.1 1.9 %collective-permute-start.4 = (bf16[8,128,128]{2,1,0:T(8,128)(2,1)S(1)}, bf16[8,128,128]{2,1,0:T(8,128)(2,1)S(1)}, u32[]{:S(2)}, u32[]{:S(2)}) collective-permute-start(bf16[8,128,128]{2,1,0:T(8,128)(2,1)S(1)} %bitcast.19), channel_id=1, source_target_pairs={{0,32},{32,64},{64,96},{96,0},{1,33},{33,65},{65,97},{97,1},{2,34}... | collective-permute-start | bytes 786440 | tf_op jit(solution)/shard_map/ppermute | solution.py:248
  36.0 1.9 %collective-permute-start.5 = (bf16[8,128,128]{2,1,0:T(8,128)(2,1)S(1)}, bf16[8,128,128]{2,1,0:T(8,128)(2,1)S(1)}, u32[]{:S(2)}, u32[]{:S(2)}) collective-permute-start(bf16[8,128,128]{2,1,0:T(8,128)(2,1)S(1)} %bitcast.20), channel_id=1, source_target_pairs={{0,64},{32,96},{64,0},{96,32},{1,65},{33,97},{65,1},{97,33},{2,66}... | collective-permute-start | bytes 786440 | tf_op jit(solution)/shard_map/ppermute | solution.py:248
  38.0 5.1 %collective-permute-start.6 = (bf16[8,128,128]{2,1,0:T(8,128)(2,1)S(1)}, bf16[8,128,128]{2,1,0:T(8,128)(2,1)S(1)}, u32[]{:S(2)}, u32[]{:S(2)}) collective-permute-start(bf16[8,128,128]{2,1,0:T(8,128)(2,1)S(1)} %bitcast.21), channel_id=1, source_target_pairs={{0,96},{32,0},{64,32},{96,64},{1,97},{33,1},{65,33},{97,65},{2,98}... | collective-permute-start | bytes 786440 | tf_op jit(solution)/shard_map/ppermute | solution.py:248
  43.1 3.3 %collective-permute-done.4 = bf16[8,128,128]{2,1,0:T(8,128)(2,1)S(1)} collective-permute-done((bf16[8,128,128]{2,1,0:T(8,128)(2,1)S(1)}, bf16[8,128,128]{2,1,0:T(8,128)(2,1)S(1)}, u32[]{:S(2)}, u32[]{:S(2)}) %collective-permute-start.4) | collective-permute-done | bytes 262176 | tf_op jit(solution)/shard_map/ppermute | solution.py:248
  46.4 0.0 collective-permute-done.5
  46.4 2.8 %collective-permute-done.6 = bf16[8,128,128]{2,1,0:T(8,128)(2,1)S(1)} collective-permute-done((bf16[8,128,128]{2,1,0:T(8,128)(2,1)S(1)}, bf16[8,128,128]{2,1,0:T(8,128)(2,1)S(1)}, u32[]{:S(2)}, u32[]{:S(2)}) %collective-permute-start.6) | collective-permute-done | bytes 262176 | tf_op jit(solution)/shard_map/ppermute | solution.py:248
  49.2 0.1 pad_maximum_fusion.refs_4_
  49.3 0.0 copy-start
  49.3 1.9 %collective-permute-start.7 = (bf16[4,8,128,128]{3,2,1,0:T(8,128)(2,1)S(1)}, bf16[4,8,128,128]{3,2,1,0:T(8,128)(2,1)S(1)}, u32[]{:S(2)}, u32[]{:S(2)}) collective-permute-start(bf16[4,8,128,128]{3,2,1,0:T(8,128)(2,1)S(1)} %pad_maximum_fusion.refs_4_), channel_id=1, source_target_pairs={{0,16},{16,0},{1,17},{17,1},{2,18},{18,2},{3,19},{19,3},{4,20},{20... | collective-permute-start | bytes 3145736 | tf_op jit(solution)/shard_map/ppermute | solution.py:250
  51.2 0.6 stack.50.place_ref
  51.8 2.5 %shard_map.123 = f32[32,8,128]{2,1,0:T(8,128)} custom-call(s32[5]{0:T(128)} %stack.50.place_ref, s32[2]{0:T(128)} %lengths_ref.1, bf16[2,8192]{1,0:T(2,128)(2,1)} %query_ref.1, bf16[2,2,128,1024]{3,2,1,0:T(8,128)(2,1)} %cache_ref.1), custom_call_target="tpu_custom_call" | custom-call | flops 1000000000 | bytes 1048576 | tf_op jit(solution)/shard_map/pallas_call | solution.py:263
  54.3 12.4 %all_to_all.20 = f32[32,8,128]{2,1,0:T(8,128)} all-to-all(f32[32,8,128]{2,1,0:T(8,128)} %shard_map.123), channel_id=1, replica_groups=mesh['z'=8,'x'=4,'c'=2,'y'=4,'w'=4] {'x','c','y'}, dimensions={0} | all-to-all | bytes 262144 | tf_op jit(solution)/shard_map/all_to_all | solution.py:23
  66.7 1.9 %shard_map.124 = bf16[192,128]{1,0:T(8,128)(2,1)} custom-call(f32[8,4,8,128]{3,2,1,0:T(8,128)} %bitcast.23), custom_call_target="tpu_custom_call" | custom-call | flops 10000000 | bytes 1048576 | tf_op jit(solution)/shard_map/pallas_call | solution.py:269
  68.6 47.9 %all_to_all.21 = bf16[96,2,128]{2,1,0:T(2,128)(2,1)} all-to-all(bf16[96,2,128]{2,1,0:T(2,128)(2,1)} %bitcast.28), channel_id=1, replica_groups=mesh['z'=8,'x'=4,'c'=2,'y'=4,'w'=4] {'z','w'}, dimensions={0} | all-to-all | bytes 98304 | tf_op jit(solution)/shard_map/all_to_all | solution.py:23
  116.4 1.7 shard_map.125
  118.1 3.4 %all-to-all-start.2 = ((f32[8,16,128]{2,1,0:T(8,128)}), f32[8,16,128]{2,1,0:T(8,128)S(1)}, u32[]{:S(2)}, u32[]{:S(2)}) async-start(f32[8,16,128]{2,1,0:T(8,128)} %shard_map.125), calls=%async_computation.2 | async-start | bytes 131072 | tf_op jit(solution)/shard_map/all_to_all | solution.py:23
  121.5 0.7 convert_element_type.6
  122.1 4.9 %all-to-all-done.2.heads_ref = f32[8,16,128]{2,1,0:T(8,128)S(1)} async-done(((f32[8,16,128]{2,1,0:T(8,128)}), f32[8,16,128]{2,1,0:T(8,128)S(1)}, u32[]{:S(2)}, u32[]{:S(2)}) %all-to-all-start.2) | async-done | bytes 65568 | tf_op jit(solution)/shard_map/all_to_all | solution.py:23
  127.0 0.0 copy-start.2
  127.0 0.6 copy-done.2
  127.6 1.7 %shard_map.126 = f32[16,2,128]{2,1,0:T(2,128)} custom-call(f32[8,16,128]{2,1,0:T(8,128)} %copy-done.2, bf16[512,128]{1,0:T(8,128)(2,1)} %weight_ref.1), custom_call_target="tpu_custom_call" | custom-call | flops 10000000 | bytes 1048576 | tf_op jit(solution)/shard_map/pallas_call | solution.py:277
  129.4 4.3 %all-to-all-start.3 = ((f32[16,2,128]{2,1,0:T(2,128)}), f32[16,2,128]{2,1,0:T(2,128)S(1)}, u32[]{:S(2)}, u32[]{:S(2)}) async-start(f32[16,2,128]{2,1,0:T(2,128)} %shard_map.126), calls=%async_computation.3 | async-start | bytes 32768 | tf_op jit(solution)/shard_map/all_to_all | solution.py:23
  133.7 0.8 multiply_cosine_fusion
  134.5 0.6 pad_maximum_fusion.3.refs_7_
  135.1 23.0 %all-to-all-done.3 = f32[16,2,128]{2,1,0:T(2,128)S(1)} async-done(((f32[16,2,128]{2,1,0:T(2,128)}), f32[16,2,128]{2,1,0:T(2,128)S(1)}, u32[]{:S(2)}, u32[]{:S(2)}) %all-to-all-start.3) | async-done | bytes 16416 | tf_op jit(solution)/shard_map/all_to_all | solution.py:23
  158.1 0.5 reduce_sum.9
  158.6 0.0 collective-permute-done.7.refs_5_
  158.6 0.0 copy-done
  158.6 0.0 copy-start.1
  158.6 1.0 copy-done.1
  159.6 11.0 %shard_map.122 = bf16[768,128]{1,0:T(8,128)(2,1)} custom-call(s32[5]{0:T(128)} %stack.50.place_ref, bf16[768,8192]{1,0:T(8,128)(2,1)} %refs_3_.1, bf16[768,8192]{1,0:T(8,128)(2,1)} %refs_3_.1, bf16[768,8192]{1,0:T(8,128)(2,1)} %refs_3_.1, bf16[768,8192]{1,0:T(8,128)(2,1)} %refs_3_.1, bf16[4,8,128,128]{3,2,1,0:T(8,128)(2,1)} %copy-done, ...), custom_call_target="tpu_custom_call" | custom-call | flops 2000000000 | bytes 12582912 | tf_op jit(solution)/shard_map/pallas_call | solution.py:194
  (1 shorter events, 0.0 us)
Async XLA Ops:
  0.6 11.2 %collective-permute-start = (bf16[1,128,128]{2,1,0:T(8,128)(2,1)}, bf16[1,128,128]{2,1,0:T(8,128)(2,1)S(1)}, u32[]{:S(2)}, u32[]{:S(2)}) collective-permute-start(bf16[1,128,128]{2,1,0:T(8,128)(2,1)} %bitcast.32), channel_id=1, source_target_pairs={{0,512},{128,640},{256,768},{384,896},{512,0},{640,128},{768,256},... | collective-permute-start | bytes 98312 | tf_op jit(solution)/shard_map/ppermute | solution.py:241
  12.6 18.7 %collective-permute-start.1 = (bf16[2,128,128]{2,1,0:T(8,128)(2,1)S(1)}, bf16[2,128,128]{2,1,0:T(8,128)(2,1)S(1)}, u32[]{:S(2)}, u32[]{:S(2)}) collective-permute-start(bf16[2,128,128]{2,1,0:T(8,128)(2,1)S(1)} %get-tuple-element.3), channel_id=1, source_target_pairs={{0,128},{128,0},{256,384},{384,256},{512,640},{640,512},{768,896},... | collective-permute-start | bytes 196616 | tf_op jit(solution)/shard_map/ppermute | solution.py:244
  26.0 7.1 %collective-permute-start.2 = (bf16[2,128,128]{2,1,0:T(8,128)(2,1)S(1)}, bf16[2,128,128]{2,1,0:T(8,128)(2,1)S(1)}, u32[]{:S(2)}, u32[]{:S(2)}) collective-permute-start(bf16[2,128,128]{2,1,0:T(8,128)(2,1)S(1)} %get-tuple-element.3), channel_id=1, source_target_pairs={{0,256},{128,384},{256,0},{384,128},{512,768},{640,896},{768,512},... | collective-permute-start | bytes 196616 | tf_op jit(solution)/shard_map/ppermute | solution.py:244
  27.9 6.2 %collective-permute-start.3 = (bf16[2,128,128]{2,1,0:T(8,128)(2,1)S(1)}, bf16[2,128,128]{2,1,0:T(8,128)(2,1)S(1)}, u32[]{:S(2)}, u32[]{:S(2)}) collective-permute-start(bf16[2,128,128]{2,1,0:T(8,128)(2,1)S(1)} %get-tuple-element.3), channel_id=1, source_target_pairs={{0,384},{128,256},{256,128},{384,0},{512,896},{640,768},{768,640},... | collective-permute-start | bytes 196616 | tf_op jit(solution)/shard_map/ppermute | solution.py:244
  34.1 12.3 %collective-permute-start.4 = (bf16[8,128,128]{2,1,0:T(8,128)(2,1)S(1)}, bf16[8,128,128]{2,1,0:T(8,128)(2,1)S(1)}, u32[]{:S(2)}, u32[]{:S(2)}) collective-permute-start(bf16[8,128,128]{2,1,0:T(8,128)(2,1)S(1)} %bitcast.19), channel_id=1, source_target_pairs={{0,32},{32,64},{64,96},{96,0},{1,33},{33,65},{65,97},{97,1},{2,34}... | collective-permute-start | bytes 786440 | tf_op jit(solution)/shard_map/ppermute | solution.py:248
  36.0 10.4 %collective-permute-start.5 = (bf16[8,128,128]{2,1,0:T(8,128)(2,1)S(1)}, bf16[8,128,128]{2,1,0:T(8,128)(2,1)S(1)}, u32[]{:S(2)}, u32[]{:S(2)}) collective-permute-start(bf16[8,128,128]{2,1,0:T(8,128)(2,1)S(1)} %bitcast.20), channel_id=1, source_target_pairs={{0,64},{32,96},{64,0},{96,32},{1,65},{33,97},{65,1},{97,33},{2,66}... | collective-permute-start | bytes 786440 | tf_op jit(solution)/shard_map/ppermute | solution.py:248
  38.0 11.2 %collective-permute-start.6 = (bf16[8,128,128]{2,1,0:T(8,128)(2,1)S(1)}, bf16[8,128,128]{2,1,0:T(8,128)(2,1)S(1)}, u32[]{:S(2)}, u32[]{:S(2)}) collective-permute-start(bf16[8,128,128]{2,1,0:T(8,128)(2,1)S(1)} %bitcast.21), channel_id=1, source_target_pairs={{0,96},{32,0},{64,32},{96,64},{1,97},{33,1},{65,33},{97,65},{2,98}... | collective-permute-start | bytes 786440 | tf_op jit(solution)/shard_map/ppermute | solution.py:248
  49.3 109.3 %copy-start = (bf16[4,8,128,128]{3,2,1,0:T(8,128)(2,1)}, bf16[4,8,128,128]{3,2,1,0:T(8,128)(2,1)S(1)}, u32[]{:S(2)}) copy-start(bf16[4,8,128,128]{3,2,1,0:T(8,128)(2,1)S(1)} %pad_maximum_fusion.refs_4_) | copy-start | bytes 3145732
  49.3 109.3 %collective-permute-start.7 = (bf16[4,8,128,128]{3,2,1,0:T(8,128)(2,1)S(1)}, bf16[4,8,128,128]{3,2,1,0:T(8,128)(2,1)S(1)}, u32[]{:S(2)}, u32[]{:S(2)}) collective-permute-start(bf16[4,8,128,128]{3,2,1,0:T(8,128)(2,1)S(1)} %pad_maximum_fusion.refs_4_), channel_id=1, source_target_pairs={{0,16},{16,0},{1,17},{17,1},{2,18},{18,2},{3,19},{19,3},{4,20},{20... | collective-permute-start | bytes 3145736 | tf_op jit(solution)/shard_map/ppermute | solution.py:250
  118.1 8.9 %all-to-all-start.2 = ((f32[8,16,128]{2,1,0:T(8,128)}), f32[8,16,128]{2,1,0:T(8,128)S(1)}, u32[]{:S(2)}, u32[]{:S(2)}) async-start(f32[8,16,128]{2,1,0:T(8,128)} %shard_map.125), calls=%async_computation.2 | async-start | bytes 131072 | tf_op jit(solution)/shard_map/all_to_all | solution.py:23
  127.0 0.6 copy-start.2
  129.4 28.7 %all-to-all-start.3 = ((f32[16,2,128]{2,1,0:T(2,128)}), f32[16,2,128]{2,1,0:T(2,128)S(1)}, u32[]{:S(2)}, u32[]{:S(2)}) async-start(f32[16,2,128]{2,1,0:T(2,128)} %shard_map.126), calls=%async_computation.3 | async-start | bytes 32768 | tf_op jit(solution)/shard_map/all_to_all | solution.py:23
  158.6 1.0 copy-start.1
